TPU v7x, 256 devices: a whole 4x4x8 slice. The times are simulated.
256 devices in a mesh: dp: 128 (over y, z_hi, x, core), seq: 2 (over z_lo).
Axes of the slice: x: 4, y: 4, z: 8 (z_hi: 4, z_lo: 2; z = z_hi * 2 + z_lo), core: 2. Of those that a mesh axis runs over, the one named last changes fastest.
Arguments:
- activations: bfloat16 [32768, 8192], P(('dp', 'seq')), may hold values from -24 to 24
- queries: bfloat16 [32768, 8192], P(('dp', 'seq')), may hold values from -180 to 180
- keys: bfloat16 [32768, 1024], P(('dp', 'seq')), may hold values from -6 to 6
- out_grad: bfloat16 [32768, 8192], P(('dp', 'seq')), may hold values from -0.03125 to 0.03125
- layout: int32 [8192], replicated, may hold values from 0 to 8191, each once
Outputs:
- value_weight_grad: float32 [8192, 1024], P(('dp', 'seq'))
Inputs may be any that keep to these rules, and one draw needn't show every extreme that they name: `layout`: every row number 0 to 8191 appears exactly once.
All inputs are finite; a program needn't handle non-finite values.
Results may differ from a plain program's by a relative error of at most 0.0049.
Values may be sent and summed in bfloat16 or wider, within the bound.
No kernel may reach another device: no remote copies, remote signals or barrier semaphores. Data moves between devices by JAX's collectives and lax.ppermute only.
A program may use at most 128 MiB of HBM per device.

v0:
```python
import jax
import jax.numpy as jnp
from jax import lax
from jax.sharding import Mesh
from jax.sharding import PartitionSpec as P

H = 64
KVH = 8
HD = 128
DP = ("dp_0", "dp_1", "dp_2", "dp_3")
DP_SEQ = ("dp_0", "dp_1", "dp_2", "dp_3", "seq")


def passed_along(value, axis, steps):
    count = lax.axis_size(axis)
    initial, last = (max(0, -steps), min(count, count - steps))
    return lax.ppermute(value, axis, [(source, source + steps) for source in range(initial, last)])


def side_by_side(arrays, axis, dim, along):
    ends, at = ([], 0)
    for a in arrays[:-1]:
        at += a.shape[along]
        ends.append(at)
    both = jnp.concatenate(arrays, axis=along)
    return tuple(jnp.split(lax.all_gather(both, axis, axis=dim, tiled=True), ends, axis=along))


def in_blocks(shard, dim, size):
    shape = shard.shape
    blocks = shard.reshape(*shape[:dim], size, shape[dim] // size, *shape[dim + 1 :])
    return jnp.moveaxis(blocks, dim, 0)


def summed_rows_2(shard, chips, core, dim):
    sizes = (lax.axis_size(chips), lax.axis_size(core))
    blocks = in_blocks(shard, dim, sizes[0] * sizes[1])
    inside = blocks.shape[1:]
    blocks = blocks.reshape(*sizes, *inside).swapaxes(0, 1).reshape(-1, *inside)
    blocks = lax.psum_scatter(blocks, core, scatter_dimension=0, tiled=True)
    return lax.psum_scatter(blocks, chips, scatter_dimension=0, tiled=True)[0]


def local_values(queries, both_keys, out_grad, allowed):
    rows_here = queries.shape[0]
    per_group = H // KVH
    inv_root = 1.0 / float(HD) ** 0.5
    pieces = []
    for group_index in range(KVH):
        offset = group_index * per_group * HD
        query_block = queries[:, offset : offset + per_group * HD].reshape(rows_here, per_group, HD)
        grad_block = out_grad[:, offset : offset + per_group * HD].reshape(rows_here, per_group, HD)
        key_block = both_keys[:, group_index * HD : (group_index + 1) * HD]
        scores = (
            jnp.einsum("igd,jd->gij", query_block, key_block, preferred_element_type=jnp.float32)
            * inv_root
        )
        scores = jnp.where(allowed[None], scores, -jnp.inf)
        weights = jax.nn.softmax(scores, axis=-1).astype(jnp.bfloat16)
        pieces.append(
            jnp.einsum("gij,igd->jd", weights, grad_block, preferred_element_type=jnp.float32)
        )
    return jnp.concatenate(pieces, axis=1)


def rounded(term):
    return lax.optimization_barrier(term.astype(jnp.bfloat16)).astype(jnp.float32)


def body(activations, queries, keys, out_grad, layout):
    rows_here = activations.shape[0]
    seq_index = lax.axis_index("seq")
    earlier = passed_along(keys, "seq", 1)
    both_keys = jnp.concatenate([earlier, keys], axis=0)
    query_place = seq_index * rows_here + jnp.arange(rows_here)
    key_place = (seq_index - 1) * rows_here + jnp.arange(2 * rows_here)
    allowed = (key_place[None, :] <= query_place[:, None]) & (key_place[None, :] >= 0)
    partial_value = local_values(queries, both_keys, out_grad, allowed)
    returned = passed_along(partial_value[:rows_here], "seq", -1)
    value_grad = (partial_value[rows_here:] + returned).astype(jnp.bfloat16)
    model_width = activations.shape[1]
    dp_count = lax.axis_size(DP)
    seq_count = lax.axis_size("seq")
    owner_rows = model_width // (dp_count * seq_count)
    pair_rows, pair_grads = side_by_side((activations, value_grad), "seq", 0, 1)
    virtual = jnp.arange(
        owner_rows * lax.axis_size(("dp_0", "dp_1", "dp_2")) * lax.axis_size("dp_3")
    )
    buffer_rows = (
        virtual // owner_rows * (seq_count * owner_rows)
        + seq_index * owner_rows
        + virtual % owner_rows
    )
    columns = jnp.take(pair_rows, jnp.take(layout, buffer_rows), axis=1)
    return summed_rows_2(
        rounded(jnp.einsum("tr,tc->rc", columns, pair_grads, preferred_element_type=jnp.float32)),
        ("dp_0", "dp_1", "dp_2"),
        "dp_3",
        0,
    )


def solution(mesh):
    finer = Mesh(
        mesh.devices.reshape(4, 4, 4, 2, mesh.shape["seq"]), ("dp_0", "dp_1", "dp_2", "dp_3", "seq")
    )
    placed = (P(DP_SEQ, None), P(DP_SEQ, None), P(DP_SEQ, None), P(DP_SEQ, None), P())
    return jax.shard_map(
        body, mesh=finer, in_specs=placed, out_specs=P(DP_SEQ, None), check_vma=False
    )
```

profile of v0, /device:TPU:0, one launch (start us, length us, event | category | flops | bytes accessed | tf_op | source)
XLA Modules:
  0.0 657.0 jit_solution(14867628792052088865)
XLA Ops:
  6.5 2.9 collective-permute-start
  9.5 2.9 fusion.99
  13.4 1.9 copy.81
  17.7 1.8 copy.78
  30.2 2.3 fusion.41
  43.7 2.7 fusion.49
  46.4 2.6 fusion.48
  49.0 2.6 fusion.47
  51.7 2.6 fusion.46
  54.3 2.7 fusion.45
  57.0 2.6 fusion.44
  61.8 1.9 slice.117
  65.3 3.2 copy.56
  68.5 10.9 %collective-permute-done.1 = f32[128,1024]{0,1:T(8,128)} collective-permute-done((f32[128,1024]{0,1:T(8,128)}, f32[128,1024]{0,1:T(8,128)}, u32[]{:S(2)}, u32[]{:S(2)}) %collective-permute-start.1) | collective-permute-done | bytes 524320 | tf_op jit(solution)/shard_map/ppermute | solution.py:17
  80.5 6.2 pad_maximum_fusion
  86.8 23.0 %gather_fusion = s32[4096]{0:T(1024)S(1)} fusion(s32[8192]{0:T(1024)S(1)} %copy-done, s32[4096]{0:T(1024)S(1)} %broadcast_clamp_fusion.1), kind=kCustom, calls=%fused_computation | custom fusion | bytes 49152 | tf_op jit(solution)/shard_map/jit(_take)/gather | solution.py:94
  110.0 46.7 %all-gather.2.cloned.1.call-done = bf16[256,9216]{0,1:T(8,128)(2,1)} async-done(((bf16[128,9216]{0,1:T(8,128)(2,1)}), bf16[256,9216]{0,1:T(8,128)(2,1)}) %all-gather.2.cloned.1.call-update) | async-done | bytes 4718608 | tf_op jit(solution)/shard_map/all_gather | solution.py:26
  156.7 4.5 split.8
  161.2 15.7 %gather_fusion.1 = bf16[4096,256]{1,0:T(8,128)(2,1)S(1)} fusion(bf16[256,8192]{0,1:T(8,128)(2,1)} %split.8, s32[4096]{0:T(1024)S(1)} %broadcast_clamp_fusion), kind=kCustom, calls=%fused_computation.1 | custom fusion | bytes 4210688 | tf_op jit(solution)/shard_map/jit(_take)/gather | solution.py:94
  176.9 5.7 convolution_convert_fusion
  182.5 11.4 %convert_bitcast_fusion = f32[2,64,32,1024]{3,2,0,1:T(8,128)} fusion(bf16[64,2,32,1024]{3,2,1,0:T(8,128)(2,1)} %bitcast.210), kind=kLoop, calls=%fused_computation.10 | loop fusion | flops 4194304 | bytes 25165824 | tf_op jit(solution)/shard_map/reshape | solution.py:39
  193.9 11.8 %copy.57 = f32[2,64,32,1024]{3,2,1,0:T(8,128)} copy(f32[2,64,32,1024]{3,2,0,1:T(8,128)} %convert_bitcast_fusion) | data formatting | bytes 33554432 | tf_op jit(solution)/shard_map/reshape | solution.py:39
  205.8 31.3 %reduce-scatter.3.cloned.1.call-done = f32[64,32,1024]{2,1,0:T(8,128)} async-done(((f32[128,32,1024]{2,1,0:T(8,128)}), f32[64,32,1024]{2,1,0:T(8,128)}) %reduce-scatter.3.cloned.1.call-update) | async-done | bytes 8388624 | tf_op jit(solution)/shard_map/reduce_scatter | solution.py:40
  237.1 413.3 %reduce-scatter.5.cloned.1.call-done = f32[1,32,1024]{2,1,0:T(8,128)} async-done(((f32[64,32,1024]{2,1,0:T(8,128)}), f32[1,32,1024]{2,1,0:T(8,128)}) %reduce-scatter.5.cloned.1.call-update) | async-done | bytes 131088 | tf_op jit(solution)/shard_map/reduce_scatter | solution.py:41
  (98 shorter events, 30.3 us)
Async XLA Ops:
  6.5 80.3 %copy-start = (s32[8192]{0:T(1024)S(1)}, s32[8192]{0:T(1024)}, u32[]{:S(2)}) copy-start(s32[8192]{0:T(1024)} %param.9) | copy-start | bytes 98308
  6.5 5.8 copy-start.2
  6.5 150.1 %all-gather.2.cloned.1.call-start = ((), (), s32[]{:S(2)}) async-start(), calls=%async_computation.2 | async-start | bytes 7077888 | tf_op jit(solution)/shard_map/all_gather | solution.py:26
  6.5 22.2 %collective-permute-start = (bf16[128,1024]{1,0:T(8,128)(2,1)}, bf16[128,1024]{1,0:T(8,128)(2,1)}, u32[]{:S(2)}, u32[]{:S(2)}) collective-permute-start(bf16[128,1024]{1,0:T(8,128)(2,1)} %param.7), channel_id=1, source_target_pairs={{0,1},{2,3},{4,5},{6,7},{8,9},{10,11},{12,13},{14,15},{16,17},{18,... | collective-permute-start | bytes 786440 | tf_op jit(solution)/shard_map/ppermute | solution.py:17
  13.4 7.9 %copy-start.8 = (bf16[128,1024]{1,0:T(8,128)(2,1)S(1)}, bf16[128,1024]{1,0:T(8,128)(2,1)}, u32[]{:S(2)}) copy-start(bf16[128,1024]{1,0:T(8,128)(2,1)} %get-tuple-element.10) | copy-start | bytes 786436
  13.4 8.8 %copy-start.7 = (bf16[128,1024]{1,0:T(8,128)(2,1)S(1)}, bf16[128,1024]{1,0:T(8,128)(2,1)}, u32[]{:S(2)}) copy-start(bf16[128,1024]{1,0:T(8,128)(2,1)} %get-tuple-element.11) | copy-start | bytes 786436
  13.4 9.6 %copy-start.6 = (bf16[128,1024]{1,0:T(8,128)(2,1)S(1)}, bf16[128,1024]{1,0:T(8,128)(2,1)}, u32[]{:S(2)}) copy-start(bf16[128,1024]{1,0:T(8,128)(2,1)} %get-tuple-element.12) | copy-start | bytes 786436
  13.4 9.8 %copy-start.5 = (bf16[128,1024]{1,0:T(8,128)(2,1)S(1)}, bf16[128,1024]{1,0:T(8,128)(2,1)}, u32[]{:S(2)}) copy-start(bf16[128,1024]{1,0:T(8,128)(2,1)} %get-tuple-element.13) | copy-start | bytes 786436
  13.4 10.6 %copy-start.4 = (bf16[128,1024]{1,0:T(8,128)(2,1)S(1)}, bf16[128,1024]{1,0:T(8,128)(2,1)}, u32[]{:S(2)}) copy-start(bf16[128,1024]{1,0:T(8,128)(2,1)} %get-tuple-element.14) | copy-start | bytes 786436
  15.3 9.6 %copy-start.3 = (bf16[128,1024]{1,0:T(8,128)(2,1)S(1)}, bf16[128,1024]{1,0:T(8,128)(2,1)}, u32[]{:S(2)}) copy-start(bf16[128,1024]{1,0:T(8,128)(2,1)} %get-tuple-element.15) | copy-start | bytes 786436
  16.5 24.8 %copy-start.11 = (bf16[128,1024]{0,1:T(8,128)(2,1)}, bf16[128,1024]{0,1:T(8,128)(2,1)S(1)}, u32[]{:S(2)}) copy-start(bf16[128,1024]{0,1:T(8,128)(2,1)S(1)} %copy.80) | copy-start | bytes 786436
  23.2 6.6 %copy-start.16 = (bf16[128,1024]{0,1:T(8,128)(2,1)}, bf16[128,1024]{0,1:T(8,128)(2,1)S(1)}, u32[]{:S(2)}) copy-start(bf16[128,1024]{0,1:T(8,128)(2,1)S(1)} %copy.74) | copy-start | bytes 786436
  23.2 6.5 copy-start.17
  28.6 3.9 copy-start.15
  30.2 4.0 copy-start.14
  32.9 3.0 copy-start.13
  34.7 3.0 copy-start.12
  39.9 3.0 copy-start.10
  54.3 2.7 copy-start.19
  63.7 15.7 %copy-start.9 = (f32[256,1024]{0,1:T(8,128)S(1)}, f32[256,1024]{0,1:T(8,128)}, u32[]{:S(2)}) copy-start(f32[256,1024]{0,1:T(8,128)} %fusion.42) | copy-start | bytes 3145732
  63.7 15.7 %collective-permute-start.1 = (f32[128,1024]{0,1:T(8,128)}, f32[128,1024]{0,1:T(8,128)}, u32[]{:S(2)}, u32[]{:S(2)}) collective-permute-start(f32[128,1024]{0,1:T(8,128)} %slice.117), channel_id=1, source_target_pairs={{1,0},{3,2},{5,4},{7,6},{9,8},{11,10},{13,12},{15,14},{17,16},{19,... | collective-permute-start | bytes 1572872 | tf_op jit(solution)/shard_map/ppermute | solution.py:17
  86.7 150.4 %reduce-scatter.3.cloned.1.call-start = ((), (), s32[]{:S(2)}) async-start(), calls=%async_computation.3 | async-start | bytes 25165824 | tf_op jit(solution)/shard_map/reduce_scatter | solution.py:40
  205.8 444.7 %reduce-scatter.5.cloned.1.call-start = ((), (), s32[]{:S(2)}) async-start(), calls=%async_computation.4 | async-start | bytes 8519680 | tf_op jit(solution)/shard_map/reduce_scatter | solution.py:41
  237.1 413.4 %copy-start.1 = (s32[8192]{0:T(1024)S(1)}, s32[8192]{0:T(1024)}, u32[]{:S(2)}) copy-start(s32[8192]{0:T(1024)} %param.9) | copy-start | bytes 98308
  (4 other events, 9.1 us)
Sparse Core Ops, SparseCore 0:
  86.8 69.8 all-gather.1
  205.9 31.1 reduce-scatter.2
  239.6 410.7 reduce-scatter.4
where the time goes:
time: 658 us; the launch traced here: 657 us
  waiting for transfers between devices  502 us (76%)
  local copies, waits for them, and re-layouts  80.2 us (12%)
  matrix products  37.5 us (6%)
  other arithmetic  19 us (3%)
  between operations  13.4 us (2%)
    reduce_scatter x1, waiting for transfers between devices, summed_rows_2(): return lax.psum_scatter(blocks, chips, scatter_dimension=0, tiled=True)[0]  413 us
    all_gather x1, waiting for transfers between devices, side_by_side(): lax.all_gather(both, axis, axis=dim, tiled=True)  46.7 us
    gather x2, local copies, waits for them, and re-layouts, body(): columns = jnp.take(pair_rows, jnp.take(layout, buffer_rows), axis=1)  38.8 us
    reduce_scatter x1, waiting for transfers between devices, summed_rows_2(): blocks = lax.psum_scatter(blocks, core, scatter_dimension=0, tiled=True)  31.3 us
    dot_general x8, matrix products, local_values(): jnp.einsum('gij,igd->jd', weights, grad_block, preferred_element_type=jnp...  18.1 us
    unnamed x56, local copies, waits for them, and re-layouts  14 us
  transfers between devices with their start and end apart: 5, of which 4 were waited for; matrix products, arithmetic and copies ran while one was open for 7% of the time, Pallas kernels for 0%

commit v1 on v0

v1 whole, which is shorter than its diff:
```python
import jax
import jax.numpy as jnp
from jax import lax
from jax.experimental import pallas as pl
from jax.experimental.pallas import tpu as pltpu
from jax.sharding import Mesh
from jax.sharding import PartitionSpec as P


H = 64
KVH = 8
HD = 128
PER = H // KVH
AXES = ("y", "zh", "x", "c", "zl")
NEAR = ("x", "c")
CHIPS = 4
OWNED = 32
SCALE = 1.4426950408889634 / float(HD) ** 0.5


def gather_kernel(layout_ref, acts_ref, out_ref, flipped, picked):
    width = acts_ref.shape[1]

    def flip(tile, carry):
        at = pl.multiple_of(tile * 128, 128)
        flipped[pl.ds(at, 128), :] = acts_ref[:, pl.ds(at, 128)].astype(jnp.float32).T
        return carry

    lax.fori_loop(0, width // 128, flip, 0)
    blocks = width // OWNED
    far = out_ref.shape[1] // OWNED
    near = blocks // far

    def pick(block, carry):
        member, owner = block // far, block % far
        base = ((owner // 2 * near + member) * 2 + owner % 2) * OWNED
        for row in range(OWNED):
            source = layout_ref[base + row]
            picked[row : row + 1, :] = flipped[pl.ds(source, 1), :]
        out_ref[member, pl.ds(pl.multiple_of(owner * OWNED, OWNED), OWNED), :] = picked[...].astype(
            jnp.bfloat16
        )
        return carry

    lax.fori_loop(0, blocks, pick, 0)


def gathered(activations, layout, near):
    rows, width = activations.shape
    return pl.pallas_call(
        gather_kernel,
        name="gather_rows",
        out_shape=jax.ShapeDtypeStruct((near, width // near, rows), jnp.bfloat16),
        in_specs=[pl.BlockSpec(memory_space=pltpu.SMEM), pl.BlockSpec(memory_space=pltpu.VMEM)],
        out_specs=pl.BlockSpec(memory_space=pltpu.VMEM),
        scratch_shapes=[
            pltpu.VMEM((width, rows), jnp.float32),
            pltpu.VMEM((OWNED, rows), jnp.float32),
        ],
        cost_estimate=pl.CostEstimate(flops=10**9, bytes_accessed=4 * 2**20, transcendentals=0),
        compiler_params=pltpu.CompilerParams(vmem_limit_bytes=24 * 2**20),
    )(layout, activations)


def attend_kernel(second_ref, queries_ref, earlier_ref, keys_ref, grads_ref, early_ref, own_ref):
    rows = queries_ref.shape[0]
    second = second_ref[0] > 0
    both = jnp.concatenate([earlier_ref[...], keys_ref[...]], axis=0)
    key_place = lax.broadcasted_iota(jnp.int32, (rows, 2 * rows), 0)
    query_place = lax.broadcasted_iota(jnp.int32, (rows, 2 * rows), 1) % rows
    causal = key_place <= query_place
    total = jnp.zeros((2 * rows, HD), jnp.float32)
    for pair in range(PER // 2):
        a, b = 2 * pair * HD, (2 * pair + 1) * HD
        ask = jnp.concatenate([queries_ref[:, a : a + HD], queries_ref[:, b : b + HD]], axis=0)
        grad = jnp.concatenate([grads_ref[:, a : a + HD], grads_ref[:, b : b + HD]], axis=0)
        scores = lax.dot_general(
            both, ask, (((1,), (1,)), ((), ())), preferred_element_type=jnp.float32
        )
        first = jnp.where(second, scores[:rows], -1e30)
        last = jnp.where(causal, scores[rows:], -1e30)
        top = jnp.maximum(
            jnp.max(first, axis=0, keepdims=True), jnp.max(last, axis=0, keepdims=True)
        )
        first = jnp.exp2((first - top) * SCALE)
        last = jnp.exp2((last - top) * SCALE)
        share = 1.0 / (
            jnp.sum(first, axis=0, keepdims=True) + jnp.sum(last, axis=0, keepdims=True)
        )
        weights = jnp.concatenate(
            [(first * share).astype(jnp.bfloat16), (last * share).astype(jnp.bfloat16)], axis=0
        )
        total += jnp.dot(weights, grad, preferred_element_type=jnp.float32)
    early_ref[...] = total[:rows].astype(early_ref.dtype)
    own_ref[...] = total[rows:]


def attended(second, queries, earlier, keys, out_grad):
    rows = queries.shape[0]
    wide = pl.BlockSpec((rows, PER * HD), lambda g: (0, g))
    narrow = pl.BlockSpec((rows, HD), lambda g: (0, g))
    return pl.pallas_call(
        attend_kernel,
        name="attend",
        grid=(KVH,),
        out_shape=(
            jax.ShapeDtypeStruct((rows, KVH * HD), jnp.bfloat16),
            jax.ShapeDtypeStruct((rows, KVH * HD), jnp.float32),
        ),
        in_specs=[pl.BlockSpec(memory_space=pltpu.SMEM), wide, narrow, narrow, wide],
        out_specs=(narrow, narrow),
        cost_estimate=pl.CostEstimate(
            flops=4 * H * rows * 2 * rows * HD,
            bytes_accessed=6 * 2**20,
            transcendentals=H * rows * 2 * rows,
        ),
        compiler_params=pltpu.CompilerParams(vmem_limit_bytes=16 * 2**20),
    )(second, queries, earlier, keys, out_grad)


def multiply_kernel(place_ref, columns_ref, *refs):
    grads, out_ref = refs[:-1], refs[-1]
    chip, core = place_ref[0], place_ref[1]
    tile = 128

    def step(number, carry):
        at = pl.ds(pl.multiple_of(number * tile, tile), tile)
        total = None
        for side in range(2):
            for back in range(0, CHIPS, 2):
                left = jnp.concatenate(
                    [
                        columns_ref[lax.rem(chip + CHIPS - back - more, CHIPS), lax.rem(core + side, 2), at, :]
                        for more in range(2)
                    ],
                    axis=1,
                )
                right = jnp.concatenate(
                    [grads[side * CHIPS + back + more][...] for more in range(2)], axis=0
                )
                term = jnp.dot(left, right, preferred_element_type=jnp.float32)
                total = term if total is None else total + term
        out_ref[at, :] = total.astype(out_ref.dtype)
        return carry

    lax.fori_loop(0, out_ref.shape[0] // tile, step, 0)


def multiplied(where, columns, grads):
    rows, width = columns.shape[2], grads[0].shape[1]
    whole = pl.BlockSpec(memory_space=pltpu.VMEM)
    return pl.pallas_call(
        multiply_kernel,
        name="multiply",
        out_shape=jax.ShapeDtypeStruct((rows, width), jnp.bfloat16),
        in_specs=[pl.BlockSpec(memory_space=pltpu.SMEM)] + [whole] * (1 + len(grads)),
        out_specs=whole,
        cost_estimate=pl.CostEstimate(
            flops=2 * rows * len(grads) * grads[0].shape[0] * width,
            bytes_accessed=8 * 2**20,
            transcendentals=0,
        ),
        compiler_params=pltpu.CompilerParams(vmem_limit_bytes=24 * 2**20),
    )(where, columns, *grads)


def place(axis):
    return lax.axis_index(axis).astype(jnp.int32).reshape(1)


def body(activations, queries, keys, out_grad, layout):
    near = lax.axis_size(NEAR)
    earlier = lax.ppermute(keys, "zl", [(0, 1)])
    columns = gathered(activations, layout, near)
    columns = lax.all_to_all(columns, NEAR, 0, 0, tiled=True)
    early, own = attended(place("zl"), queries, earlier, keys, out_grad)
    returned = lax.ppermute(early, "zl", [(1, 0)])
    value_grad = (own + returned.astype(jnp.float32)).astype(jnp.bfloat16)
    mine = [value_grad] + [
        lax.ppermute(value_grad, "x", [(i, (i + ahead) % CHIPS) for i in range(CHIPS)])
        for ahead in range(1, CHIPS)
    ]
    other = [lax.ppermute(part, "c", [(0, 1), (1, 0)]) for part in mine]
    term = multiplied(
        jnp.concatenate([place("x"), place("c")]),
        columns.reshape(CHIPS, 2, *columns.shape[1:]),
        mine + other,
    )
    width = KVH * HD
    parts = lax.all_to_all(term.reshape(lax.axis_size("y"), -1, width), "y", 0, 0, tiled=True)
    half = jnp.sum(parts.astype(jnp.float32), axis=0).astype(jnp.bfloat16)
    parts = lax.all_to_all(half.reshape(-1, OWNED, width), ("zh", "zl"), 0, 0, tiled=True)
    return jnp.sum(parts.astype(jnp.float32), axis=0)


def solution(mesh):
    finer = Mesh(mesh.devices.reshape(4, 4, 4, 2, mesh.shape["seq"]), AXES)
    placed = (P(AXES, None), P(AXES, None), P(AXES, None), P(AXES, None), P())
    return jax.shard_map(
        body, mesh=finer, in_specs=placed, out_specs=P(AXES, None), check_vma=False
    )
```

time: 658 us -> 135 us (0.21)
  waiting for transfers between devices: 502 us -> 25.3 us
  local copies, waits for them, and re-layouts: 80.2 us -> 3.95 us
  blocking collectives: 0 us -> 54.6 us
  matrix products: 37.5 us -> 0 us
  Pallas kernels: 0 us -> 34 us
  other arithmetic: 19 us -> 1.28 us
  between operations: 13.4 us -> 0.08 us
  starting transfers between devices: 4.63 us -> 13.7 us
    reduce_scatter x2 -> x0, waiting for transfers between devices: 445 us -> none  [the longest x1 413 us: summed_rows_2(): return lax.psum_scatter(blocks, chips, scatter_dimension=0, tiled=True)[0]]
    all_to_all x0 -> x2, blocking collectives: none -> 54.6 us  [the longest x1 30.9 us: body(): lax.all_to_all(term.reshape(lax.axis_size('y'), -1, width), 'y', 0, 0, ti...]
    all_gather x1 -> x0, waiting for transfers between devices: 46.7 us -> none  [side_by_side(): lax.all_gather(both, axis, axis=dim, tiled=True)]
    gather x2 -> x0, local copies, waits for them, and re-layouts: 38.8 us -> none  [body(): columns = jnp.take(pair_rows, jnp.take(layout, buffer_rows), axis=1)]
    pallas_call x0 -> x3, Pallas kernels: none -> 34 us  [the longest x1 20.7 us: gathered(): pl.pallas_call(gather_kernel, name='gather_rows', out_shape=jax.ShapeDtyp...]
    dot_general x17 -> x0, matrix products: 33.9 us -> none  [the longest x8 18.1 us: local_values(): jnp.einsum('gij,igd->jd', weights, grad_block, preferred_element_type=jnp...]
    ppermute x2 -> x9, waiting for transfers between devices: 10.9 us -> 25.3 us  [the longest x3 9.22 us: body(): lax.ppermute(value_grad, 'x', [(i, (i + ahead) % CHIPS) for i in range(CH...]
    reshape x1 -> x0, local copies, waits for them, and re-layouts: 11.8 us -> none  [summed_rows_2(): blocks = blocks.reshape(*sizes, *inside).swapaxes(0, 1).reshape(-1, *inside)]
  transfers between devices with their start and end apart: 5 -> 10, of which waited for: 4 -> 7; matrix products, arithmetic and copies ran while one was open for 7% -> 0% of each run, Pallas kernels for 0% -> 6%
where the time goes in v1:
time: 135 us; the launch traced here: 133 us
  blocking collectives  54.6 us (40%)
  Pallas kernels  34 us (25%)
  waiting for transfers between devices  25.3 us (19%)
  starting transfers between devices  13.7 us (10%)
  local copies, waits for them, and re-layouts  3.95 us (3%)
    all_to_all x1, blocking collectives, body(): lax.all_to_all(term.reshape(lax.axis_size('y'), -1, width), 'y', 0, 0, ti...  30.9 us
    all_to_all x1, blocking collectives, body(): lax.all_to_all(half.reshape(-1, OWNED, width), ('zh', 'zl'), 0, 0, tiled=...  23.7 us
    pallas_call x1, Pallas kernels, gathered(): pl.pallas_call(gather_kernel, name='gather_rows', out_shape=jax.ShapeDtyp...  20.7 us
    ppermute x3, waiting for transfers between devices, body(): lax.ppermute(value_grad, 'x', [(i, (i + ahead) % CHIPS) for i in range(CH...  9.22 us
    ppermute x1, waiting for transfers between devices, body(): returned = lax.ppermute(early, 'zl', [(1, 0)])  8.6 us
    pallas_call x1, Pallas kernels, attended(): pl.pallas_call(attend_kernel, name='attend', grid=(KVH,), out_shape=(jax....  8.11 us
    ppermute x1, waiting for transfers between devices, body(): earlier = lax.ppermute(keys, 'zl', [(0, 1)])  6.12 us
    ppermute x3, starting transfers between devices, body(): lax.ppermute(value_grad, 'x', [(i, (i + ahead) % CHIPS) for i in range(CH...  5.54 us
  transfers between devices with their start and end apart: 10, of which 7 were waited for; matrix products, arithmetic and copies ran while one was open for 0% of the time, Pallas kernels for 6%

profile of v1, /device:TPU:0, one launch (start us, length us, event | category | flops | bytes accessed | tf_op | source)
XLA Modules:
  0.0 132.9 jit_solution(18408763283335543435)
XLA Ops:
  0.0 1.6 %copy-done.2 = bf16[128,8192]{1,0:T(8,128)(2,1)S(1)} copy-done((bf16[128,8192]{1,0:T(8,128)(2,1)S(1)}, bf16[128,8192]{1,0:T(8,128)(2,1)}, u32[]{:S(2)}) %copy-start.2) | copy-done | bytes 2097176
  1.6 0.8 copy-done.4
  2.4 20.7 %gather_rows.1 = bf16[8,1024,128]{2,1,0:T(8,128)(2,1)} custom-call(s32[8192]{0:T(1024)S(1)} %copy-done.4, bf16[128,8192]{1,0:T(8,128)(2,1)S(1)} %copy-done.2), custom_call_target="tpu_custom_call" | custom-call | flops 1000000000 | bytes 4194304 | tf_op jit(solution)/shard_map/gather_rows/pallas_call | solution.py:50
  23.1 4.5 %all-to-all-start = ((bf16[8,1024,128]{2,1,0:T(8,128)(2,1)}), bf16[8,1024,128]{2,1,0:T(8,128)(2,1)}, u32[]{:S(2)}, u32[]{:S(2)}) async-start(bf16[8,1024,128]{2,1,0:T(8,128)(2,1)} %gather_rows.1), calls=%async_computation | async-start | bytes 4194304 | tf_op jit(solution)/shard_map/all_to_all | solution.py:175
  27.6 2.1 %collective-permute-start = (bf16[128,1024]{1,0:T(8,128)(2,1)S(1)}, bf16[128,1024]{1,0:T(8,128)(2,1)S(1)}, u32[]{:S(2)}, u32[]{:S(2)}) collective-permute-start(bf16[128,1024]{1,0:T(8,128)(2,1)S(1)} %copy-done.3), channel_id=1, source_target_pairs={{0,1},{2,3},{4,5},{6,7},{8,9},{10,11},{12,13},{14,15},{16,17},{18,... | collective-permute-start | bytes 786440 | tf_op jit(solution)/shard_map/ppermute | solution.py:173
  29.7 6.1 %collective-permute-done.earlier_ref = bf16[128,1024]{1,0:T(8,128)(2,1)S(1)} collective-permute-done((bf16[128,1024]{1,0:T(8,128)(2,1)S(1)}, bf16[128,1024]{1,0:T(8,128)(2,1)S(1)}, u32[]{:S(2)}, u32[]{:S(2)}) %collective-permute-start) | collective-permute-done | bytes 262176 | tf_op jit(solution)/shard_map/ppermute | solution.py:173
  35.8 1.6 %copy-done.1 = bf16[128,8192]{1,0:T(8,128)(2,1)S(1)} copy-done((bf16[128,8192]{1,0:T(8,128)(2,1)S(1)}, bf16[128,8192]{1,0:T(8,128)(2,1)}, u32[]{:S(2)}) %copy-start.1) | copy-done | bytes 2097176
  37.4 8.1 %attend.1 = (bf16[128,1024]{1,0:T(8,128)(2,1)S(1)}, f32[128,1024]{1,0:T(8,128)S(1)}) custom-call(s32[1]{0:T(128)} %bitcast.3.second_ref, bf16[128,8192]{1,0:T(8,128)(2,1)S(1)} %copy-done, bf16[128,1024]{1,0:T(8,128)(2,1)S(1)} %collective-permute-done.earlier_ref, bf16[128,1024]{1,0:T(8,128)(2,1)S(1)} %copy-done.3, bf16[128,8192]{1,0:T(8,128)(2,1)S(1)} %copy-done.1), custom_call_target="tpu_custom_call" | custom-call | flops 1073741824 | bytes 6291456 | tf_op jit(solution)/shard_map/attend/pallas_call | solution.py:102
  45.5 1.3 collective-permute-start.1
  46.8 8.6 %collective-permute-done.1 = bf16[128,1024]{1,0:T(8,128)(2,1)S(1)} collective-permute-done((bf16[128,1024]{1,0:T(8,128)(2,1)S(1)}, bf16[128,1024]{1,0:T(8,128)(2,1)S(1)}, u32[]{:S(2)}, u32[]{:S(2)}) %collective-permute-start.1) | collective-permute-done | bytes 262176 | tf_op jit(solution)/shard_map/ppermute | solution.py:177
  55.5 1.4 %collective-permute-start.2 = (bf16[128,1024]{1,0:T(8,128)(2,1)S(1)}, bf16[128,1024]{1,0:T(8,128)(2,1)S(1)}, u32[]{:S(2)}, u32[]{:S(2)}) collective-permute-start(bf16[128,1024]{1,0:T(8,128)(2,1)S(1)} %add_convert_fusion.refs_0_), channel_id=1, source_target_pairs={{0,4},{4,8},{8,12},{12,0},{1,5},{5,9},{9,13},{13,1},{2,6},{6,10},{... | collective-permute-start | bytes 786440 | tf_op jit(solution)/shard_map/ppermute | solution.py:180
  56.9 2.7 %collective-permute-start.3 = (bf16[128,1024]{1,0:T(8,128)(2,1)S(1)}, bf16[128,1024]{1,0:T(8,128)(2,1)S(1)}, u32[]{:S(2)}, u32[]{:S(2)}) collective-permute-start(bf16[128,1024]{1,0:T(8,128)(2,1)S(1)} %add_convert_fusion.refs_0_), channel_id=1, source_target_pairs={{0,8},{4,12},{8,0},{12,4},{1,9},{5,13},{9,1},{13,5},{2,10},{6,14},... | collective-permute-start | bytes 786440 | tf_op jit(solution)/shard_map/ppermute | solution.py:180
  59.6 1.5 %collective-permute-start.4 = (bf16[128,1024]{1,0:T(8,128)(2,1)S(1)}, bf16[128,1024]{1,0:T(8,128)(2,1)S(1)}, u32[]{:S(2)}, u32[]{:S(2)}) collective-permute-start(bf16[128,1024]{1,0:T(8,128)(2,1)S(1)} %add_convert_fusion.refs_0_), channel_id=1, source_target_pairs={{0,12},{4,0},{8,4},{12,8},{1,13},{5,1},{9,5},{13,9},{2,14},{6,2},{... | collective-permute-start | bytes 786440 | tf_op jit(solution)/shard_map/ppermute | solution.py:180
  61.0 5.0 %collective-permute-done.2.refs_1_ = bf16[128,1024]{1,0:T(8,128)(2,1)S(1)} collective-permute-done((bf16[128,1024]{1,0:T(8,128)(2,1)S(1)}, bf16[128,1024]{1,0:T(8,128)(2,1)S(1)}, u32[]{:S(2)}, u32[]{:S(2)}) %collective-permute-start.2) | collective-permute-done | bytes 262176 | tf_op jit(solution)/shard_map/ppermute | solution.py:180
  66.0 4.0 %collective-permute-done.3.refs_2_ = bf16[128,1024]{1,0:T(8,128)(2,1)S(1)} collective-permute-done((bf16[128,1024]{1,0:T(8,128)(2,1)S(1)}, bf16[128,1024]{1,0:T(8,128)(2,1)S(1)}, u32[]{:S(2)}, u32[]{:S(2)}) %collective-permute-start.3) | collective-permute-done | bytes 262176 | tf_op jit(solution)/shard_map/ppermute | solution.py:180
  70.0 0.3 collective-permute-done.4.refs_3_
  70.3 0.2 collective-permute-start.8
  70.6 0.9 collective-permute-done.7.refs_6_
  71.5 0.4 collective-permute-done.8.refs_7_
  71.9 5.2 %multiply.1 = bf16[1024,1024]{1,0:T(8,128)(2,1)S(1)} custom-call(s32[2]{0:T(128)S(1)} %pad_add_fusion.place_ref, bf16[4,2,1024,128]{3,2,1,0:T(8,128)(2,1)} %bitcast.2.columns_ref, bf16[128,1024]{1,0:T(8,128)(2,1)S(1)} %add_convert_fusion.refs_0_, bf16[128,1024]{1,0:T(8,128)(2,1)S(1)} %collective-permute-done.2.refs_1_, ...), custom_call_target="tpu_custom_call" | custom-call | flops 2147483648 | bytes 8388608 | tf_op jit(solution)/shard_map/multiply/pallas_call | solution.py:152
  77.1 30.9 %all_to_all.15 = bf16[4,256,1024]{2,1,0:T(8,128)(2,1)S(1)} all-to-all(bf16[4,256,1024]{2,1,0:T(8,128)(2,1)S(1)} %bitcast.6), channel_id=1, replica_groups=mesh['y'=4,'zh'=4,'x'=4,'c'=2,'zl'=2] {'y'}, dimensions={0} | all-to-all | bytes 4194304 | tf_op jit(solution)/shard_map/all_to_all | solution.py:190
  108.0 0.4 reduce_sum.21
  108.5 23.7 %all_to_all.16 = bf16[8,32,1024]{2,1,0:T(8,128)(2,1)S(1)} all-to-all(bf16[8,32,1024]{2,1,0:T(8,128)(2,1)S(1)} %bitcast.7), channel_id=1, replica_groups=mesh['y'=4,'zh'=4,'x'=4,'c'=2,'zl'=2] {'zh','zl'}, dimensions={0} | all-to-all | bytes 1048576 | tf_op jit(solution)/shard_map/all_to_all | solution.py:192
  132.2 0.7 convert_reduce_fusion
  (15 shorter events, 0.2 us)
Async XLA Ops:
  0.0 1.6 %copy-start.2 = (bf16[128,8192]{1,0:T(8,128)(2,1)S(1)}, bf16[128,8192]{1,0:T(8,128)(2,1)}, u32[]{:S(2)}) copy-start(bf16[128,8192]{1,0:T(8,128)(2,1)} %acts_ref.1) | copy-start | bytes 6291460
  1.6 0.8 copy-start.4
  23.1 4.5 %copy-start.3 = (bf16[128,1024]{1,0:T(8,128)(2,1)S(1)}, bf16[128,1024]{1,0:T(8,128)(2,1)}, u32[]{:S(2)}) copy-start(bf16[128,1024]{1,0:T(8,128)(2,1)} %keys_ref.1) | copy-start | bytes 786436
  23.1 12.8 %copy-start = (bf16[128,8192]{1,0:T(8,128)(2,1)S(1)}, bf16[128,8192]{1,0:T(8,128)(2,1)}, u32[]{:S(2)}) copy-start(bf16[128,8192]{1,0:T(8,128)(2,1)} %queries_ref.1) | copy-start | bytes 6291460
  23.1 48.8 %all-to-all-start = ((bf16[8,1024,128]{2,1,0:T(8,128)(2,1)}), bf16[8,1024,128]{2,1,0:T(8,128)(2,1)}, u32[]{:S(2)}, u32[]{:S(2)}) async-start(bf16[8,1024,128]{2,1,0:T(8,128)(2,1)} %gather_rows.1), calls=%async_computation | async-start | bytes 4194304 | tf_op jit(solution)/shard_map/all_to_all | solution.py:175
  27.6 8.3 %collective-permute-start = (bf16[128,1024]{1,0:T(8,128)(2,1)S(1)}, bf16[128,1024]{1,0:T(8,128)(2,1)S(1)}, u32[]{:S(2)}, u32[]{:S(2)}) collective-permute-start(bf16[128,1024]{1,0:T(8,128)(2,1)S(1)} %copy-done.3), channel_id=1, source_target_pairs={{0,1},{2,3},{4,5},{6,7},{8,9},{10,11},{12,13},{14,15},{16,17},{18,... | collective-permute-start | bytes 786440 | tf_op jit(solution)/shard_map/ppermute | solution.py:173
  35.8 1.6 %copy-start.1 = (bf16[128,8192]{1,0:T(8,128)(2,1)S(1)}, bf16[128,8192]{1,0:T(8,128)(2,1)}, u32[]{:S(2)}) copy-start(bf16[128,8192]{1,0:T(8,128)(2,1)} %grads_ref.1) | copy-start | bytes 6291460
  45.5 9.9 %collective-permute-start.1 = (bf16[128,1024]{1,0:T(8,128)(2,1)S(1)}, bf16[128,1024]{1,0:T(8,128)(2,1)S(1)}, u32[]{:S(2)}, u32[]{:S(2)}) collective-permute-start(bf16[128,1024]{1,0:T(8,128)(2,1)S(1)} %get-tuple-element.8), channel_id=1, source_target_pairs={{1,0},{3,2},{5,4},{7,6},{9,8},{11,10},{13,12},{15,14},{17,16},{19,... | collective-permute-start | bytes 786440 | tf_op jit(solution)/shard_map/ppermute | solution.py:177
  55.5 10.5 %collective-permute-start.2 = (bf16[128,1024]{1,0:T(8,128)(2,1)S(1)}, bf16[128,1024]{1,0:T(8,128)(2,1)S(1)}, u32[]{:S(2)}, u32[]{:S(2)}) collective-permute-start(bf16[128,1024]{1,0:T(8,128)(2,1)S(1)} %add_convert_fusion.refs_0_), channel_id=1, source_target_pairs={{0,4},{4,8},{8,12},{12,0},{1,5},{5,9},{9,13},{13,1},{2,6},{6,10},{... | collective-permute-start | bytes 786440 | tf_op jit(solution)/shard_map/ppermute | solution.py:180
  56.9 13.1 %collective-permute-start.3 = (bf16[128,1024]{1,0:T(8,128)(2,1)S(1)}, bf16[128,1024]{1,0:T(8,128)(2,1)S(1)}, u32[]{:S(2)}, u32[]{:S(2)}) collective-permute-start(bf16[128,1024]{1,0:T(8,128)(2,1)S(1)} %add_convert_fusion.refs_0_), channel_id=1, source_target_pairs={{0,8},{4,12},{8,0},{12,4},{1,9},{5,13},{9,1},{13,5},{2,10},{6,14},... | collective-permute-start | bytes 786440 | tf_op jit(solution)/shard_map/ppermute | solution.py:180
  59.6 10.7 %collective-permute-start.4 = (bf16[128,1024]{1,0:T(8,128)(2,1)S(1)}, bf16[128,1024]{1,0:T(8,128)(2,1)S(1)}, u32[]{:S(2)}, u32[]{:S(2)}) collective-permute-start(bf16[128,1024]{1,0:T(8,128)(2,1)S(1)} %add_convert_fusion.refs_0_), channel_id=1, source_target_pairs={{0,12},{4,0},{8,4},{12,8},{1,13},{5,1},{9,5},{13,9},{2,14},{6,2},{... | collective-permute-start | bytes 786440 | tf_op jit(solution)/shard_map/ppermute | solution.py:180
  61.0 9.5 %collective-permute-start.5 = (bf16[128,1024]{1,0:T(8,128)(2,1)S(1)}, bf16[128,1024]{1,0:T(8,128)(2,1)S(1)}, u32[]{:S(2)}, u32[]{:S(2)}) collective-permute-start(bf16[128,1024]{1,0:T(8,128)(2,1)S(1)} %add_convert_fusion.refs_0_), channel_id=1, source_target_pairs={{0,2},{2,0},{1,3},{3,1},{4,6},{6,4},{5,7},{7,5},{8,10},{10,8},{9,1... | collective-permute-start | bytes 786440 | tf_op jit(solution)/shard_map/ppermute | solution.py:183
  66.0 4.6 %collective-permute-start.6 = (bf16[128,1024]{1,0:T(8,128)(2,1)S(1)}, bf16[128,1024]{1,0:T(8,128)(2,1)S(1)}, u32[]{:S(2)}, u32[]{:S(2)}) collective-permute-start(bf16[128,1024]{1,0:T(8,128)(2,1)S(1)} %collective-permute-done.2.refs_1_), channel_id=1, source_target_pairs={{0,2},{2,0},{1,3},{3,1},{4,6},{6,4},{5,7},{7,5},{8,10},{10,8},{9,1... | collective-permute-start | bytes 786440 | tf_op jit(solution)/shard_map/ppermute | solution.py:183
  70.0 1.5 %collective-permute-start.7 = (bf16[128,1024]{1,0:T(8,128)(2,1)S(1)}, bf16[128,1024]{1,0:T(8,128)(2,1)S(1)}, u32[]{:S(2)}, u32[]{:S(2)}) collective-permute-start(bf16[128,1024]{1,0:T(8,128)(2,1)S(1)} %collective-permute-done.3.refs_2_), channel_id=1, source_target_pairs={{0,2},{2,0},{1,3},{3,1},{4,6},{6,4},{5,7},{7,5},{8,10},{10,8},{9,1... | collective-permute-start | bytes 786440 | tf_op jit(solution)/shard_map/ppermute | solution.py:183
  70.3 1.6 %collective-permute-start.8 = (bf16[128,1024]{1,0:T(8,128)(2,1)S(1)}, bf16[128,1024]{1,0:T(8,128)(2,1)S(1)}, u32[]{:S(2)}, u32[]{:S(2)}) collective-permute-start(bf16[128,1024]{1,0:T(8,128)(2,1)S(1)} %collective-permute-done.4.refs_3_), channel_id=1, source_target_pairs={{0,2},{2,0},{1,3},{3,1},{4,6},{6,4},{5,7},{7,5},{8,10},{10,8},{9,1... | collective-permute-start | bytes 786440 | tf_op jit(solution)/shard_map/ppermute | solution.py:183

commit v2 on v0

v2 whole, which is shorter than its diff:
```python
import functools

import jax
import jax.numpy as jnp
from jax import lax
from jax.experimental import pallas as pl
from jax.experimental.pallas import tpu as pltpu
from jax.sharding import Mesh
from jax.sharding import PartitionSpec as P


H = 64
KVH = 8
HD = 128
WIDTH = KVH * HD
PER = H // KVH
AXES = ("y", "zh", "x", "c", "zl")
Z = ("zh", "zl")
SIDE, Z_SIZE = 4, 8
OWNED = 32
PART = OWNED // 2
SCALE = 1.4426950408889634 / float(HD) ** 0.5
SMEM = pl.BlockSpec(memory_space=pltpu.SMEM)
VMEM = pl.BlockSpec(memory_space=pltpu.VMEM)


def flip(acts_ref, flipped, landed, arrivals):
    width = acts_ref.shape[1]
    count = arrivals.shape[0]
    share = width // count

    def arriving(part):
        at = pl.ds(pl.multiple_of(part * share, share), share)
        return pltpu.make_async_copy(acts_ref.at[:, at], landed.at[:, at], arrivals.at[part])

    for part in range(count):
        arriving(part).start()

    def step(part, carry):
        arriving(part).wait()
        for tile in range(share // 128):
            at = pl.ds(pl.multiple_of(part * share + tile * 128, 128), 128)
            flipped[at, :] = landed[:, at].astype(jnp.float32).T
        return carry

    lax.fori_loop(0, count, step, 0)


def pick(routes, place_ref, layout_ref, flipped, picked, outs):
    y, z, x, core = (place_ref[i] for i in range(4))
    for (axis, steps), out_ref in zip(routes, outs):

        def step(tile, carry):
            to_core, off = (core + (tile >> 2)) & 1, tile & (SIDE - 1)
            x_steps, y_steps = (steps, off) if axis == "x" else (off, steps)
            to_x, to_y = (x + x_steps) & (SIDE - 1), (y + y_steps) & (SIDE - 1)
            for block in range(Z_SIZE):
                to_z = (z + block) & (Z_SIZE - 1)
                owner = ((((to_y * 4 + (to_z >> 1)) * 4 + to_x) * 2 + to_core) * 2) + (to_z & 1)
                base = owner * OWNED + (0 if axis == "x" else PART)
                for row in range(PART):
                    source = layout_ref[base + row]
                    at = block * PART + row
                    picked[at : at + 1, :] = flipped[pl.ds(source, 1), :]
            rows = Z_SIZE * PART
            out_ref[pl.ds(pl.multiple_of(tile * rows, rows), rows), :] = picked[...].astype(
                jnp.bfloat16
            )
            return carry

        lax.fori_loop(0, 2 * SIDE, step, 0)


def first_pick_kernel(routes, place_ref, layout_ref, acts_ref, flipped, *refs):
    outs = refs[: len(routes)]
    picked, landed, arrivals, rows_ref, rows_arrival = refs[len(routes) :]
    rows_copy = pltpu.make_async_copy(layout_ref, rows_ref, rows_arrival)
    rows_copy.start()
    flip(acts_ref, flipped, landed, arrivals)
    rows_copy.wait()
    pick(routes, place_ref, rows_ref, flipped, picked, outs)


def later_pick_kernel(routes, place_ref, layout_ref, flipped, *refs):
    pick(routes, place_ref, layout_ref, flipped, refs[-1], refs[:-1])


def picked_rows(routes, where, layout, source, first):
    tokens = 128
    width = layout.shape[0]
    piece = jax.ShapeDtypeStruct((2 * SIDE * Z_SIZE * PART, tokens), jnp.bfloat16)
    shapes = [piece] * len(routes)
    scratch = [pltpu.VMEM((Z_SIZE * PART, tokens), jnp.float32)]
    if first:
        shapes = [jax.ShapeDtypeStruct((width, tokens), jnp.float32)] + shapes
        scratch += [
            pltpu.VMEM((tokens, width), jnp.bfloat16),
            pltpu.SemaphoreType.DMA((8,)),
            pltpu.SMEM((width,), jnp.int32),
            pltpu.SemaphoreType.DMA,
        ]
    far = pl.BlockSpec(memory_space=pl.ANY)
    return pl.pallas_call(
        functools.partial(first_pick_kernel if first else later_pick_kernel, routes),
        name="pick",
        out_shape=tuple(shapes),
        in_specs=[SMEM, far, far] if first else [SMEM, SMEM, VMEM],
        out_specs=tuple([VMEM] * len(shapes)),
        scratch_shapes=scratch,
        cost_estimate=pl.CostEstimate(
            flops=10**9 * len(routes), bytes_accessed=4 * 2**20, transcendentals=0
        ),
        compiler_params=pltpu.CompilerParams(vmem_limit_bytes=16 * 2**20),
    )(where, layout, source)


def attend_kernel(
    first, groups, place_ref, queries_ref, earlier_ref, keys_ref, grads_ref, early_ref, own_ref
):
    rows = queries_ref.shape[0]
    second = (place_ref[1] & 1) > 0
    shape = (rows, rows)
    causal = lax.broadcasted_iota(jnp.int32, shape, 0) <= lax.broadcasted_iota(jnp.int32, shape, 1)

    def group(number, carry):
        head = pl.ds(pl.multiple_of((number + first) * HD, HD), HD)
        both = jnp.concatenate([earlier_ref[:, head], keys_ref[:, head]], axis=0)
        total = jnp.zeros((2 * rows, HD), jnp.float32)
        for query_head in range(PER):
            at = pl.ds(pl.multiple_of(((number + first) * PER + query_head) * HD, HD), HD)
            scores = lax.dot_general(
                both, queries_ref[:, at], (((1,), (1,)), ((), ())), preferred_element_type=jnp.float32
            )
            before = jnp.where(second, scores[:rows], -1e30)
            last = jnp.where(causal, scores[rows:], -1e30)
            top = jnp.maximum(
                jnp.max(before, axis=0, keepdims=True), jnp.max(last, axis=0, keepdims=True)
            )
            before = jnp.exp2((before - top) * SCALE)
            last = jnp.exp2((last - top) * SCALE)
            share = 1.0 / (
                jnp.sum(before, axis=0, keepdims=True) + jnp.sum(last, axis=0, keepdims=True)
            )
            weights = jnp.concatenate(
                [(before * share).astype(jnp.bfloat16), (last * share).astype(jnp.bfloat16)], axis=0
            )
            total += jnp.dot(weights, grads_ref[:, at], preferred_element_type=jnp.float32)
        out = pl.ds(pl.multiple_of(number * HD, HD), HD)
        early_ref[:, out] = total[:rows].astype(early_ref.dtype)
        own_ref[:, out] = total[rows:]
        return carry

    lax.fori_loop(0, groups, group, 0)


def attended(first, groups, where, queries, earlier, keys, out_grad):
    rows = queries.shape[0]
    return pl.pallas_call(
        functools.partial(attend_kernel, first, groups),
        name="attend",
        out_shape=(
            jax.ShapeDtypeStruct((rows, groups * HD), jnp.bfloat16),
            jax.ShapeDtypeStruct((rows, groups * HD), jnp.float32),
        ),
        in_specs=[SMEM, VMEM, VMEM, VMEM, VMEM],
        out_specs=(VMEM, VMEM),
        cost_estimate=pl.CostEstimate(
            flops=4 * groups * PER * rows * 2 * rows * HD,
            bytes_accessed=3 * 2**20,
            transcendentals=groups * PER * rows * 2 * rows,
        ),
        compiler_params=pltpu.CompilerParams(vmem_limit_bytes=16 * 2**20),
    )(where, queries, earlier, keys, out_grad)


def multiply_kernel(*refs):
    columns, grads, (own_ref, away_ref) = refs[:SIDE], refs[SIDE : 2 * SIDE], refs[2 * SIDE :]
    tile = 256
    half = own_ref.shape[0]
    for number in range(2 * half // tile):
        at = slice(number * tile, (number + 1) * tile)
        total = None
        for i in range(0, SIDE, 2):
            left = jnp.concatenate([columns[i][at, :], columns[i + 1][at, :]], axis=1)
            right = jnp.concatenate([grads[i][...], grads[i + 1][...]], axis=0)
            term = jnp.dot(left, right, preferred_element_type=jnp.float32)
            total = term if total is None else total + term
        if number * tile < half:
            own_ref[at, :] = total
        else:
            away_ref[number * tile - half : (number + 1) * tile - half, :] = total.astype(
                away_ref.dtype
            )


def multiplied(columns, grads):
    half = columns[0].shape[0] // 2
    return pl.pallas_call(
        multiply_kernel,
        name="multiply",
        out_shape=(
            jax.ShapeDtypeStruct((half, WIDTH), jnp.float32),
            jax.ShapeDtypeStruct((half, WIDTH), jnp.bfloat16),
        ),
        in_specs=[VMEM] * (2 * SIDE),
        out_specs=(VMEM, VMEM),
        cost_estimate=pl.CostEstimate(
            flops=4 * half * SIDE * 128 * WIDTH, bytes_accessed=4 * 2**20, transcendentals=0
        ),
        compiler_params=pltpu.CompilerParams(vmem_limit_bytes=16 * 2**20),
    )(*columns, *grads)


def merge_kernel(own_ref, got_ref, *outs):
    rows = outs[0].shape[0]
    for number, out_ref in enumerate(outs):
        at = slice(number * rows, (number + 1) * rows)
        out_ref[...] = (own_ref[at, :] + got_ref[at, :].astype(jnp.float32)).astype(out_ref.dtype)


def merged(own, got):
    shape = jax.ShapeDtypeStruct((own.shape[0] // SIDE, WIDTH), jnp.bfloat16)
    return pl.pallas_call(
        merge_kernel,
        name="merge",
        out_shape=tuple([shape] * SIDE),
        in_specs=[VMEM, VMEM],
        out_specs=tuple([VMEM] * SIDE),
        cost_estimate=pl.CostEstimate(flops=5 * 10**8, bytes_accessed=2**20, transcendentals=0),
        compiler_params=pltpu.CompilerParams(vmem_limit_bytes=4 * 2**20),
    )(own, got)


def halfway_kernel(place_ref, *refs):
    out_ref = refs[-1]
    z = place_ref[1]
    for way in range(2):
        parts = refs[way * SIDE : (way + 1) * SIDE]
        for block in range(Z_SIZE):
            at = slice(block * PART, (block + 1) * PART)
            total = parts[0][at, :].astype(jnp.float32)
            for part in parts[1:]:
                total += part[at, :].astype(jnp.float32)
            out_ref[(z + block) & (Z_SIZE - 1), way * PART : (way + 1) * PART, :] = total.astype(
                out_ref.dtype
            )


def halfway(where, parts):
    return pl.pallas_call(
        halfway_kernel,
        name="halfway",
        out_shape=jax.ShapeDtypeStruct((Z_SIZE, OWNED, WIDTH), jnp.bfloat16),
        in_specs=[SMEM] + [VMEM] * len(parts),
        out_specs=VMEM,
        cost_estimate=pl.CostEstimate(flops=5 * 10**8, bytes_accessed=2**20, transcendentals=0),
        compiler_params=pltpu.CompilerParams(vmem_limit_bytes=4 * 2**20),
    )(where, *parts)


def finish_kernel(parts_ref, out_ref):
    total = parts_ref[0].astype(jnp.float32)
    for part in range(1, Z_SIZE):
        total += parts_ref[part].astype(jnp.float32)
    out_ref[...] = total


def finished(parts):
    return pl.pallas_call(
        finish_kernel,
        name="finish",
        out_shape=jax.ShapeDtypeStruct((OWNED, WIDTH), jnp.float32),
        in_specs=[VMEM],
        out_specs=VMEM,
        cost_estimate=pl.CostEstimate(flops=5 * 10**8, bytes_accessed=2**20, transcendentals=0),
        compiler_params=pltpu.CompilerParams(vmem_limit_bytes=4 * 2**20),
    )(parts)


def ahead(value, axis, steps):
    count = lax.axis_size(axis)
    return lax.ppermute(value, axis, [(i, (i + steps) % count) for i in range(count)])


FAR = (("x", 2), ("y", 2))
NEXT = (("x", 1), ("x", 3), ("y", 1), ("y", 3))
HERE = (("x", 0), ("y", 0))


def body(activations, queries, keys, out_grad, layout):
    where = jnp.stack([lax.axis_index(axis).astype(jnp.int32) for axis in ("y", Z, "x", "c")])
    columns = {}
    earlier = lax.ppermute(keys, "zl", [(0, 1)])
    flipped, *pieces = picked_rows(FAR, where, layout, activations, True)
    for route, piece in zip(FAR, pieces):
        columns[route] = ahead(piece, *route)
    groups = KVH // 2
    own, returned = [], []
    for half in range(2):
        early, mine = attended(half * groups, groups, where, queries, earlier, keys, out_grad)
        own.append(mine)
        returned.append(lax.ppermute(early, "zl", [(1, 0)]))
    pieces = picked_rows(NEXT, where, layout, flipped, False)
    for route, piece in zip(NEXT, pieces):
        columns[route] = ahead(piece, *route)
    pieces = picked_rows(HERE, where, layout, flipped, False)
    columns.update(zip(HERE, pieces))
    value_grad = jnp.concatenate(
        [(a + b.astype(jnp.float32)).astype(jnp.bfloat16) for a, b in zip(own, returned)], axis=1
    )
    grads = {route: value_grad for route in HERE}
    for route in FAR + NEXT:
        grads[route] = ahead(value_grad, *route)
    parts = []
    for way, across in (("x", "y"), ("y", "x")):
        routes = [(way, steps) for steps in range(SIDE)]
        kept, away = multiplied([columns[r] for r in routes], [grads[r] for r in routes])
        got = ahead(away, "c", 1)
        terms = merged(kept, got)
        parts += [terms[0]] + [ahead(terms[i], across, i) for i in range(1, SIDE)]
    terms = halfway(where, parts)
    terms = lax.all_to_all(terms, Z, 0, 0, tiled=True)
    return finished(terms)


def solution(mesh):
    finer = Mesh(mesh.devices.reshape(4, 4, 4, 2, mesh.shape["seq"]), AXES)
    placed = (P(AXES, None), P(AXES, None), P(AXES, None), P(AXES, None), P())
    return jax.shard_map(
        body, mesh=finer, in_specs=placed, out_specs=P(AXES, None), check_vma=False
    )
```

time: 658 us -> 115 us (0.17)
  the two profiles are of different devices: /device:TPU:0 before, /device:TPU:2 now
where the time goes in v2:
time: 115 us; the launch traced here: 114 us
  starting transfers between devices  37.3 us (32%)
  waiting for transfers between devices  25.2 us (22%)
  blocking collectives  25 us (22%)
  Pallas kernels  24.1 us (21%)
  local copies, waits for them, and re-layouts  2.36 us (2%)
    ppermute x20, starting transfers between devices, ahead(): lax.ppermute(value, axis, [(i, (i + steps) % count) for i in range(count)])  30.9 us
    all_to_all x1, blocking collectives, body(): terms = lax.all_to_all(terms, Z, 0, 0, tiled=True)  25 us
    ppermute x20, waiting for transfers between devices, ahead(): lax.ppermute(value, axis, [(i, (i + steps) % count) for i in range(count)])  19.7 us
    pallas_call x3, Pallas kernels, picked_rows(): pl.pallas_call(functools.partial(first_pick_kernel if first else later_pi...  13 us
    pallas_call x2, Pallas kernels, attended(): pl.pallas_call(functools.partial(attend_kernel, first, groups), name='att...  6.62 us
    ppermute x2, waiting for transfers between devices, body(): returned.append(lax.ppermute(early, 'zl', [(1, 0)]))  5.53 us
    ppermute x1, starting transfers between devices, body(): earlier = lax.ppermute(keys, 'zl', [(0, 1)])  3.83 us
    ppermute x2, starting transfers between devices, body(): returned.append(lax.ppermute(early, 'zl', [(1, 0)]))  2.58 us
  transfers between devices with their start and end apart: 23, of which 10 were waited for; matrix products, arithmetic and copies ran while one was open for 0% of the time, Pallas kernels for 17%

profile of v2, /device:TPU:2, one launch (start us, length us, event | category | flops | bytes accessed | tf_op | source)
XLA Modules:
  0.0 114.4 jit_solution(17752088078596093486)
XLA Ops:
  0.0 3.8 %collective-permute-start.3 = (bf16[128,1024]{1,0:T(8,128)(2,1)}, bf16[128,1024]{1,0:T(8,128)(2,1)S(1)}, u32[]{:S(2)}, u32[]{:S(2)}) collective-permute-start(bf16[128,1024]{1,0:T(8,128)(2,1)} %keys_ref.3), channel_id=1, source_target_pairs={{0,1},{2,3},{4,5},{6,7},{8,9},{10,11},{12,13},{14,15},{16,17},{18,... | collective-permute-start | bytes 786440 | tf_op jit(solution)/shard_map/ppermute | solution.py:293
  3.9 1.6 %copy-done.3 = bf16[128,8192]{1,0:T(8,128)(2,1)S(1)} copy-done((bf16[128,8192]{1,0:T(8,128)(2,1)S(1)}, bf16[128,8192]{1,0:T(8,128)(2,1)}, u32[]{:S(2)}) %copy-start.3) | copy-done | bytes 2097176
  6.3 4.2 %pick.3 = (f32[8192,128]{1,0:T(8,128)S(1)}, bf16[1024,128]{1,0:T(8,128)(2,1)S(1)}, bf16[1024,128]{1,0:T(8,128)(2,1)S(1)}) custom-call(s32[4]{0:T(128)S(1)} %pad_add_fusion.place_ref, s32[8192]{0:T(1024)S(1)} %copy-done.4, bf16[128,8192]{1,0:T(8,128)(2,1)S(1)} %copy-done.3), custom_call_target="tpu_custom_call" | custom-call | flops 2000000000 | bytes 4194304 | tf_op jit(solution)/shard_map/pick/pallas_call | solution.py:103
  10.5 3.3 %attend.3 = (bf16[128,512]{1,0:T(8,128)(2,1)S(1)}, f32[128,512]{1,0:T(8,128)S(1)}) custom-call(s32[4]{0:T(128)S(1)} %pad_add_fusion.place_ref, bf16[128,8192]{1,0:T(8,128)(2,1)S(1)} %copy-done, bf16[128,1024]{1,0:T(8,128)(2,1)S(1)} %collective-permute-done.3.earlier_ref, bf16[128,1024]{1,0:T(8,128)(2,1)S(1)} %copy-done.2, bf16[128,8192]{1,0:T(8,128)(2,1)S(1)} %copy-done.1), custom_call_target="tpu_custom_call" | custom-call | flops 536870912 | bytes 3145728 | tf_op jit(solution)/shard_map/attend/pallas_call | solution.py:158
  15.1 5.6 %pick.5 = (bf16[1024,128]{1,0:T(8,128)(2,1)S(1)}, bf16[1024,128]{1,0:T(8,128)(2,1)S(1)}, bf16[1024,128]{1,0:T(8,128)(2,1)S(1)}, bf16[1024,128]{1,0:T(8,128)(2,1)S(1)}) custom-call(s32[4]{0:T(128)S(1)} %pad_add_fusion.place_ref, s32[8192]{0:T(1024)S(1)} %copy-done.4, f32[8192,128]{1,0:T(8,128)S(1)} %get-tuple-element.30.flipped), custom_call_target="tpu_custom_call" | custom-call | flops 4000000000 | bytes 4194304 | tf_op jit(solution)/shard_map/pick/pallas_call | solution.py:103
  23.4 2.2 %collective-permute-start.2 = (bf16[1024,128]{1,0:T(8,128)(2,1)S(1)}, bf16[1024,128]{1,0:T(8,128)(2,1)S(1)}, u32[]{:S(2)}, u32[]{:S(2)}) collective-permute-start(bf16[1024,128]{1,0:T(8,128)(2,1)S(1)} %get-tuple-element.34), channel_id=1, source_target_pairs={{0,12},{4,0},{8,4},{12,8},{1,13},{5,1},{9,5},{13,9},{2,14},{6,2},{... | collective-permute-start | bytes 786440 | tf_op jit(solution)/shard_map/ppermute | solution.py:282
  25.5 1.6 %collective-permute-start.13 = (bf16[1024,128]{1,0:T(8,128)(2,1)S(1)}, bf16[1024,128]{1,0:T(8,128)(2,1)S(1)}, u32[]{:S(2)}, u32[]{:S(2)}) collective-permute-start(bf16[1024,128]{1,0:T(8,128)(2,1)S(1)} %get-tuple-element.46), channel_id=1, source_target_pairs={{0,64},{64,128},{128,192},{192,0},{1,65},{65,129},{129,193},{193,1... | collective-permute-start | bytes 786440 | tf_op jit(solution)/shard_map/ppermute | solution.py:282
  27.1 3.3 %attend.2 = (bf16[128,512]{1,0:T(8,128)(2,1)S(1)}, f32[128,512]{1,0:T(8,128)S(1)}) custom-call(s32[4]{0:T(128)S(1)} %pad_add_fusion.place_ref, bf16[128,8192]{1,0:T(8,128)(2,1)S(1)} %copy-done, bf16[128,1024]{1,0:T(8,128)(2,1)S(1)} %collective-permute-done.3.earlier_ref, bf16[128,1024]{1,0:T(8,128)(2,1)S(1)} %copy-done.2, bf16[128,8192]{1,0:T(8,128)(2,1)S(1)} %copy-done.1), custom_call_target="tpu_custom_call" | custom-call | flops 536870912 | bytes 3145728 | tf_op jit(solution)/shard_map/attend/pallas_call | solution.py:158
  31.7 5.5 %collective-permute-done.4 = bf16[128,512]{1,0:T(8,128)(2,1)S(1)} collective-permute-done((bf16[128,512]{1,0:T(8,128)(2,1)S(1)}, bf16[128,512]{1,0:T(8,128)(2,1)S(1)}, u32[]{:S(2)}, u32[]{:S(2)}) %collective-permute-start.4) | collective-permute-done | bytes 131104 | tf_op jit(solution)/shard_map/ppermute | solution.py:302
  37.4 3.5 %collective-permute-start.7 = (bf16[128,1024]{1,0:T(8,128)(2,1)S(1)}, bf16[128,1024]{1,0:T(8,128)(2,1)S(1)}, u32[]{:S(2)}, u32[]{:S(2)}) collective-permute-start(bf16[128,1024]{1,0:T(8,128)(2,1)S(1)} %pad_maximum_fusion.refs_4_), channel_id=1, source_target_pairs={{0,8},{4,12},{8,0},{12,4},{1,9},{5,13},{9,1},{13,5},{2,10},{6,14},... | collective-permute-start | bytes 786440 | tf_op jit(solution)/shard_map/ppermute | solution.py:282
  40.9 3.0 %collective-permute-start.14 = (bf16[1024,128]{1,0:T(8,128)(2,1)S(1)}, bf16[1024,128]{1,0:T(8,128)(2,1)S(1)}, u32[]{:S(2)}, u32[]{:S(2)}) collective-permute-start(bf16[1024,128]{1,0:T(8,128)(2,1)S(1)} %get-tuple-element.47), channel_id=1, source_target_pairs={{0,128},{64,192},{128,0},{192,64},{1,129},{65,193},{129,1},{193,65... | collective-permute-start | bytes 786440 | tf_op jit(solution)/shard_map/ppermute | solution.py:282
  47.7 2.9 %collective-permute-start.17 = (bf16[128,1024]{1,0:T(8,128)(2,1)S(1)}, bf16[128,1024]{1,0:T(8,128)(2,1)S(1)}, u32[]{:S(2)}, u32[]{:S(2)}) collective-permute-start(bf16[128,1024]{1,0:T(8,128)(2,1)S(1)} %pad_maximum_fusion.refs_4_), channel_id=1, source_target_pairs={{0,128},{64,192},{128,0},{192,64},{1,129},{65,193},{129,1},{193,65... | collective-permute-start | bytes 786440 | tf_op jit(solution)/shard_map/ppermute | solution.py:282
  52.1 3.3 %pick.4 = (bf16[1024,128]{1,0:T(8,128)(2,1)S(1)}, bf16[1024,128]{1,0:T(8,128)(2,1)S(1)}) custom-call(s32[4]{0:T(128)S(1)} %pad_add_fusion.place_ref, s32[8192]{0:T(1024)S(1)} %copy-done.4, f32[8192,128]{1,0:T(8,128)S(1)} %get-tuple-element.30.flipped), custom_call_target="tpu_custom_call" | custom-call | flops 2000000000 | bytes 4194304 | tf_op jit(solution)/shard_map/pick/pallas_call | solution.py:103
  57.0 2.6 %collective-permute-done.16.refs_5_ = bf16[128,1024]{1,0:T(8,128)(2,1)S(1)} collective-permute-done((bf16[128,1024]{1,0:T(8,128)(2,1)S(1)}, bf16[128,1024]{1,0:T(8,128)(2,1)S(1)}, u32[]{:S(2)}, u32[]{:S(2)}) %collective-permute-start.16) | collective-permute-done | bytes 262176 | tf_op jit(solution)/shard_map/ppermute | solution.py:282
  59.6 4.1 %collective-permute-done.18.refs_7_ = bf16[128,1024]{1,0:T(8,128)(2,1)S(1)} collective-permute-done((bf16[128,1024]{1,0:T(8,128)(2,1)S(1)}, bf16[128,1024]{1,0:T(8,128)(2,1)S(1)}, u32[]{:S(2)}, u32[]{:S(2)}) %collective-permute-start.18) | collective-permute-done | bytes 262176 | tf_op jit(solution)/shard_map/ppermute | solution.py:282
  65.3 1.8 %collective-permute-start.10 = (bf16[128,1024]{1,0:T(8,128)(2,1)S(1)}, bf16[128,1024]{1,0:T(8,128)(2,1)S(1)}, u32[]{:S(2)}, u32[]{:S(2)}) collective-permute-start(bf16[128,1024]{1,0:T(8,128)(2,1)S(1)} %get-tuple-element.42), channel_id=1, source_target_pairs={{0,64},{64,128},{128,192},{192,0},{1,65},{65,129},{129,193},{193,1... | collective-permute-start | bytes 786440 | tf_op jit(solution)/shard_map/ppermute | solution.py:282
  67.0 2.4 %collective-permute-start.11 = (bf16[128,1024]{1,0:T(8,128)(2,1)S(1)}, bf16[128,1024]{1,0:T(8,128)(2,1)S(1)}, u32[]{:S(2)}, u32[]{:S(2)}) collective-permute-start(bf16[128,1024]{1,0:T(8,128)(2,1)S(1)} %get-tuple-element.43), channel_id=1, source_target_pairs={{0,128},{64,192},{128,0},{192,64},{1,129},{65,193},{129,1},{193,65... | collective-permute-start | bytes 786440 | tf_op jit(solution)/shard_map/ppermute | solution.py:282
  69.4 1.8 %collective-permute-start.12 = (bf16[128,1024]{1,0:T(8,128)(2,1)S(1)}, bf16[128,1024]{1,0:T(8,128)(2,1)S(1)}, u32[]{:S(2)}, u32[]{:S(2)}) collective-permute-start(bf16[128,1024]{1,0:T(8,128)(2,1)S(1)} %get-tuple-element.44), channel_id=1, source_target_pairs={{0,192},{64,0},{128,64},{192,128},{1,193},{65,1},{129,65},{193,129... | collective-permute-start | bytes 786440 | tf_op jit(solution)/shard_map/ppermute | solution.py:282
  71.4 1.7 %collective-permute-start.20 = (bf16[128,1024]{1,0:T(8,128)(2,1)S(1)}, bf16[128,1024]{1,0:T(8,128)(2,1)S(1)}, u32[]{:S(2)}, u32[]{:S(2)}) collective-permute-start(bf16[128,1024]{1,0:T(8,128)(2,1)S(1)} %get-tuple-element.52), channel_id=1, source_target_pairs={{0,4},{4,8},{8,12},{12,0},{1,5},{5,9},{9,13},{13,1},{2,6},{6,10},{... | collective-permute-start | bytes 786440 | tf_op jit(solution)/shard_map/ppermute | solution.py:282
  73.1 1.6 %collective-permute-start.21 = (bf16[128,1024]{1,0:T(8,128)(2,1)S(1)}, bf16[128,1024]{1,0:T(8,128)(2,1)S(1)}, u32[]{:S(2)}, u32[]{:S(2)}) collective-permute-start(bf16[128,1024]{1,0:T(8,128)(2,1)S(1)} %get-tuple-element.53), channel_id=1, source_target_pairs={{0,8},{4,12},{8,0},{12,4},{1,9},{5,13},{9,1},{13,5},{2,10},{6,14},... | collective-permute-start | bytes 786440 | tf_op jit(solution)/shard_map/ppermute | solution.py:282
  76.4 5.3 %collective-permute-done.11.refs_2_ = bf16[128,1024]{1,0:T(8,128)(2,1)S(1)} collective-permute-done((bf16[128,1024]{1,0:T(8,128)(2,1)S(1)}, bf16[128,1024]{1,0:T(8,128)(2,1)S(1)}, u32[]{:S(2)}, u32[]{:S(2)}) %collective-permute-start.11) | collective-permute-done | bytes 262176 | tf_op jit(solution)/shard_map/ppermute | solution.py:282
  81.7 2.1 %collective-permute-done.21.refs_6_ = bf16[128,1024]{1,0:T(8,128)(2,1)S(1)} collective-permute-done((bf16[128,1024]{1,0:T(8,128)(2,1)S(1)}, bf16[128,1024]{1,0:T(8,128)(2,1)S(1)}, u32[]{:S(2)}, u32[]{:S(2)}) %collective-permute-start.21) | collective-permute-done | bytes 262176 | tf_op jit(solution)/shard_map/ppermute | solution.py:282
  83.8 4.0 %collective-permute-done.22.refs_7_ = bf16[128,1024]{1,0:T(8,128)(2,1)S(1)} collective-permute-done((bf16[128,1024]{1,0:T(8,128)(2,1)S(1)}, bf16[128,1024]{1,0:T(8,128)(2,1)S(1)}, u32[]{:S(2)}, u32[]{:S(2)}) %collective-permute-start.22) | collective-permute-done | bytes 262176 | tf_op jit(solution)/shard_map/ppermute | solution.py:282
  88.6 25.0 %all_to_all.5.parts_ref = bf16[8,32,1024]{2,1,0:T(8,128)(2,1)S(1)} all-to-all(bf16[8,32,1024]{2,1,0:T(8,128)(2,1)S(1)} %halfway.1), channel_id=1, replica_groups=mesh['y'=4,'zh'=4,'x'=4,'c'=2,'zl'=2] {'zh','zl'}, dimensions={0} | all-to-all | bytes 1048576 | tf_op jit(solution)/shard_map/all_to_all | solution.py:322
  (48 shorter events, 18.1 us)
Async XLA Ops:
  0.0 10.5 %collective-permute-start.3 = (bf16[128,1024]{1,0:T(8,128)(2,1)}, bf16[128,1024]{1,0:T(8,128)(2,1)S(1)}, u32[]{:S(2)}, u32[]{:S(2)}) collective-permute-start(bf16[128,1024]{1,0:T(8,128)(2,1)} %keys_ref.3), channel_id=1, source_target_pairs={{0,1},{2,3},{4,5},{6,7},{8,9},{10,11},{12,13},{14,15},{16,17},{18,... | collective-permute-start | bytes 786440 | tf_op jit(solution)/shard_map/ppermute | solution.py:293
  6.3 4.2 %copy-start.2 = (bf16[128,1024]{1,0:T(8,128)(2,1)S(1)}, bf16[128,1024]{1,0:T(8,128)(2,1)}, u32[]{:S(2)}) copy-start(bf16[128,1024]{1,0:T(8,128)(2,1)} %keys_ref.3) | copy-start | bytes 786436
  13.8 16.6 %collective-permute-start.5 = (bf16[128,512]{1,0:T(8,128)(2,1)S(1)}, bf16[128,512]{1,0:T(8,128)(2,1)S(1)}, u32[]{:S(2)}, u32[]{:S(2)}) collective-permute-start(bf16[128,512]{1,0:T(8,128)(2,1)S(1)} %get-tuple-element.38), channel_id=1, source_target_pairs={{1,0},{3,2},{5,4},{7,6},{9,8},{11,10},{13,12},{15,14},{17,16},{19,... | collective-permute-start | bytes 393224 | tf_op jit(solution)/shard_map/ppermute | solution.py:302
  20.7 16.8 %collective-permute-start = (bf16[1024,128]{1,0:T(8,128)(2,1)S(1)}, bf16[1024,128]{1,0:T(8,128)(2,1)S(1)}, u32[]{:S(2)}, u32[]{:S(2)}) collective-permute-start(bf16[1024,128]{1,0:T(8,128)(2,1)S(1)} %get-tuple-element.32), channel_id=1, source_target_pairs={{0,4},{4,8},{8,12},{12,0},{1,5},{5,9},{9,13},{13,1},{2,6},{6,10},{... | collective-permute-start | bytes 786440 | tf_op jit(solution)/shard_map/ppermute | solution.py:282
  22.2 18.7 %collective-permute-start.1 = (bf16[1024,128]{1,0:T(8,128)(2,1)S(1)}, bf16[1024,128]{1,0:T(8,128)(2,1)S(1)}, u32[]{:S(2)}, u32[]{:S(2)}) collective-permute-start(bf16[1024,128]{1,0:T(8,128)(2,1)S(1)} %get-tuple-element.33), channel_id=1, source_target_pairs={{0,8},{4,12},{8,0},{12,4},{1,9},{5,13},{9,1},{13,5},{2,10},{6,14},... | collective-permute-start | bytes 786440 | tf_op jit(solution)/shard_map/ppermute | solution.py:282
  23.4 17.6 %collective-permute-start.2 = (bf16[1024,128]{1,0:T(8,128)(2,1)S(1)}, bf16[1024,128]{1,0:T(8,128)(2,1)S(1)}, u32[]{:S(2)}, u32[]{:S(2)}) collective-permute-start(bf16[1024,128]{1,0:T(8,128)(2,1)S(1)} %get-tuple-element.34), channel_id=1, source_target_pairs={{0,12},{4,0},{8,4},{12,8},{1,13},{5,1},{9,5},{13,9},{2,14},{6,2},{... | collective-permute-start | bytes 786440 | tf_op jit(solution)/shard_map/ppermute | solution.py:282
  25.5 18.4 %collective-permute-start.13 = (bf16[1024,128]{1,0:T(8,128)(2,1)S(1)}, bf16[1024,128]{1,0:T(8,128)(2,1)S(1)}, u32[]{:S(2)}, u32[]{:S(2)}) collective-permute-start(bf16[1024,128]{1,0:T(8,128)(2,1)S(1)} %get-tuple-element.46), channel_id=1, source_target_pairs={{0,64},{64,128},{128,192},{192,0},{1,65},{65,129},{129,193},{193,1... | collective-permute-start | bytes 786440 | tf_op jit(solution)/shard_map/ppermute | solution.py:282
  30.4 6.9 %collective-permute-start.4 = (bf16[128,512]{1,0:T(8,128)(2,1)S(1)}, bf16[128,512]{1,0:T(8,128)(2,1)S(1)}, u32[]{:S(2)}, u32[]{:S(2)}) collective-permute-start(bf16[128,512]{1,0:T(8,128)(2,1)S(1)} %get-tuple-element.36), channel_id=1, source_target_pairs={{1,0},{3,2},{5,4},{7,6},{9,8},{11,10},{13,12},{15,14},{17,16},{19,... | collective-permute-start | bytes 393224 | tf_op jit(solution)/shard_map/ppermute | solution.py:302
  37.3 8.7 %collective-permute-start.6 = (bf16[128,1024]{1,0:T(8,128)(2,1)S(1)}, bf16[128,1024]{1,0:T(8,128)(2,1)S(1)}, u32[]{:S(2)}, u32[]{:S(2)}) collective-permute-start(bf16[128,1024]{1,0:T(8,128)(2,1)S(1)} %pad_maximum_fusion.refs_4_), channel_id=1, source_target_pairs={{0,4},{4,8},{8,12},{12,0},{1,5},{5,9},{9,13},{13,1},{2,6},{6,10},{... | collective-permute-start | bytes 786440 | tf_op jit(solution)/shard_map/ppermute | solution.py:282
  37.4 10.3 %collective-permute-start.7 = (bf16[128,1024]{1,0:T(8,128)(2,1)S(1)}, bf16[128,1024]{1,0:T(8,128)(2,1)S(1)}, u32[]{:S(2)}, u32[]{:S(2)}) collective-permute-start(bf16[128,1024]{1,0:T(8,128)(2,1)S(1)} %pad_maximum_fusion.refs_4_), channel_id=1, source_target_pairs={{0,8},{4,12},{8,0},{12,4},{1,9},{5,13},{9,1},{13,5},{2,10},{6,14},... | collective-permute-start | bytes 786440 | tf_op jit(solution)/shard_map/ppermute | solution.py:282
  40.9 9.7 %collective-permute-start.8 = (bf16[128,1024]{1,0:T(8,128)(2,1)S(1)}, bf16[128,1024]{1,0:T(8,128)(2,1)S(1)}, u32[]{:S(2)}, u32[]{:S(2)}) collective-permute-start(bf16[128,1024]{1,0:T(8,128)(2,1)S(1)} %pad_maximum_fusion.refs_4_), channel_id=1, source_target_pairs={{0,12},{4,0},{8,4},{12,8},{1,13},{5,1},{9,5},{13,9},{2,14},{6,2},{... | collective-permute-start | bytes 786440 | tf_op jit(solution)/shard_map/ppermute | solution.py:282
  40.9 15.8 %collective-permute-start.14 = (bf16[1024,128]{1,0:T(8,128)(2,1)S(1)}, bf16[1024,128]{1,0:T(8,128)(2,1)S(1)}, u32[]{:S(2)}, u32[]{:S(2)}) collective-permute-start(bf16[1024,128]{1,0:T(8,128)(2,1)S(1)} %get-tuple-element.47), channel_id=1, source_target_pairs={{0,128},{64,192},{128,0},{192,64},{1,129},{65,193},{129,1},{193,65... | collective-permute-start | bytes 786440 | tf_op jit(solution)/shard_map/ppermute | solution.py:282
  43.9 13.1 %collective-permute-start.15 = (bf16[1024,128]{1,0:T(8,128)(2,1)S(1)}, bf16[1024,128]{1,0:T(8,128)(2,1)S(1)}, u32[]{:S(2)}, u32[]{:S(2)}) collective-permute-start(bf16[1024,128]{1,0:T(8,128)(2,1)S(1)} %get-tuple-element.48), channel_id=1, source_target_pairs={{0,192},{64,0},{128,64},{192,128},{1,193},{65,1},{129,65},{193,129... | collective-permute-start | bytes 786440 | tf_op jit(solution)/shard_map/ppermute | solution.py:282
  46.0 13.6 %collective-permute-start.16 = (bf16[128,1024]{1,0:T(8,128)(2,1)S(1)}, bf16[128,1024]{1,0:T(8,128)(2,1)S(1)}, u32[]{:S(2)}, u32[]{:S(2)}) collective-permute-start(bf16[128,1024]{1,0:T(8,128)(2,1)S(1)} %pad_maximum_fusion.refs_4_), channel_id=1, source_target_pairs={{0,64},{64,128},{128,192},{192,0},{1,65},{65,129},{129,193},{193,1... | collective-permute-start | bytes 786440 | tf_op jit(solution)/shard_map/ppermute | solution.py:282
  47.7 11.9 %collective-permute-start.17 = (bf16[128,1024]{1,0:T(8,128)(2,1)S(1)}, bf16[128,1024]{1,0:T(8,128)(2,1)S(1)}, u32[]{:S(2)}, u32[]{:S(2)}) collective-permute-start(bf16[128,1024]{1,0:T(8,128)(2,1)S(1)} %pad_maximum_fusion.refs_4_), channel_id=1, source_target_pairs={{0,128},{64,192},{128,0},{192,64},{1,129},{65,193},{129,1},{193,65... | collective-permute-start | bytes 786440 | tf_op jit(solution)/shard_map/ppermute | solution.py:282
  50.6 13.1 %collective-permute-start.18 = (bf16[128,1024]{1,0:T(8,128)(2,1)S(1)}, bf16[128,1024]{1,0:T(8,128)(2,1)S(1)}, u32[]{:S(2)}, u32[]{:S(2)}) collective-permute-start(bf16[128,1024]{1,0:T(8,128)(2,1)S(1)} %pad_maximum_fusion.refs_4_), channel_id=1, source_target_pairs={{0,192},{64,0},{128,64},{192,128},{1,193},{65,1},{129,65},{193,129... | collective-permute-start | bytes 786440 | tf_op jit(solution)/shard_map/ppermute | solution.py:282
  56.7 8.3 %collective-permute-start.9 = (bf16[512,1024]{1,0:T(8,128)(2,1)S(1)}, bf16[512,1024]{1,0:T(8,128)(2,1)S(1)}, u32[]{:S(2)}, u32[]{:S(2)}) collective-permute-start(bf16[512,1024]{1,0:T(8,128)(2,1)S(1)} %get-tuple-element.40), channel_id=1, source_target_pairs={{0,2},{2,0},{1,3},{3,1},{4,6},{6,4},{5,7},{7,5},{8,10},{10,8},{9,1... | collective-permute-start | bytes 3145736 | tf_op jit(solution)/shard_map/ppermute | solution.py:282
  65.0 6.2 %collective-permute-start.19 = (bf16[512,1024]{1,0:T(8,128)(2,1)S(1)}, bf16[512,1024]{1,0:T(8,128)(2,1)S(1)}, u32[]{:S(2)}, u32[]{:S(2)}) collective-permute-start(bf16[512,1024]{1,0:T(8,128)(2,1)S(1)} %get-tuple-element.50), channel_id=1, source_target_pairs={{0,2},{2,0},{1,3},{3,1},{4,6},{6,4},{5,7},{7,5},{8,10},{10,8},{9,1... | collective-permute-start | bytes 3145736 | tf_op jit(solution)/shard_map/ppermute | solution.py:282
  65.3 10.0 %collective-permute-start.10 = (bf16[128,1024]{1,0:T(8,128)(2,1)S(1)}, bf16[128,1024]{1,0:T(8,128)(2,1)S(1)}, u32[]{:S(2)}, u32[]{:S(2)}) collective-permute-start(bf16[128,1024]{1,0:T(8,128)(2,1)S(1)} %get-tuple-element.42), channel_id=1, source_target_pairs={{0,64},{64,128},{128,192},{192,0},{1,65},{65,129},{129,193},{193,1... | collective-permute-start | bytes 786440 | tf_op jit(solution)/shard_map/ppermute | solution.py:282
  67.0 14.7 %collective-permute-start.11 = (bf16[128,1024]{1,0:T(8,128)(2,1)S(1)}, bf16[128,1024]{1,0:T(8,128)(2,1)S(1)}, u32[]{:S(2)}, u32[]{:S(2)}) collective-permute-start(bf16[128,1024]{1,0:T(8,128)(2,1)S(1)} %get-tuple-element.43), channel_id=1, source_target_pairs={{0,128},{64,192},{128,0},{192,64},{1,129},{65,193},{129,1},{193,65... | collective-permute-start | bytes 786440 | tf_op jit(solution)/shard_map/ppermute | solution.py:282
  69.4 12.3 %collective-permute-start.12 = (bf16[128,1024]{1,0:T(8,128)(2,1)S(1)}, bf16[128,1024]{1,0:T(8,128)(2,1)S(1)}, u32[]{:S(2)}, u32[]{:S(2)}) collective-permute-start(bf16[128,1024]{1,0:T(8,128)(2,1)S(1)} %get-tuple-element.44), channel_id=1, source_target_pairs={{0,192},{64,0},{128,64},{192,128},{1,193},{65,1},{129,65},{193,129... | collective-permute-start | bytes 786440 | tf_op jit(solution)/shard_map/ppermute | solution.py:282
  71.4 10.3 %collective-permute-start.20 = (bf16[128,1024]{1,0:T(8,128)(2,1)S(1)}, bf16[128,1024]{1,0:T(8,128)(2,1)S(1)}, u32[]{:S(2)}, u32[]{:S(2)}) collective-permute-start(bf16[128,1024]{1,0:T(8,128)(2,1)S(1)} %get-tuple-element.52), channel_id=1, source_target_pairs={{0,4},{4,8},{8,12},{12,0},{1,5},{5,9},{9,13},{13,1},{2,6},{6,10},{... | collective-permute-start | bytes 786440 | tf_op jit(solution)/shard_map/ppermute | solution.py:282
  73.1 10.7 %collective-permute-start.21 = (bf16[128,1024]{1,0:T(8,128)(2,1)S(1)}, bf16[128,1024]{1,0:T(8,128)(2,1)S(1)}, u32[]{:S(2)}, u32[]{:S(2)}) collective-permute-start(bf16[128,1024]{1,0:T(8,128)(2,1)S(1)} %get-tuple-element.53), channel_id=1, source_target_pairs={{0,8},{4,12},{8,0},{12,4},{1,9},{5,13},{9,1},{13,5},{2,10},{6,14},... | collective-permute-start | bytes 786440 | tf_op jit(solution)/shard_map/ppermute | solution.py:282
  75.2 12.6 %collective-permute-start.22 = (bf16[128,1024]{1,0:T(8,128)(2,1)S(1)}, bf16[128,1024]{1,0:T(8,128)(2,1)S(1)}, u32[]{:S(2)}, u32[]{:S(2)}) collective-permute-start(bf16[128,1024]{1,0:T(8,128)(2,1)S(1)} %get-tuple-element.54), channel_id=1, source_target_pairs={{0,12},{4,0},{8,4},{12,8},{1,13},{5,1},{9,5},{13,9},{2,14},{6,2},{... | collective-permute-start | bytes 786440 | tf_op jit(solution)/shard_map/ppermute | solution.py:282
  (4 other events, 10.7 us)

commit v3 on v2

--- a/solution.py
+++ b/solution.py
@@ -19,6 +19,7 @@
 SIDE, Z_SIZE = 4, 8
 OWNED = 32
 PART = OWNED // 2
+COLUMNS = 2 * SIDE * Z_SIZE * PART
 SCALE = 1.4426950408889634 / float(HD) ** 0.5
 SMEM = pl.BlockSpec(memory_space=pltpu.SMEM)
 VMEM = pl.BlockSpec(memory_space=pltpu.VMEM)
@@ -85,10 +86,10 @@
     pick(routes, place_ref, layout_ref, flipped, refs[-1], refs[:-1])
 
 
-def picked_rows(routes, where, layout, source, first):
+def picked_rows(routes, where, layout, source, first, spare=0):
     tokens = 128
     width = layout.shape[0]
-    piece = jax.ShapeDtypeStruct((2 * SIDE * Z_SIZE * PART, tokens), jnp.bfloat16)
+    piece = jax.ShapeDtypeStruct((COLUMNS + spare, tokens), jnp.bfloat16)
     shapes = [piece] * len(routes)
     scratch = [pltpu.VMEM((Z_SIZE * PART, tokens), jnp.float32)]
     if first:
@@ -99,7 +100,7 @@
             pltpu.SMEM((width,), jnp.int32),
             pltpu.SemaphoreType.DMA,
         ]
-    far = pl.BlockSpec(memory_space=pl.ANY)
+    far = pl.BlockSpec(memory_space=pltpu.HBM)
     return pl.pallas_call(
         functools.partial(first_pick_kernel if first else later_pick_kernel, routes),
         name="pick",
@@ -173,62 +174,102 @@
     )(where, queries, earlier, keys, out_grad)
 
 
-def multiply_kernel(*refs):
-    columns, grads, (own_ref, away_ref) = refs[:SIDE], refs[SIDE : 2 * SIDE], refs[2 * SIDE :]
+def completed_kernel(count, *refs):
+    own, returned = refs[:2], refs[2:4]
+    grads_ref, *sent = refs[4 + count : 5 + 2 * count]
+    tokens = own[0].shape[0]
+    for half in range(2):
+        for block in range(KVH // 2):
+            at = slice(block * HD, (block + 1) * HD)
+            row = (half * KVH // 2 + block) * tokens
+            grads_ref[row : row + tokens, :] = (
+                own[half][:, at] + returned[half][:, at].astype(jnp.float32)
+            ).astype(jnp.bfloat16)
+    for out_ref in sent:
+        out_ref[COLUMNS:, :] = grads_ref[...]
+
+
+def completed(own, returned, pieces):
+    count = len(pieces)
+    shape = jax.ShapeDtypeStruct((KVH * own[0].shape[0], HD), jnp.bfloat16)
+    return pl.pallas_call(
+        functools.partial(completed_kernel, count),
+        name="complete",
+        out_shape=(shape, *(jax.ShapeDtypeStruct(p.shape, p.dtype) for p in pieces)),
+        in_specs=[VMEM] * (4 + count),
+        out_specs=tuple([VMEM] * (1 + count)),
+        input_output_aliases={4 + i: 1 + i for i in range(count)},
+        cost_estimate=pl.CostEstimate(flops=5 * 10**8, bytes_accessed=2**20, transcendentals=0),
+        compiler_params=pltpu.CompilerParams(vmem_limit_bytes=4 * 2**20),
+    )(*own, *returned, *pieces)
+
+
+def multiply_kernel(places, away, *refs):
     tile = 256
-    half = own_ref.shape[0]
-    for number in range(2 * half // tile):
-        at = slice(number * tile, (number + 1) * tile)
+    first = COLUMNS // 2 if away else 0
+    if away:
+        arrays, outs = refs[:-1], refs[-1:]
+    else:
+        arrays, got_ref, outs = refs[: -1 - SIDE], refs[-1 - SIDE], refs[-SIDE:]
+    tokens = arrays[0].shape[1]
+    rows = outs[0].shape[0]
+
+    def right(place):
+        which, base = place
+        return jnp.concatenate(
+            [
+                arrays[which][base + block * tokens : base + (block + 1) * tokens, :]
+                for block in range(KVH)
+            ],
+            axis=1,
+        )
+
+    for number in range(COLUMNS // 2 // tile):
+        at = slice(first + number * tile, first + (number + 1) * tile)
         total = None
         for i in range(0, SIDE, 2):
-            left = jnp.concatenate([columns[i][at, :], columns[i + 1][at, :]], axis=1)
-            right = jnp.concatenate([grads[i][...], grads[i + 1][...]], axis=0)
-            term = jnp.dot(left, right, preferred_element_type=jnp.float32)
+            (left_a, grads_a), (left_b, grads_b) = places[i], places[i + 1]
+            left = jnp.concatenate([arrays[left_a][at, :], arrays[left_b][at, :]], axis=1)
+            both = jnp.concatenate([right(grads_a), right(grads_b)], axis=0)
+            term = jnp.dot(left, both, preferred_element_type=jnp.float32)
             total = term if total is None else total + term
-        if number * tile < half:
-            own_ref[at, :] = total
+        if not away:
+            total += got_ref[at, :].astype(jnp.float32)
+        total = total.astype(jnp.bfloat16)
+        for start in range(number * tile, (number + 1) * tile, min(rows, tile)):
+            count = min(rows, tile)
+            base = start % rows
+            outs[start // rows][base : base + count, :] = total[
+                start - number * tile : start - number * tile + count
+            ]
+
+
+def multiplied(pairs, got=None):
+    arrays, places = [], []
+    for columns, grads in pairs:
+        arrays.append(columns)
+        left = len(arrays) - 1
+        if grads is None:
+            places.append((left, (left, COLUMNS)))
         else:
-            away_ref[number * tile - half : (number + 1) * tile - half, :] = total.astype(
-                away_ref.dtype
-            )
-
-
-def multiplied(columns, grads):
-    half = columns[0].shape[0] // 2
-    return pl.pallas_call(
-        multiply_kernel,
+            arrays.append(grads)
+            places.append((left, (left + 1, 0)))
+    half = COLUMNS // 2
+    away = got is None
+    count, rows = (1, half) if away else (SIDE, half // SIDE)
+    if not away:
+        arrays.append(got)
+    return pl.pallas_call(
+        functools.partial(multiply_kernel, tuple(places), away),
         name="multiply",
-        out_shape=(
-            jax.ShapeDtypeStruct((half, WIDTH), jnp.float32),
-            jax.ShapeDtypeStruct((half, WIDTH), jnp.bfloat16),
-        ),
-        in_specs=[VMEM] * (2 * SIDE),
-        out_specs=(VMEM, VMEM),
+        out_shape=tuple([jax.ShapeDtypeStruct((rows, WIDTH), jnp.bfloat16)] * count),
+        in_specs=[VMEM] * len(arrays),
+        out_specs=tuple([VMEM] * count),
         cost_estimate=pl.CostEstimate(
-            flops=4 * half * SIDE * 128 * WIDTH, bytes_accessed=4 * 2**20, transcendentals=0
+            flops=2 * half * SIDE * 128 * WIDTH, bytes_accessed=4 * 2**20, transcendentals=0
         ),
         compiler_params=pltpu.CompilerParams(vmem_limit_bytes=16 * 2**20),
-    )(*columns, *grads)
-
-
-def merge_kernel(own_ref, got_ref, *outs):
-    rows = outs[0].shape[0]
-    for number, out_ref in enumerate(outs):
-        at = slice(number * rows, (number + 1) * rows)
-        out_ref[...] = (own_ref[at, :] + got_ref[at, :].astype(jnp.float32)).astype(out_ref.dtype)
-
-
-def merged(own, got):
-    shape = jax.ShapeDtypeStruct((own.shape[0] // SIDE, WIDTH), jnp.bfloat16)
-    return pl.pallas_call(
-        merge_kernel,
-        name="merge",
-        out_shape=tuple([shape] * SIDE),
-        in_specs=[VMEM, VMEM],
-        out_specs=tuple([VMEM] * SIDE),
-        cost_estimate=pl.CostEstimate(flops=5 * 10**8, bytes_accessed=2**20, transcendentals=0),
-        compiler_params=pltpu.CompilerParams(vmem_limit_bytes=4 * 2**20),
-    )(own, got)
+    )(*arrays)
 
 
 def halfway_kernel(place_ref, *refs):
@@ -291,7 +332,13 @@
     where = jnp.stack([lax.axis_index(axis).astype(jnp.int32) for axis in ("y", Z, "x", "c")])
     columns = {}
     earlier = lax.ppermute(keys, "zl", [(0, 1)])
-    flipped, *pieces = picked_rows(FAR, where, layout, activations, True)
+    flipped, *pieces = picked_rows(
+        FAR,
+        where,
+        pltpu.with_memory_space_constraint(layout, pltpu.HBM),
+        pltpu.with_memory_space_constraint(activations, pltpu.HBM),
+        True,
+    )
     for route, piece in zip(FAR, pieces):
         columns[route] = ahead(piece, *route)
     groups = KVH // 2
@@ -300,24 +347,28 @@
         early, mine = attended(half * groups, groups, where, queries, earlier, keys, out_grad)
         own.append(mine)
         returned.append(lax.ppermute(early, "zl", [(1, 0)]))
-    pieces = picked_rows(NEXT, where, layout, flipped, False)
+    pieces = picked_rows(NEXT, where, layout, flipped, False, WIDTH)
+    value_grad, *pieces = completed(own, returned, pieces)
+    pairs = {}
     for route, piece in zip(NEXT, pieces):
-        columns[route] = ahead(piece, *route)
+        pairs[route] = (ahead(piece, *route), None)
+    for route in FAR:
+        pairs[route] = (columns[route], ahead(value_grad, *route))
     pieces = picked_rows(HERE, where, layout, flipped, False)
-    columns.update(zip(HERE, pieces))
-    value_grad = jnp.concatenate(
-        [(a + b.astype(jnp.float32)).astype(jnp.bfloat16) for a, b in zip(own, returned)], axis=1
-    )
-    grads = {route: value_grad for route in HERE}
-    for route in FAR + NEXT:
-        grads[route] = ahead(value_grad, *route)
+    for route, piece in zip(HERE, pieces):
+        pairs[route] = (piece, value_grad)
+    ways = {way: [pairs[way, steps] for steps in range(SIDE)] for way in ("x", "y")}
+    got = {}
+    for way in ways:
+        (away,) = multiplied(ways[way])
+        got[way] = ahead(away, "c", 1)
     parts = []
     for way, across in (("x", "y"), ("y", "x")):
-        routes = [(way, steps) for steps in range(SIDE)]
-        kept, away = multiplied([columns[r] for r in routes], [grads[r] for r in routes])
-        got = ahead(away, "c", 1)
-        terms = merged(kept, got)
-        parts += [terms[0]] + [ahead(terms[i], across, i) for i in range(1, SIDE)]
+        terms = multiplied(ways[way], got[way])
+        moved = [terms[0]]
+        for steps in range(1, SIDE):
+            moved.append(ahead(terms[steps], across, steps))
+        parts += moved
     terms = halfway(where, parts)
     terms = lax.all_to_all(terms, Z, 0, 0, tiled=True)
     return finished(terms)

time: 115 us -> 120 us (1.043)
  the two profiles are of different devices: /device:TPU:2 before, /device:TPU:6 now
where the time goes in v3:
time: 120 us
  starting transfers between devices  34.8 us (29%)
  waiting for transfers between devices  33.5 us (28%)
  blocking collectives  25.7 us (21%)
  Pallas kernels  25.3 us (21%)
    ppermute x16, waiting for transfers between devices, ahead(): lax.ppermute(value, axis, [(i, (i + steps) % count) for i in range(count)])  33 us
    ppermute x16, starting transfers between devices, ahead(): lax.ppermute(value, axis, [(i, (i + steps) % count) for i in range(count)])  28.4 us
    all_to_all x1, blocking collectives, body(): terms = lax.all_to_all(terms, Z, 0, 0, tiled=True)  25.7 us
    pallas_call x3, Pallas kernels, picked_rows(): pl.pallas_call(functools.partial(first_pick_kernel if first else later_pi...  14.1 us
    pallas_call x2, Pallas kernels, attended(): pl.pallas_call(functools.partial(attend_kernel, first, groups), name='att...  6.62 us
    ppermute x1, starting transfers between devices, body(): earlier = lax.ppermute(keys, 'zl', [(0, 1)])  3.83 us
    pallas_call x4, Pallas kernels, multiplied(): pl.pallas_call(functools.partial(multiply_kernel, tuple(places), away), n...  2.85 us
    ppermute x2, starting transfers between devices, body(): returned.append(lax.ppermute(early, 'zl', [(1, 0)]))  2.58 us
  transfers between devices with their start and end apart: 19, of which 8 were waited for; matrix products, arithmetic and copies ran while one was open for 0% of the time, Pallas kernels for 17%

profile of v3, /device:TPU:6, one launch (start us, length us, event | category | flops | bytes accessed | tf_op | source)
XLA Modules:
  0.0 119.6 jit_solution(8887678793179022239)
XLA Ops:
  0.0 3.8 %collective-permute-start = (bf16[128,1024]{1,0:T(8,128)(2,1)}, bf16[128,1024]{1,0:T(8,128)(2,1)S(1)}, u32[]{:S(2)}, u32[]{:S(2)}) collective-permute-start(bf16[128,1024]{1,0:T(8,128)(2,1)} %keys_ref.3), channel_id=1, source_target_pairs={{0,1},{2,3},{4,5},{6,7},{8,9},{10,11},{12,13},{14,15},{16,17},{18,... | collective-permute-start | bytes 786440 | tf_op jit(solution)/shard_map/ppermute | solution.py:334
  3.9 5.2 %pick.3 = (f32[8192,128]{1,0:T(8,128)S(1)}, bf16[1024,128]{1,0:T(8,128)(2,1)S(1)}, bf16[1024,128]{1,0:T(8,128)(2,1)S(1)}) custom-call(s32[4]{0:T(128)S(1)} %pad_add_fusion.place_ref, s32[8192]{0:T(1024)} %layout_ref.5, bf16[128,8192]{1,0:T(8,128)(2,1)} %acts_ref.1), custom_call_target="tpu_custom_call" | custom-call | flops 2000000000 | bytes 4194304 | tf_op jit(solution)/shard_map/pick/pallas_call | solution.py:104
  9.7 3.3 %attend.2 = (bf16[128,512]{1,0:T(8,128)(2,1)S(1)}, f32[128,512]{1,0:T(8,128)S(1)}) custom-call(s32[4]{0:T(128)S(1)} %pad_add_fusion.place_ref, bf16[128,8192]{1,0:T(8,128)(2,1)S(1)} %copy-done, bf16[128,1024]{1,0:T(8,128)(2,1)S(1)} %collective-permute-done.earlier_ref, bf16[128,1024]{1,0:T(8,128)(2,1)S(1)} %copy-done.2, bf16[128,8192]{1,0:T(8,128)(2,1)S(1)} %copy-done.1), custom_call_target="tpu_custom_call" | custom-call | flops 536870912 | bytes 3145728 | tf_op jit(solution)/shard_map/attend/pallas_call | solution.py:159
  14.3 3.3 %attend.3 = (bf16[128,512]{1,0:T(8,128)(2,1)S(1)}, f32[128,512]{1,0:T(8,128)S(1)}) custom-call(s32[4]{0:T(128)S(1)} %pad_add_fusion.place_ref, bf16[128,8192]{1,0:T(8,128)(2,1)S(1)} %copy-done, bf16[128,1024]{1,0:T(8,128)(2,1)S(1)} %collective-permute-done.earlier_ref, bf16[128,1024]{1,0:T(8,128)(2,1)S(1)} %copy-done.2, bf16[128,8192]{1,0:T(8,128)(2,1)S(1)} %copy-done.1), custom_call_target="tpu_custom_call" | custom-call | flops 536870912 | bytes 3145728 | tf_op jit(solution)/shard_map/attend/pallas_call | solution.py:159
  18.9 5.6 %pick.5 = (bf16[2048,128]{1,0:T(8,128)(2,1)S(1)}, bf16[2048,128]{1,0:T(8,128)(2,1)S(1)}, bf16[2048,128]{1,0:T(8,128)(2,1)S(1)}, bf16[2048,128]{1,0:T(8,128)(2,1)S(1)}) custom-call(s32[4]{0:T(128)S(1)} %pad_add_fusion.place_ref, s32[8192]{0:T(1024)S(1)} %copy-done.3, f32[8192,128]{1,0:T(8,128)S(1)} %get-tuple-element.31.flipped), custom_call_target="tpu_custom_call" | custom-call | flops 4000000000 | bytes 4194304 | tf_op jit(solution)/shard_map/pick/pallas_call | solution.py:104
  25.3 2.4 %collective-permute-start.4 = (bf16[1024,128]{1,0:T(8,128)(2,1)S(1)}, bf16[1024,128]{1,0:T(8,128)(2,1)S(1)}, u32[]{:S(2)}, u32[]{:S(2)}) collective-permute-start(bf16[1024,128]{1,0:T(8,128)(2,1)S(1)} %get-tuple-element.43), channel_id=1, source_target_pairs={{0,8},{4,12},{8,0},{12,4},{1,9},{5,13},{9,1},{13,5},{2,10},{6,14},... | collective-permute-start | bytes 786440 | tf_op jit(solution)/shard_map/ppermute | solution.py:323
  27.7 3.3 %collective-permute-start.5 = (bf16[1024,128]{1,0:T(8,128)(2,1)S(1)}, bf16[1024,128]{1,0:T(8,128)(2,1)S(1)}, u32[]{:S(2)}, u32[]{:S(2)}) collective-permute-start(bf16[1024,128]{1,0:T(8,128)(2,1)S(1)} %get-tuple-element.41.refs_1_), channel_id=1, source_target_pairs={{0,8},{4,12},{8,0},{12,4},{1,9},{5,13},{9,1},{13,5},{2,10},{6,14},... | collective-permute-start | bytes 786440 | tf_op jit(solution)/shard_map/ppermute | solution.py:323
  30.9 1.6 %collective-permute-start.11 = (bf16[2048,128]{1,0:T(8,128)(2,1)S(1)}, bf16[2048,128]{1,0:T(8,128)(2,1)S(1)}, u32[]{:S(2)}, u32[]{:S(2)}) collective-permute-start(bf16[2048,128]{1,0:T(8,128)(2,1)S(1)} %get-tuple-element.50), channel_id=1, source_target_pairs={{0,64},{64,128},{128,192},{192,0},{1,65},{65,129},{129,193},{193,1... | collective-permute-start | bytes 1572872 | tf_op jit(solution)/shard_map/ppermute | solution.py:323
  32.5 3.4 %collective-permute-done.4.refs_3_ = bf16[1024,128]{1,0:T(8,128)(2,1)S(1)} collective-permute-done((bf16[1024,128]{1,0:T(8,128)(2,1)S(1)}, bf16[1024,128]{1,0:T(8,128)(2,1)S(1)}, u32[]{:S(2)}, u32[]{:S(2)}) %collective-permute-start.4) | collective-permute-done | bytes 262176 | tf_op jit(solution)/shard_map/ppermute | solution.py:323
  36.0 3.0 %collective-permute-start.14 = (bf16[2048,128]{1,0:T(8,128)(2,1)S(1)}, bf16[2048,128]{1,0:T(8,128)(2,1)S(1)}, u32[]{:S(2)}, u32[]{:S(2)}) collective-permute-start(bf16[2048,128]{1,0:T(8,128)(2,1)S(1)} %get-tuple-element.52), channel_id=1, source_target_pairs={{0,192},{64,0},{128,64},{192,128},{1,193},{65,1},{129,65},{193,129... | collective-permute-start | bytes 1572872 | tf_op jit(solution)/shard_map/ppermute | solution.py:323
  39.0 11.7 %collective-permute-done.5.refs_4_ = bf16[1024,128]{1,0:T(8,128)(2,1)S(1)} collective-permute-done((bf16[1024,128]{1,0:T(8,128)(2,1)S(1)}, bf16[1024,128]{1,0:T(8,128)(2,1)S(1)}, u32[]{:S(2)}, u32[]{:S(2)}) %collective-permute-start.5) | collective-permute-done | bytes 262176 | tf_op jit(solution)/shard_map/ppermute | solution.py:323
  50.6 3.2 %collective-permute-start.12 = (bf16[1024,128]{1,0:T(8,128)(2,1)S(1)}, bf16[1024,128]{1,0:T(8,128)(2,1)S(1)}, u32[]{:S(2)}, u32[]{:S(2)}) collective-permute-start(bf16[1024,128]{1,0:T(8,128)(2,1)S(1)} %get-tuple-element.51), channel_id=1, source_target_pairs={{0,128},{64,192},{128,0},{192,64},{1,129},{65,193},{129,1},{193,65... | collective-permute-start | bytes 786440 | tf_op jit(solution)/shard_map/ppermute | solution.py:323
  54.2 3.3 %pick.4 = (bf16[1024,128]{1,0:T(8,128)(2,1)S(1)}, bf16[1024,128]{1,0:T(8,128)(2,1)S(1)}) custom-call(s32[4]{0:T(128)S(1)} %pad_add_fusion.place_ref, s32[8192]{0:T(1024)S(1)} %copy-done.3, f32[8192,128]{1,0:T(8,128)S(1)} %get-tuple-element.31.flipped), custom_call_target="tpu_custom_call" | custom-call | flops 2000000000 | bytes 4194304 | tf_op jit(solution)/shard_map/pick/pallas_call | solution.py:104
  58.3 2.9 %collective-permute-done.12.refs_3_ = bf16[1024,128]{1,0:T(8,128)(2,1)S(1)} collective-permute-done((bf16[1024,128]{1,0:T(8,128)(2,1)S(1)}, bf16[1024,128]{1,0:T(8,128)(2,1)S(1)}, u32[]{:S(2)}, u32[]{:S(2)}) %collective-permute-start.12) | collective-permute-done | bytes 262176 | tf_op jit(solution)/shard_map/ppermute | solution.py:323
  61.2 2.8 %collective-permute-done.13.refs_4_ = bf16[1024,128]{1,0:T(8,128)(2,1)S(1)} collective-permute-done((bf16[1024,128]{1,0:T(8,128)(2,1)S(1)}, bf16[1024,128]{1,0:T(8,128)(2,1)S(1)}, u32[]{:S(2)}, u32[]{:S(2)}) %collective-permute-start.13) | collective-permute-done | bytes 262176 | tf_op jit(solution)/shard_map/ppermute | solution.py:323
  65.6 1.6 %collective-permute-start.8 = (bf16[128,1024]{1,0:T(8,128)(2,1)S(1)}, bf16[128,1024]{1,0:T(8,128)(2,1)S(1)}, u32[]{:S(2)}, u32[]{:S(2)}) collective-permute-start(bf16[128,1024]{1,0:T(8,128)(2,1)S(1)} %get-tuple-element.46), channel_id=1, source_target_pairs={{0,64},{64,128},{128,192},{192,0},{1,65},{65,129},{129,193},{193,1... | collective-permute-start | bytes 786440 | tf_op jit(solution)/shard_map/ppermute | solution.py:323
  67.1 2.9 %collective-permute-start.9 = (bf16[128,1024]{1,0:T(8,128)(2,1)S(1)}, bf16[128,1024]{1,0:T(8,128)(2,1)S(1)}, u32[]{:S(2)}, u32[]{:S(2)}) collective-permute-start(bf16[128,1024]{1,0:T(8,128)(2,1)S(1)} %get-tuple-element.47), channel_id=1, source_target_pairs={{0,128},{64,192},{128,0},{192,64},{1,129},{65,193},{129,1},{193,65... | collective-permute-start | bytes 786440 | tf_op jit(solution)/shard_map/ppermute | solution.py:323
  70.0 1.4 %collective-permute-start.10 = (bf16[128,1024]{1,0:T(8,128)(2,1)S(1)}, bf16[128,1024]{1,0:T(8,128)(2,1)S(1)}, u32[]{:S(2)}, u32[]{:S(2)}) collective-permute-start(bf16[128,1024]{1,0:T(8,128)(2,1)S(1)} %get-tuple-element.48), channel_id=1, source_target_pairs={{0,192},{64,0},{128,64},{192,128},{1,193},{65,1},{129,65},{193,129... | collective-permute-start | bytes 786440 | tf_op jit(solution)/shard_map/ppermute | solution.py:323
  72.1 5.3 %collective-permute-start.16 = (bf16[128,1024]{1,0:T(8,128)(2,1)S(1)}, bf16[128,1024]{1,0:T(8,128)(2,1)S(1)}, u32[]{:S(2)}, u32[]{:S(2)}) collective-permute-start(bf16[128,1024]{1,0:T(8,128)(2,1)S(1)} %get-tuple-element.54), channel_id=1, source_target_pairs={{0,4},{4,8},{8,12},{12,0},{1,5},{5,9},{9,13},{13,1},{2,6},{6,10},{... | collective-permute-start | bytes 786440 | tf_op jit(solution)/shard_map/ppermute | solution.py:323
  77.6 2.6 %collective-permute-start.18 = (bf16[128,1024]{1,0:T(8,128)(2,1)S(1)}, bf16[128,1024]{1,0:T(8,128)(2,1)S(1)}, u32[]{:S(2)}, u32[]{:S(2)}) collective-permute-start(bf16[128,1024]{1,0:T(8,128)(2,1)S(1)} %get-tuple-element.56), channel_id=1, source_target_pairs={{0,12},{4,0},{8,4},{12,8},{1,13},{5,1},{9,5},{13,9},{2,14},{6,2},{... | collective-permute-start | bytes 786440 | tf_op jit(solution)/shard_map/ppermute | solution.py:323
  80.2 2.1 %collective-permute-done.9.refs_2_ = bf16[128,1024]{1,0:T(8,128)(2,1)S(1)} collective-permute-done((bf16[128,1024]{1,0:T(8,128)(2,1)S(1)}, bf16[128,1024]{1,0:T(8,128)(2,1)S(1)}, u32[]{:S(2)}, u32[]{:S(2)}) %collective-permute-start.9) | collective-permute-done | bytes 262176 | tf_op jit(solution)/shard_map/ppermute | solution.py:323
  82.3 6.3 %collective-permute-done.16.refs_5_ = bf16[128,1024]{1,0:T(8,128)(2,1)S(1)} collective-permute-done((bf16[128,1024]{1,0:T(8,128)(2,1)S(1)}, bf16[128,1024]{1,0:T(8,128)(2,1)S(1)}, u32[]{:S(2)}, u32[]{:S(2)}) %collective-permute-start.16) | collective-permute-done | bytes 262176 | tf_op jit(solution)/shard_map/ppermute | solution.py:323
  88.6 3.7 %collective-permute-done.18.refs_7_ = bf16[128,1024]{1,0:T(8,128)(2,1)S(1)} collective-permute-done((bf16[128,1024]{1,0:T(8,128)(2,1)S(1)}, bf16[128,1024]{1,0:T(8,128)(2,1)S(1)}, u32[]{:S(2)}, u32[]{:S(2)}) %collective-permute-start.18) | collective-permute-done | bytes 262176 | tf_op jit(solution)/shard_map/ppermute | solution.py:323
  93.2 25.7 %all_to_all.5.parts_ref = bf16[8,32,1024]{2,1,0:T(8,128)(2,1)S(1)} all-to-all(bf16[8,32,1024]{2,1,0:T(8,128)(2,1)S(1)} %halfway.1), channel_id=1, replica_groups=mesh['y'=4,'zh'=4,'x'=4,'c'=2,'zl'=2] {'zh','zl'}, dimensions={0} | all-to-all | bytes 1048576 | tf_op jit(solution)/shard_map/all_to_all | solution.py:373
  (36 shorter events, 9.0 us)
Async XLA Ops:
  0.0 9.7 %collective-permute-start = (bf16[128,1024]{1,0:T(8,128)(2,1)}, bf16[128,1024]{1,0:T(8,128)(2,1)S(1)}, u32[]{:S(2)}, u32[]{:S(2)}) collective-permute-start(bf16[128,1024]{1,0:T(8,128)(2,1)} %keys_ref.3), channel_id=1, source_target_pairs={{0,1},{2,3},{4,5},{6,7},{8,9},{10,11},{12,13},{14,15},{16,17},{18,... | collective-permute-start | bytes 786440 | tf_op jit(solution)/shard_map/ppermute | solution.py:334
  3.9 5.8 %copy-start = (bf16[128,8192]{1,0:T(8,128)(2,1)S(1)}, bf16[128,8192]{1,0:T(8,128)(2,1)}, u32[]{:S(2)}) copy-start(bf16[128,8192]{1,0:T(8,128)(2,1)} %queries_ref.3) | copy-start | bytes 6291460
  3.9 5.8 %copy-start.1 = (bf16[128,8192]{1,0:T(8,128)(2,1)S(1)}, bf16[128,8192]{1,0:T(8,128)(2,1)}, u32[]{:S(2)}) copy-start(bf16[128,8192]{1,0:T(8,128)(2,1)} %grads_ref.3) | copy-start | bytes 6291460
  3.9 5.8 %copy-start.2 = (bf16[128,1024]{1,0:T(8,128)(2,1)S(1)}, bf16[128,1024]{1,0:T(8,128)(2,1)}, u32[]{:S(2)}) copy-start(bf16[128,1024]{1,0:T(8,128)(2,1)} %keys_ref.3) | copy-start | bytes 786436
  13.0 5.9 %copy-start.3 = (s32[8192]{0:T(1024)S(1)}, s32[8192]{0:T(1024)}, u32[]{:S(2)}) copy-start(s32[8192]{0:T(1024)} %layout_ref.5) | copy-start | bytes 98308
  13.0 11.5 %collective-permute-start.1 = (bf16[128,512]{1,0:T(8,128)(2,1)S(1)}, bf16[128,512]{1,0:T(8,128)(2,1)S(1)}, u32[]{:S(2)}, u32[]{:S(2)}) collective-permute-start(bf16[128,512]{1,0:T(8,128)(2,1)S(1)} %get-tuple-element.35), channel_id=1, source_target_pairs={{1,0},{3,2},{5,4},{7,6},{9,8},{11,10},{13,12},{15,14},{17,16},{19,... | collective-permute-start | bytes 393224 | tf_op jit(solution)/shard_map/ppermute | solution.py:349
  17.6 6.9 %collective-permute-start.2 = (bf16[128,512]{1,0:T(8,128)(2,1)S(1)}, bf16[128,512]{1,0:T(8,128)(2,1)S(1)}, u32[]{:S(2)}, u32[]{:S(2)}) collective-permute-start(bf16[128,512]{1,0:T(8,128)(2,1)S(1)} %get-tuple-element.36), channel_id=1, source_target_pairs={{1,0},{3,2},{5,4},{7,6},{9,8},{11,10},{13,12},{15,14},{17,16},{19,... | collective-permute-start | bytes 393224 | tf_op jit(solution)/shard_map/ppermute | solution.py:349
  24.7 29.1 %collective-permute-start.3 = (bf16[2048,128]{1,0:T(8,128)(2,1)S(1)}, bf16[2048,128]{1,0:T(8,128)(2,1)S(1)}, u32[]{:S(2)}, u32[]{:S(2)}) collective-permute-start(bf16[2048,128]{1,0:T(8,128)(2,1)S(1)} %get-tuple-element.42), channel_id=1, source_target_pairs={{0,4},{4,8},{8,12},{12,0},{1,5},{5,9},{9,13},{13,1},{2,6},{6,10},{... | collective-permute-start | bytes 1572872 | tf_op jit(solution)/shard_map/ppermute | solution.py:323
  25.3 10.7 %collective-permute-start.4 = (bf16[1024,128]{1,0:T(8,128)(2,1)S(1)}, bf16[1024,128]{1,0:T(8,128)(2,1)S(1)}, u32[]{:S(2)}, u32[]{:S(2)}) collective-permute-start(bf16[1024,128]{1,0:T(8,128)(2,1)S(1)} %get-tuple-element.43), channel_id=1, source_target_pairs={{0,8},{4,12},{8,0},{12,4},{1,9},{5,13},{9,1},{13,5},{2,10},{6,14},... | collective-permute-start | bytes 786440 | tf_op jit(solution)/shard_map/ppermute | solution.py:323
  27.7 29.8 %collective-permute-start.6 = (bf16[2048,128]{1,0:T(8,128)(2,1)S(1)}, bf16[2048,128]{1,0:T(8,128)(2,1)S(1)}, u32[]{:S(2)}, u32[]{:S(2)}) collective-permute-start(bf16[2048,128]{1,0:T(8,128)(2,1)S(1)} %get-tuple-element.44), channel_id=1, source_target_pairs={{0,12},{4,0},{8,4},{12,8},{1,13},{5,1},{9,5},{13,9},{2,14},{6,2},{... | collective-permute-start | bytes 1572872 | tf_op jit(solution)/shard_map/ppermute | solution.py:323
  27.7 22.9 %collective-permute-start.5 = (bf16[1024,128]{1,0:T(8,128)(2,1)S(1)}, bf16[1024,128]{1,0:T(8,128)(2,1)S(1)}, u32[]{:S(2)}, u32[]{:S(2)}) collective-permute-start(bf16[1024,128]{1,0:T(8,128)(2,1)S(1)} %get-tuple-element.41.refs_1_), channel_id=1, source_target_pairs={{0,8},{4,12},{8,0},{12,4},{1,9},{5,13},{9,1},{13,5},{2,10},{6,14},... | collective-permute-start | bytes 786440 | tf_op jit(solution)/shard_map/ppermute | solution.py:323
  30.9 33.1 %collective-permute-start.11 = (bf16[2048,128]{1,0:T(8,128)(2,1)S(1)}, bf16[2048,128]{1,0:T(8,128)(2,1)S(1)}, u32[]{:S(2)}, u32[]{:S(2)}) collective-permute-start(bf16[2048,128]{1,0:T(8,128)(2,1)S(1)} %get-tuple-element.50), channel_id=1, source_target_pairs={{0,64},{64,128},{128,192},{192,0},{1,65},{65,129},{129,193},{193,1... | collective-permute-start | bytes 1572872 | tf_op jit(solution)/shard_map/ppermute | solution.py:323
  36.0 28.1 %collective-permute-start.14 = (bf16[2048,128]{1,0:T(8,128)(2,1)S(1)}, bf16[2048,128]{1,0:T(8,128)(2,1)S(1)}, u32[]{:S(2)}, u32[]{:S(2)}) collective-permute-start(bf16[2048,128]{1,0:T(8,128)(2,1)S(1)} %get-tuple-element.52), channel_id=1, source_target_pairs={{0,192},{64,0},{128,64},{192,128},{1,193},{65,1},{129,65},{193,129... | collective-permute-start | bytes 1572872 | tf_op jit(solution)/shard_map/ppermute | solution.py:323
  50.6 10.6 %collective-permute-start.12 = (bf16[1024,128]{1,0:T(8,128)(2,1)S(1)}, bf16[1024,128]{1,0:T(8,128)(2,1)S(1)}, u32[]{:S(2)}, u32[]{:S(2)}) collective-permute-start(bf16[1024,128]{1,0:T(8,128)(2,1)S(1)} %get-tuple-element.51), channel_id=1, source_target_pairs={{0,128},{64,192},{128,0},{192,64},{1,129},{65,193},{129,1},{193,65... | collective-permute-start | bytes 786440 | tf_op jit(solution)/shard_map/ppermute | solution.py:323
  53.8 10.2 %collective-permute-start.13 = (bf16[1024,128]{1,0:T(8,128)(2,1)S(1)}, bf16[1024,128]{1,0:T(8,128)(2,1)S(1)}, u32[]{:S(2)}, u32[]{:S(2)}) collective-permute-start(bf16[1024,128]{1,0:T(8,128)(2,1)S(1)} %get-tuple-element.41.refs_1_), channel_id=1, source_target_pairs={{0,128},{64,192},{128,0},{192,64},{1,129},{65,193},{129,1},{193,65... | collective-permute-start | bytes 786440 | tf_op jit(solution)/shard_map/ppermute | solution.py:323
  58.2 6.6 %collective-permute-start.7 = (bf16[512,1024]{1,0:T(8,128)(2,1)S(1)}, bf16[512,1024]{1,0:T(8,128)(2,1)S(1)}, u32[]{:S(2)}, u32[]{:S(2)}) collective-permute-start(bf16[512,1024]{1,0:T(8,128)(2,1)S(1)} %multiply.4), channel_id=1, source_target_pairs={{0,2},{2,0},{1,3},{3,1},{4,6},{6,4},{5,7},{7,5},{8,10},{10,8},{9,1... | collective-permute-start | bytes 3145736 | tf_op jit(solution)/shard_map/ppermute | solution.py:323
  64.7 6.6 %collective-permute-start.15 = (bf16[512,1024]{1,0:T(8,128)(2,1)S(1)}, bf16[512,1024]{1,0:T(8,128)(2,1)S(1)}, u32[]{:S(2)}, u32[]{:S(2)}) collective-permute-start(bf16[512,1024]{1,0:T(8,128)(2,1)S(1)} %multiply.6), channel_id=1, source_target_pairs={{0,2},{2,0},{1,3},{3,1},{4,6},{6,4},{5,7},{7,5},{8,10},{10,8},{9,1... | collective-permute-start | bytes 3145736 | tf_op jit(solution)/shard_map/ppermute | solution.py:323
  65.6 12.0 %collective-permute-start.8 = (bf16[128,1024]{1,0:T(8,128)(2,1)S(1)}, bf16[128,1024]{1,0:T(8,128)(2,1)S(1)}, u32[]{:S(2)}, u32[]{:S(2)}) collective-permute-start(bf16[128,1024]{1,0:T(8,128)(2,1)S(1)} %get-tuple-element.46), channel_id=1, source_target_pairs={{0,64},{64,128},{128,192},{192,0},{1,65},{65,129},{129,193},{193,1... | collective-permute-start | bytes 786440 | tf_op jit(solution)/shard_map/ppermute | solution.py:323
  67.1 15.2 %collective-permute-start.9 = (bf16[128,1024]{1,0:T(8,128)(2,1)S(1)}, bf16[128,1024]{1,0:T(8,128)(2,1)S(1)}, u32[]{:S(2)}, u32[]{:S(2)}) collective-permute-start(bf16[128,1024]{1,0:T(8,128)(2,1)S(1)} %get-tuple-element.47), channel_id=1, source_target_pairs={{0,128},{64,192},{128,0},{192,64},{1,129},{65,193},{129,1},{193,65... | collective-permute-start | bytes 786440 | tf_op jit(solution)/shard_map/ppermute | solution.py:323
  70.0 12.3 %collective-permute-start.10 = (bf16[128,1024]{1,0:T(8,128)(2,1)S(1)}, bf16[128,1024]{1,0:T(8,128)(2,1)S(1)}, u32[]{:S(2)}, u32[]{:S(2)}) collective-permute-start(bf16[128,1024]{1,0:T(8,128)(2,1)S(1)} %get-tuple-element.48), channel_id=1, source_target_pairs={{0,192},{64,0},{128,64},{192,128},{1,193},{65,1},{129,65},{193,129... | collective-permute-start | bytes 786440 | tf_op jit(solution)/shard_map/ppermute | solution.py:323
  72.1 16.6 %collective-permute-start.16 = (bf16[128,1024]{1,0:T(8,128)(2,1)S(1)}, bf16[128,1024]{1,0:T(8,128)(2,1)S(1)}, u32[]{:S(2)}, u32[]{:S(2)}) collective-permute-start(bf16[128,1024]{1,0:T(8,128)(2,1)S(1)} %get-tuple-element.54), channel_id=1, source_target_pairs={{0,4},{4,8},{8,12},{12,0},{1,5},{5,9},{9,13},{13,1},{2,6},{6,10},{... | collective-permute-start | bytes 786440 | tf_op jit(solution)/shard_map/ppermute | solution.py:323
  77.4 11.3 %collective-permute-start.17 = (bf16[128,1024]{1,0:T(8,128)(2,1)S(1)}, bf16[128,1024]{1,0:T(8,128)(2,1)S(1)}, u32[]{:S(2)}, u32[]{:S(2)}) collective-permute-start(bf16[128,1024]{1,0:T(8,128)(2,1)S(1)} %get-tuple-element.55), channel_id=1, source_target_pairs={{0,8},{4,12},{8,0},{12,4},{1,9},{5,13},{9,1},{13,5},{2,10},{6,14},... | collective-permute-start | bytes 786440 | tf_op jit(solution)/shard_map/ppermute | solution.py:323
  77.6 14.8 %collective-permute-start.18 = (bf16[128,1024]{1,0:T(8,128)(2,1)S(1)}, bf16[128,1024]{1,0:T(8,128)(2,1)S(1)}, u32[]{:S(2)}, u32[]{:S(2)}) collective-permute-start(bf16[128,1024]{1,0:T(8,128)(2,1)S(1)} %get-tuple-element.56), channel_id=1, source_target_pairs={{0,12},{4,0},{8,4},{12,8},{1,13},{5,1},{9,5},{13,9},{2,14},{6,2},{... | collective-permute-start | bytes 786440 | tf_op jit(solution)/shard_map/ppermute | solution.py:323

commit v4 on v3

v4 whole, which is shorter than its diff:
```python
import functools

import jax
import jax.numpy as jnp
from jax import lax
from jax.experimental import pallas as pl
from jax.experimental.pallas import tpu as pltpu
from jax.sharding import Mesh
from jax.sharding import PartitionSpec as P


H = 64
KVH = 8
HD = 128
WIDTH = KVH * HD
PER = H // KVH
AXES = ("y", "zh", "x", "c", "zl")
Z = ("zh", "zl")
SIDE, Z_SIZE = 4, 8
OWNED = 32
COLUMNS = SIDE * Z_SIZE * OWNED
WAYS = ("x", "y")
SCALE = 1.4426950408889634 / float(HD) ** 0.5
SMEM = pl.BlockSpec(memory_space=pltpu.SMEM)
VMEM = pl.BlockSpec(memory_space=pltpu.VMEM)


def flip(acts_ref, flipped, landed, arrivals):
    width = acts_ref.shape[1]
    count = arrivals.shape[0]
    share = width // count

    def arriving(part):
        at = pl.ds(pl.multiple_of(part * share, share), share)
        return pltpu.make_async_copy(acts_ref.at[:, at], landed.at[:, at], arrivals.at[part])

    for part in range(count):
        arriving(part).start()

    def step(part, carry):
        arriving(part).wait()
        for tile in range(share // 128):
            at = pl.ds(pl.multiple_of(part * share + tile * 128, 128), 128)
            flipped[at, :] = landed[:, at].astype(jnp.float32).T
        return carry

    lax.fori_loop(0, count, step, 0)


def pick(routes, layout_ref, flipped, picked, outs):
    y, z, x = (lax.axis_index(axis) for axis in ("y", Z, "x"))
    for (axis, steps), out_ref in zip(routes, outs):

        def step(tile, carry):
            off = tile >> 1
            x_steps, y_steps = (steps, off) if axis == "x" else (off, steps)
            to_x, to_y = (x + x_steps) & (SIDE - 1), (y + y_steps) & (SIDE - 1)
            for block in range(Z_SIZE // 2):
                to_z = (z + (tile & 1) * (Z_SIZE // 2) + block) & (Z_SIZE - 1)
                owner = (((to_y * 4 + (to_z >> 1)) * 4 + to_x) * 2 + WAYS.index(axis)) * 2 + (to_z & 1)
                for row in range(OWNED):
                    source = layout_ref[owner * OWNED + row]
                    at = block * OWNED + row
                    picked[at : at + 1, :] = flipped[pl.ds(source, 1), :]
            rows = Z_SIZE // 2 * OWNED
            out_ref[pl.ds(pl.multiple_of(tile * rows, rows), rows), :] = picked[...].astype(
                jnp.bfloat16
            )
            return carry

        lax.fori_loop(0, 2 * SIDE, step, 0)


def first_pick_kernel(routes, layout_ref, acts_ref, flipped, *refs):
    outs = refs[: len(routes)]
    picked, landed, arrivals, rows_ref, rows_arrival = refs[len(routes) :]
    rows_copy = pltpu.make_async_copy(layout_ref, rows_ref, rows_arrival)
    rows_copy.start()
    flip(acts_ref, flipped, landed, arrivals)
    rows_copy.wait()
    pick(routes, rows_ref, flipped, picked, outs)


def later_pick_kernel(routes, layout_ref, flipped, *refs):
    pick(routes, layout_ref, flipped, refs[-1], refs[:-1])


def picked_rows(routes, layout, source, first, spare=0):
    tokens = 128
    width = layout.shape[0]
    piece = jax.ShapeDtypeStruct((COLUMNS + spare, tokens), jnp.bfloat16)
    shapes = [piece] * len(routes)
    scratch = [pltpu.VMEM((Z_SIZE // 2 * OWNED, tokens), jnp.float32)]
    if first:
        shapes = [jax.ShapeDtypeStruct((width, tokens), jnp.float32)] + shapes
        scratch += [
            pltpu.VMEM((tokens, width), jnp.bfloat16),
            pltpu.SemaphoreType.DMA((8,)),
            pltpu.SMEM((width,), jnp.int32),
            pltpu.SemaphoreType.DMA,
        ]
    far = pl.BlockSpec(memory_space=pltpu.HBM)
    return pl.pallas_call(
        functools.partial(first_pick_kernel if first else later_pick_kernel, routes),
        name="pick",
        out_shape=tuple(shapes),
        in_specs=[far, far] if first else [SMEM, VMEM],
        out_specs=tuple([VMEM] * len(shapes)),
        scratch_shapes=scratch,
        cost_estimate=pl.CostEstimate(
            flops=10**9 * len(routes), bytes_accessed=4 * 2**20, transcendentals=0
        ),
        compiler_params=pltpu.CompilerParams(vmem_limit_bytes=16 * 2**20),
    )(layout, source)


def attend_kernel(
    first, groups, queries_ref, earlier_ref, keys_ref, grads_ref, early_ref, own_ref
):
    rows = queries_ref.shape[0]
    second = lax.axis_index("zl") > 0
    shape = (rows, rows)
    causal = lax.broadcasted_iota(jnp.int32, shape, 0) <= lax.broadcasted_iota(jnp.int32, shape, 1)

    def group(number, carry):
        head = pl.ds(pl.multiple_of((number + first) * HD, HD), HD)
        both = jnp.concatenate([earlier_ref[:, head], keys_ref[:, head]], axis=0)
        total = jnp.zeros((2 * rows, HD), jnp.float32)
        for query_head in range(PER):
            at = pl.ds(pl.multiple_of(((number + first) * PER + query_head) * HD, HD), HD)
            scores = lax.dot_general(
                both, queries_ref[:, at], (((1,), (1,)), ((), ())), preferred_element_type=jnp.float32
            )
            before = jnp.where(second, scores[:rows], -1e30)
            last = jnp.where(causal, scores[rows:], -1e30)
            top = jnp.maximum(
                jnp.max(before, axis=0, keepdims=True), jnp.max(last, axis=0, keepdims=True)
            )
            before = jnp.exp2((before - top) * SCALE)
            last = jnp.exp2((last - top) * SCALE)
            share = 1.0 / (
                jnp.sum(before, axis=0, keepdims=True) + jnp.sum(last, axis=0, keepdims=True)
            )
            weights = jnp.concatenate(
                [(before * share).astype(jnp.bfloat16), (last * share).astype(jnp.bfloat16)], axis=0
            )
            total += jnp.dot(weights, grads_ref[:, at], preferred_element_type=jnp.float32)
        out = pl.ds(pl.multiple_of(number * HD, HD), HD)
        early_ref[:, out] = total[:rows].astype(early_ref.dtype)
        own_ref[:, out] = total[rows:]
        return carry

    lax.fori_loop(0, groups, group, 0)


def attended(first, groups, queries, earlier, keys, out_grad):
    rows = queries.shape[0]
    return pl.pallas_call(
        functools.partial(attend_kernel, first, groups),
        name="attend",
        out_shape=(
            jax.ShapeDtypeStruct((rows, groups * HD), jnp.bfloat16),
            jax.ShapeDtypeStruct((rows, groups * HD), jnp.float32),
        ),
        in_specs=[VMEM, VMEM, VMEM, VMEM],
        out_specs=(VMEM, VMEM),
        cost_estimate=pl.CostEstimate(
            flops=4 * groups * PER * rows * 2 * rows * HD,
            bytes_accessed=3 * 2**20,
            transcendentals=groups * PER * rows * 2 * rows,
        ),
        compiler_params=pltpu.CompilerParams(vmem_limit_bytes=16 * 2**20),
    )(queries, earlier, keys, out_grad)


def completed_kernel(count, *refs):
    own, returned = refs[:2], refs[2:4]
    grads_ref, *sent = refs[4 + count : 5 + 2 * count]
    tokens = own[0].shape[0]
    for half in range(2):
        for block in range(KVH // 2):
            at = slice(block * HD, (block + 1) * HD)
            row = (half * KVH // 2 + block) * tokens
            grads_ref[row : row + tokens, :] = (
                own[half][:, at] + returned[half][:, at].astype(jnp.float32)
            ).astype(jnp.bfloat16)
    for out_ref in sent:
        out_ref[COLUMNS:, :] = grads_ref[...]


def completed(own, returned, pieces):
    count = len(pieces)
    shape = jax.ShapeDtypeStruct((KVH * own[0].shape[0], HD), jnp.bfloat16)
    return pl.pallas_call(
        functools.partial(completed_kernel, count),
        name="complete",
        out_shape=(shape, *(jax.ShapeDtypeStruct(p.shape, p.dtype) for p in pieces)),
        in_specs=[VMEM] * (4 + count),
        out_specs=tuple([VMEM] * (1 + count)),
        input_output_aliases={4 + i: 1 + i for i in range(count)},
        cost_estimate=pl.CostEstimate(flops=5 * 10**8, bytes_accessed=2**20, transcendentals=0),
        compiler_params=pltpu.CompilerParams(vmem_limit_bytes=4 * 2**20),
    )(*own, *returned, *pieces)


def multiply_kernel(places, offs, away, *refs):
    count = 1 + max(max(left, grads) for way in places for left, (grads, _) in way)
    arrays, rest = refs[:count], refs[count:]
    tile = COLUMNS // SIDE
    core = lax.axis_index("c")

    def product(way, at):
        def right(place):
            which, base = place
            tokens = arrays[which].shape[1]
            return jnp.concatenate(
                [
                    arrays[which][base + block * tokens : base + (block + 1) * tokens, :]
                    for block in range(KVH)
                ],
                axis=1,
            )

        total = None
        for i in range(0, SIDE, 2):
            (left_a, grads_a), (left_b, grads_b) = places[way][i], places[way][i + 1]
            left = jnp.concatenate([arrays[left_a][at, :], arrays[left_b][at, :]], axis=1)
            both = jnp.concatenate([right(grads_a), right(grads_b)], axis=0)
            term = jnp.dot(left, both, preferred_element_type=jnp.float32)
            total = term if total is None else total + term
        return total

    def work(way):
        def step(number, carry):
            off = offs[0] + number * (offs[1] - offs[0])
            total = product(way, pl.ds(pl.multiple_of(off * tile, tile), tile))
            at = pl.ds(pl.multiple_of(number * tile, tile), tile)
            if away:
                rest[0][at, :] = total.astype(jnp.bfloat16)
                return carry
            total = (total + rest[0][at, :].astype(jnp.float32)).astype(jnp.bfloat16)
            for which in range(2):

                @pl.when(number == which)
                def _():
                    rest[1 + which][...] = total

            return carry

        lax.fori_loop(0, 2, step, 0)

    for way in range(2):

        @pl.when(core == (1 - way if away else way))
        def _():
            work(way)


def multiplied(offs, ways, got=None):
    arrays, places = [], []
    for pairs in ways:
        way = []
        for columns, grads in pairs:
            found = []
            for array in (columns, grads):
                if array is not None:
                    known = [i for i, other in enumerate(arrays) if other is array]
                    if not known:
                        arrays.append(array)
                    found.append(known[0] if known else len(arrays) - 1)
            way.append((found[0], (found[0], COLUMNS) if grads is None else (found[1], 0)))
        places.append(tuple(way))
    tile = COLUMNS // SIDE
    away = got is None
    shapes = [(len(offs) * tile, WIDTH)] if away else [(tile, WIDTH)] * len(offs)
    operands = arrays if away else arrays + [got]
    return pl.pallas_call(
        functools.partial(multiply_kernel, tuple(places), offs, away),
        name="multiply",
        out_shape=tuple(jax.ShapeDtypeStruct(shape, jnp.bfloat16) for shape in shapes),
        in_specs=[VMEM] * len(operands),
        out_specs=tuple([VMEM] * len(shapes)),
        cost_estimate=pl.CostEstimate(
            flops=2 * len(offs) * tile * SIDE * 128 * WIDTH,
            bytes_accessed=4 * 2**20,
            transcendentals=0,
        ),
        compiler_params=pltpu.CompilerParams(vmem_limit_bytes=16 * 2**20),
    )(*operands)


def halfway_kernel(*refs):
    parts, out_ref = refs[:-1], refs[-1]
    z = lax.axis_index(Z)
    for block in range(Z_SIZE):
        at = slice(block * OWNED, (block + 1) * OWNED)
        total = parts[0][at, :].astype(jnp.float32)
        for part in parts[1:]:
            total += part[at, :].astype(jnp.float32)
        out_ref[(z + block) & (Z_SIZE - 1)] = total.astype(out_ref.dtype)


def halfway(parts):
    return pl.pallas_call(
        halfway_kernel,
        name="halfway",
        out_shape=jax.ShapeDtypeStruct((Z_SIZE, OWNED, WIDTH), jnp.bfloat16),
        in_specs=[VMEM] * len(parts),
        out_specs=VMEM,
        cost_estimate=pl.CostEstimate(flops=5 * 10**8, bytes_accessed=2**20, transcendentals=0),
        compiler_params=pltpu.CompilerParams(vmem_limit_bytes=4 * 2**20),
    )(*parts)


def finish_kernel(parts_ref, out_ref):
    total = parts_ref[0].astype(jnp.float32)
    for part in range(1, Z_SIZE):
        total += parts_ref[part].astype(jnp.float32)
    out_ref[...] = total


def finished(parts):
    return pl.pallas_call(
        finish_kernel,
        name="finish",
        out_shape=jax.ShapeDtypeStruct((OWNED, WIDTH), jnp.float32),
        in_specs=[VMEM],
        out_specs=VMEM,
        cost_estimate=pl.CostEstimate(flops=5 * 10**8, bytes_accessed=2**20, transcendentals=0),
        compiler_params=pltpu.CompilerParams(vmem_limit_bytes=4 * 2**20),
    )(parts)


def ahead(value, axis, steps):
    count = lax.axis_size(axis)
    return lax.ppermute(value, axis, [(i, (i + steps) % count) for i in range(count)])


def crossed(value, steps):
    pairs = []
    for y in range(SIDE):
        for x in range(SIDE):
            pairs.append(((y * SIDE + x) * 2, ((y + steps) % SIDE * SIDE + x) * 2))
            pairs.append(((y * SIDE + x) * 2 + 1, (y * SIDE + (x + steps) % SIDE) * 2 + 1))
    return lax.ppermute(value, ("y", "x", "c"), pairs)


FAR = (("x", 2), ("y", 2))
NEXT = (("x", 1), ("x", 3), ("y", 1), ("y", 3))
HERE = (("x", 0), ("y", 0))


def body(activations, queries, keys, out_grad, layout):
    columns = {}
    earlier = lax.ppermute(keys, "zl", [(0, 1)])
    flipped, *pieces = picked_rows(
        FAR,
        pltpu.with_memory_space_constraint(layout, pltpu.HBM),
        pltpu.with_memory_space_constraint(activations, pltpu.HBM),
        True,
    )
    for route, piece in zip(FAR, pieces):
        columns[route] = ahead(piece, *route)
    groups = KVH // 2
    own, returned = [], []
    for half in range(2):
        early, mine = attended(half * groups, groups, queries, earlier, keys, out_grad)
        own.append(mine)
        returned.append(lax.ppermute(early, "zl", [(1, 0)]))
    pieces = picked_rows(NEXT, layout, flipped, False, WIDTH)
    value_grad, *pieces = completed(own, returned, pieces)
    pairs = {}
    for route, piece in zip(NEXT, pieces):
        pairs[route] = (ahead(piece, *route), None)
    for route in FAR:
        pairs[route] = (columns[route], ahead(value_grad, *route))
    pieces = picked_rows(HERE, layout, flipped, False)
    for route, piece in zip(HERE, pieces):
        pairs[route] = (piece, value_grad)
    ways = [[pairs[way, steps] for steps in range(SIDE)] for way in WAYS]
    halves = ((1, 3), (2, 0))
    got = []
    for offs in halves:
        (away,) = multiplied(offs, ways)
        got.append(ahead(away, "c", 1))
    parts = []
    for half, offs in enumerate(halves):
        terms = multiplied(offs, ways, got[half])
        for steps, term in zip(offs, terms):
            parts.append(crossed(term, steps) if steps else term)
    terms = halfway(parts)
    terms = lax.all_to_all(terms, Z, 0, 0, tiled=True)
    return finished(terms)


def solution(mesh):
    finer = Mesh(mesh.devices.reshape(4, 4, 4, 2, mesh.shape["seq"]), AXES)
    placed = (P(AXES, None), P(AXES, None), P(AXES, None), P(AXES, None), P())
    return jax.shard_map(
        body, mesh=finer, in_specs=placed, out_specs=P(AXES, None), check_vma=False
    )
```

time: 120 us -> 96.4 us (0.80)
  the two profiles are of different devices: /device:TPU:6 before, /device:TPU:0 now
where the time goes in v4:
time: 96.4 us; the launch traced here: 94.7 us
  blocking collectives  25.2 us (26%)
  starting transfers between devices  25.1 us (26%)
  Pallas kernels  23 us (24%)
  waiting for transfers between devices  21.2 us (22%)
    all_to_all x1, blocking collectives, body(): terms = lax.all_to_all(terms, Z, 0, 0, tiled=True)  25.2 us
    ppermute x10, starting transfers between devices, ahead(): lax.ppermute(value, axis, [(i, (i + steps) % count) for i in range(count)])  14.8 us
    pallas_call x3, Pallas kernels, picked_rows(): pl.pallas_call(functools.partial(first_pick_kernel if first else later_pi...  12.5 us
    ppermute x3, waiting for transfers between devices, crossed(): return lax.ppermute(value, ('y', 'x', 'c'), pairs)  10.9 us
    ppermute x10, waiting for transfers between devices, ahead(): lax.ppermute(value, axis, [(i, (i + steps) % count) for i in range(count)])  9.92 us
    pallas_call x2, Pallas kernels, attended(): pl.pallas_call(functools.partial(attend_kernel, first, groups), name='att...  5.58 us
    ppermute x3, starting transfers between devices, crossed(): return lax.ppermute(value, ('y', 'x', 'c'), pairs)  5.36 us
    pallas_call x4, Pallas kernels, multiplied(): pl.pallas_call(functools.partial(multiply_kernel, tuple(places), offs, aw...  3.74 us
  transfers between devices with their start and end apart: 16, of which 9 were waited for; matrix products, arithmetic and copies ran while one was open for 0% of the time, Pallas kernels for 22%

profile of v4, /device:TPU:0, one launch (start us, length us, event | category | flops | bytes accessed | tf_op | source)
XLA Modules:
  0.0 94.7 jit_solution(12785236849758145635)
XLA Ops:
  0.0 2.4 %collective-permute-start = (bf16[128,1024]{1,0:T(8,128)(2,1)}, bf16[128,1024]{1,0:T(8,128)(2,1)S(1)}, u32[]{:S(2)}, u32[]{:S(2)}) collective-permute-start(bf16[128,1024]{1,0:T(8,128)(2,1)} %keys_ref.3), channel_id=1, source_target_pairs={{0,1},{2,3},{4,5},{6,7},{8,9},{10,11},{12,13},{14,15},{16,17},{18,... | collective-permute-start | bytes 786440 | tf_op jit(solution)/shard_map/ppermute | solution.py:355
  2.4 4.2 %pick.3 = (f32[8192,128]{1,0:T(8,128)S(1)}, bf16[1024,128]{1,0:T(8,128)(2,1)S(1)}, bf16[1024,128]{1,0:T(8,128)(2,1)S(1)}) custom-call(s32[8192]{0:T(1024)} %layout_ref.5, bf16[128,8192]{1,0:T(8,128)(2,1)} %acts_ref.1), custom_call_target="tpu_custom_call" | custom-call | flops 2000000000 | bytes 4194304 | tf_op jit(solution)/shard_map/pick/pallas_call | solution.py:103
  6.6 3.1 %collective-permute-start.4 = (bf16[1024,128]{1,0:T(8,128)(2,1)S(1)}, bf16[1024,128]{1,0:T(8,128)(2,1)S(1)}, u32[]{:S(2)}, u32[]{:S(2)}) collective-permute-start(bf16[1024,128]{1,0:T(8,128)(2,1)S(1)} %get-tuple-element.39), channel_id=1, source_target_pairs={{0,8},{4,12},{8,0},{12,4},{1,9},{5,13},{9,1},{13,5},{2,10},{6,14},... | collective-permute-start | bytes 786440 | tf_op jit(solution)/shard_map/ppermute | solution.py:336
  9.8 3.2 %collective-permute-start.8 = (bf16[1024,128]{1,0:T(8,128)(2,1)S(1)}, bf16[1024,128]{1,0:T(8,128)(2,1)S(1)}, u32[]{:S(2)}, u32[]{:S(2)}) collective-permute-start(bf16[1024,128]{1,0:T(8,128)(2,1)S(1)} %get-tuple-element.43), channel_id=1, source_target_pairs={{0,128},{64,192},{128,0},{192,64},{1,129},{65,193},{129,1},{193,65... | collective-permute-start | bytes 786440 | tf_op jit(solution)/shard_map/ppermute | solution.py:336
  13.0 2.8 %attend.2 = (bf16[128,512]{1,0:T(8,128)(2,1)S(1)}, f32[128,512]{1,0:T(8,128)S(1)}) custom-call(bf16[128,8192]{1,0:T(8,128)(2,1)S(1)} %copy-done, bf16[128,1024]{1,0:T(8,128)(2,1)S(1)} %collective-permute-done.earlier_ref, bf16[128,1024]{1,0:T(8,128)(2,1)S(1)} %copy-done.2, bf16[128,8192]{1,0:T(8,128)(2,1)S(1)} %copy-done.1), custom_call_target="tpu_custom_call" | custom-call | flops 536870912 | bytes 3145728 | tf_op jit(solution)/shard_map/attend/pallas_call | solution.py:158
  15.8 1.3 %collective-permute-start.1 = (bf16[128,512]{1,0:T(8,128)(2,1)S(1)}, bf16[128,512]{1,0:T(8,128)(2,1)S(1)}, u32[]{:S(2)}, u32[]{:S(2)}) collective-permute-start(bf16[128,512]{1,0:T(8,128)(2,1)S(1)} %get-tuple-element.31), channel_id=1, source_target_pairs={{1,0},{3,2},{5,4},{7,6},{9,8},{11,10},{13,12},{15,14},{17,16},{19,... | collective-permute-start | bytes 393224 | tf_op jit(solution)/shard_map/ppermute | solution.py:369
  17.1 2.8 %attend.3 = (bf16[128,512]{1,0:T(8,128)(2,1)S(1)}, f32[128,512]{1,0:T(8,128)S(1)}) custom-call(bf16[128,8192]{1,0:T(8,128)(2,1)S(1)} %copy-done, bf16[128,1024]{1,0:T(8,128)(2,1)S(1)} %collective-permute-done.earlier_ref, bf16[128,1024]{1,0:T(8,128)(2,1)S(1)} %copy-done.2, bf16[128,8192]{1,0:T(8,128)(2,1)S(1)} %copy-done.1), custom_call_target="tpu_custom_call" | custom-call | flops 536870912 | bytes 3145728 | tf_op jit(solution)/shard_map/attend/pallas_call | solution.py:158
  19.9 1.3 %collective-permute-start.2 = (bf16[128,512]{1,0:T(8,128)(2,1)S(1)}, bf16[128,512]{1,0:T(8,128)(2,1)S(1)}, u32[]{:S(2)}, u32[]{:S(2)}) collective-permute-start(bf16[128,512]{1,0:T(8,128)(2,1)S(1)} %get-tuple-element.32), channel_id=1, source_target_pairs={{1,0},{3,2},{5,4},{7,6},{9,8},{11,10},{13,12},{15,14},{17,16},{19,... | collective-permute-start | bytes 393224 | tf_op jit(solution)/shard_map/ppermute | solution.py:369
  21.2 5.2 %pick.5 = (bf16[2048,128]{1,0:T(8,128)(2,1)S(1)}, bf16[2048,128]{1,0:T(8,128)(2,1)S(1)}, bf16[2048,128]{1,0:T(8,128)(2,1)S(1)}, bf16[2048,128]{1,0:T(8,128)(2,1)S(1)}) custom-call(s32[8192]{0:T(1024)S(1)} %copy-done.3, f32[8192,128]{1,0:T(8,128)S(1)} %get-tuple-element.27.flipped), custom_call_target="tpu_custom_call" | custom-call | flops 4000000000 | bytes 4194304 | tf_op jit(solution)/shard_map/pick/pallas_call | solution.py:103
  27.9 2.6 %collective-permute-start.6 = (bf16[2048,128]{1,0:T(8,128)(2,1)S(1)}, bf16[2048,128]{1,0:T(8,128)(2,1)S(1)}, u32[]{:S(2)}, u32[]{:S(2)}) collective-permute-start(bf16[2048,128]{1,0:T(8,128)(2,1)S(1)} %get-tuple-element.40), channel_id=1, source_target_pairs={{0,12},{4,0},{8,4},{12,8},{1,13},{5,1},{9,5},{13,9},{2,14},{6,2},{... | collective-permute-start | bytes 1572872 | tf_op jit(solution)/shard_map/ppermute | solution.py:336
  30.6 1.6 %collective-permute-start.7 = (bf16[2048,128]{1,0:T(8,128)(2,1)S(1)}, bf16[2048,128]{1,0:T(8,128)(2,1)S(1)}, u32[]{:S(2)}, u32[]{:S(2)}) collective-permute-start(bf16[2048,128]{1,0:T(8,128)(2,1)S(1)} %get-tuple-element.42), channel_id=1, source_target_pairs={{0,64},{64,128},{128,192},{192,0},{1,65},{65,129},{129,193},{193,1... | collective-permute-start | bytes 1572872 | tf_op jit(solution)/shard_map/ppermute | solution.py:336
  32.2 1.7 %collective-permute-start.10 = (bf16[2048,128]{1,0:T(8,128)(2,1)S(1)}, bf16[2048,128]{1,0:T(8,128)(2,1)S(1)}, u32[]{:S(2)}, u32[]{:S(2)}) collective-permute-start(bf16[2048,128]{1,0:T(8,128)(2,1)S(1)} %get-tuple-element.44), channel_id=1, source_target_pairs={{0,192},{64,0},{128,64},{192,128},{1,193},{65,1},{129,65},{193,129... | collective-permute-start | bytes 1572872 | tf_op jit(solution)/shard_map/ppermute | solution.py:336
  33.8 3.5 %collective-permute-done.9.refs_9_ = bf16[1024,128]{1,0:T(8,128)(2,1)S(1)} collective-permute-done((bf16[1024,128]{1,0:T(8,128)(2,1)S(1)}, bf16[1024,128]{1,0:T(8,128)(2,1)S(1)}, u32[]{:S(2)}, u32[]{:S(2)}) %collective-permute-start.9) | collective-permute-done | bytes 262176 | tf_op jit(solution)/shard_map/ppermute | solution.py:336
  38.2 3.1 %pick.4 = (bf16[1024,128]{1,0:T(8,128)(2,1)S(1)}, bf16[1024,128]{1,0:T(8,128)(2,1)S(1)}) custom-call(s32[8192]{0:T(1024)S(1)} %copy-done.3, f32[8192,128]{1,0:T(8,128)S(1)} %get-tuple-element.27.flipped), custom_call_target="tpu_custom_call" | custom-call | flops 2000000000 | bytes 4194304 | tf_op jit(solution)/shard_map/pick/pallas_call | solution.py:103
  41.3 4.5 %collective-permute-done.5.refs_4_ = bf16[1024,128]{1,0:T(8,128)(2,1)S(1)} collective-permute-done((bf16[1024,128]{1,0:T(8,128)(2,1)S(1)}, bf16[1024,128]{1,0:T(8,128)(2,1)S(1)}, u32[]{:S(2)}, u32[]{:S(2)}) %collective-permute-start.5) | collective-permute-done | bytes 262176 | tf_op jit(solution)/shard_map/ppermute | solution.py:336
  49.1 1.2 %collective-permute-done.11.refs_11_ = bf16[512,1024]{1,0:T(8,128)(2,1)S(1)} collective-permute-done((bf16[512,1024]{1,0:T(8,128)(2,1)S(1)}, bf16[512,1024]{1,0:T(8,128)(2,1)S(1)}, u32[]{:S(2)}, u32[]{:S(2)}) %collective-permute-start.11) | collective-permute-done | bytes 1048608 | tf_op jit(solution)/shard_map/ppermute | solution.py:336
  51.2 1.6 %collective-permute-start.12 = (bf16[256,1024]{1,0:T(8,128)(2,1)S(1)}, bf16[256,1024]{1,0:T(8,128)(2,1)S(1)}, u32[]{:S(2)}, u32[]{:S(2)}) collective-permute-start(bf16[256,1024]{1,0:T(8,128)(2,1)S(1)} %get-tuple-element.45), channel_id=1, source_target_pairs={{0,64},{2,6},{4,68},{6,10},{8,72},{10,14},{12,76},{14,2},{64,128},... | collective-permute-start | bytes 1572872 | tf_op jit(solution)/shard_map/ppermute | solution.py:345
  52.8 1.9 %collective-permute-start.13 = (bf16[256,1024]{1,0:T(8,128)(2,1)S(1)}, bf16[256,1024]{1,0:T(8,128)(2,1)S(1)}, u32[]{:S(2)}, u32[]{:S(2)}) collective-permute-start(bf16[256,1024]{1,0:T(8,128)(2,1)S(1)} %get-tuple-element.46), channel_id=1, source_target_pairs={{0,192},{2,14},{4,196},{6,2},{8,200},{10,6},{12,204},{14,10},{64,0... | collective-permute-start | bytes 1572872 | tf_op jit(solution)/shard_map/ppermute | solution.py:345
  54.7 1.0 %multiply.7 = (bf16[256,1024]{1,0:T(8,128)(2,1)S(1)}, bf16[256,1024]{1,0:T(8,128)(2,1)S(1)}) custom-call(bf16[1024,128]{1,0:T(8,128)(2,1)S(1)} %get-tuple-element.28.refs_0_, bf16[1024,128]{1,0:T(8,128)(2,1)S(1)} %get-tuple-element.37.refs_1_, bf16[2048,128]{1,0:T(8,128)(2,1)S(1)} %collective-permute-done.3.refs_2_, ...), custom_call_target="tpu_custom_call" | custom-call | flops 536870912 | bytes 4194304 | tf_op jit(solution)/shard_map/multiply/pallas_call | solution.py:277
  55.7 1.9 %collective-permute-start.15 = (bf16[256,1024]{1,0:T(8,128)(2,1)S(1)}, bf16[256,1024]{1,0:T(8,128)(2,1)S(1)}, u32[]{:S(2)}, u32[]{:S(2)}) collective-permute-start(bf16[256,1024]{1,0:T(8,128)(2,1)S(1)} %get-tuple-element.47), channel_id=1, source_target_pairs={{0,128},{2,10},{4,132},{6,14},{8,136},{10,2},{12,140},{14,6},{64,1... | collective-permute-start | bytes 1572872 | tf_op jit(solution)/shard_map/ppermute | solution.py:345
  57.6 4.3 %collective-permute-done.12.refs_0_ = bf16[256,1024]{1,0:T(8,128)(2,1)S(1)} collective-permute-done((bf16[256,1024]{1,0:T(8,128)(2,1)S(1)}, bf16[256,1024]{1,0:T(8,128)(2,1)S(1)}, u32[]{:S(2)}, u32[]{:S(2)}) %collective-permute-start.12) | collective-permute-done | bytes 524320 | tf_op jit(solution)/shard_map/ppermute | solution.py:345
  61.9 5.2 %collective-permute-done.13.refs_1_ = bf16[256,1024]{1,0:T(8,128)(2,1)S(1)} collective-permute-done((bf16[256,1024]{1,0:T(8,128)(2,1)S(1)}, bf16[256,1024]{1,0:T(8,128)(2,1)S(1)}, u32[]{:S(2)}, u32[]{:S(2)}) %collective-permute-start.13) | collective-permute-done | bytes 524320 | tf_op jit(solution)/shard_map/ppermute | solution.py:345
  67.1 1.5 %collective-permute-done.15.refs_2_ = bf16[256,1024]{1,0:T(8,128)(2,1)S(1)} collective-permute-done((bf16[256,1024]{1,0:T(8,128)(2,1)S(1)}, bf16[256,1024]{1,0:T(8,128)(2,1)S(1)}, u32[]{:S(2)}, u32[]{:S(2)}) %collective-permute-start.15) | collective-permute-done | bytes 524320 | tf_op jit(solution)/shard_map/ppermute | solution.py:345
  68.8 25.2 %all_to_all.5.parts_ref = bf16[8,32,1024]{2,1,0:T(8,128)(2,1)S(1)} all-to-all(bf16[8,32,1024]{2,1,0:T(8,128)(2,1)S(1)} %halfway.1), channel_id=1, replica_groups=mesh['y'=4,'zh'=4,'x'=4,'c'=2,'zl'=2] {'zh','zl'}, dimensions={0} | all-to-all | bytes 1048576 | tf_op jit(solution)/shard_map/all_to_all | solution.py:392
  (29 shorter events, 7.6 us)
Async XLA Ops:
  0.0 13.0 %copy-start.2 = (bf16[128,1024]{1,0:T(8,128)(2,1)S(1)}, bf16[128,1024]{1,0:T(8,128)(2,1)}, u32[]{:S(2)}) copy-start(bf16[128,1024]{1,0:T(8,128)(2,1)} %keys_ref.3) | copy-start | bytes 786436
  0.0 13.0 %copy-start.1 = (bf16[128,8192]{1,0:T(8,128)(2,1)S(1)}, bf16[128,8192]{1,0:T(8,128)(2,1)}, u32[]{:S(2)}) copy-start(bf16[128,8192]{1,0:T(8,128)(2,1)} %grads_ref.3) | copy-start | bytes 6291460
  0.0 13.0 %copy-start = (bf16[128,8192]{1,0:T(8,128)(2,1)S(1)}, bf16[128,8192]{1,0:T(8,128)(2,1)}, u32[]{:S(2)}) copy-start(bf16[128,8192]{1,0:T(8,128)(2,1)} %queries_ref.3) | copy-start | bytes 6291460
  0.0 12.9 %collective-permute-start = (bf16[128,1024]{1,0:T(8,128)(2,1)}, bf16[128,1024]{1,0:T(8,128)(2,1)S(1)}, u32[]{:S(2)}, u32[]{:S(2)}) collective-permute-start(bf16[128,1024]{1,0:T(8,128)(2,1)} %keys_ref.3), channel_id=1, source_target_pairs={{0,1},{2,3},{4,5},{6,7},{8,9},{10,11},{12,13},{14,15},{16,17},{18,... | collective-permute-start | bytes 786440 | tf_op jit(solution)/shard_map/ppermute | solution.py:355
  6.6 23.9 %collective-permute-start.4 = (bf16[1024,128]{1,0:T(8,128)(2,1)S(1)}, bf16[1024,128]{1,0:T(8,128)(2,1)S(1)}, u32[]{:S(2)}, u32[]{:S(2)}) collective-permute-start(bf16[1024,128]{1,0:T(8,128)(2,1)S(1)} %get-tuple-element.39), channel_id=1, source_target_pairs={{0,8},{4,12},{8,0},{12,4},{1,9},{5,13},{9,1},{13,5},{2,10},{6,14},... | collective-permute-start | bytes 786440 | tf_op jit(solution)/shard_map/ppermute | solution.py:336
  9.8 22.4 %collective-permute-start.8 = (bf16[1024,128]{1,0:T(8,128)(2,1)S(1)}, bf16[1024,128]{1,0:T(8,128)(2,1)S(1)}, u32[]{:S(2)}, u32[]{:S(2)}) collective-permute-start(bf16[1024,128]{1,0:T(8,128)(2,1)S(1)} %get-tuple-element.43), channel_id=1, source_target_pairs={{0,128},{64,192},{128,0},{192,64},{1,129},{65,193},{129,1},{193,65... | collective-permute-start | bytes 786440 | tf_op jit(solution)/shard_map/ppermute | solution.py:336
  15.8 5.4 %copy-start.3 = (s32[8192]{0:T(1024)S(1)}, s32[8192]{0:T(1024)}, u32[]{:S(2)}) copy-start(s32[8192]{0:T(1024)} %layout_ref.5) | copy-start | bytes 98308
  15.8 10.6 %collective-permute-start.1 = (bf16[128,512]{1,0:T(8,128)(2,1)S(1)}, bf16[128,512]{1,0:T(8,128)(2,1)S(1)}, u32[]{:S(2)}, u32[]{:S(2)}) collective-permute-start(bf16[128,512]{1,0:T(8,128)(2,1)S(1)} %get-tuple-element.31), channel_id=1, source_target_pairs={{1,0},{3,2},{5,4},{7,6},{9,8},{11,10},{13,12},{15,14},{17,16},{19,... | collective-permute-start | bytes 393224 | tf_op jit(solution)/shard_map/ppermute | solution.py:369
  19.9 6.9 %collective-permute-start.2 = (bf16[128,512]{1,0:T(8,128)(2,1)S(1)}, bf16[128,512]{1,0:T(8,128)(2,1)S(1)}, u32[]{:S(2)}, u32[]{:S(2)}) collective-permute-start(bf16[128,512]{1,0:T(8,128)(2,1)S(1)} %get-tuple-element.32), channel_id=1, source_target_pairs={{1,0},{3,2},{5,4},{7,6},{9,8},{11,10},{13,12},{15,14},{17,16},{19,... | collective-permute-start | bytes 393224 | tf_op jit(solution)/shard_map/ppermute | solution.py:369
  26.9 10.4 %collective-permute-start.9 = (bf16[1024,128]{1,0:T(8,128)(2,1)S(1)}, bf16[1024,128]{1,0:T(8,128)(2,1)S(1)}, u32[]{:S(2)}, u32[]{:S(2)}) collective-permute-start(bf16[1024,128]{1,0:T(8,128)(2,1)S(1)} %get-tuple-element.37.refs_1_), channel_id=1, source_target_pairs={{0,128},{64,192},{128,0},{192,64},{1,129},{65,193},{129,1},{193,65... | collective-permute-start | bytes 786440 | tf_op jit(solution)/shard_map/ppermute | solution.py:336
  27.3 19.0 %collective-permute-start.3 = (bf16[2048,128]{1,0:T(8,128)(2,1)S(1)}, bf16[2048,128]{1,0:T(8,128)(2,1)S(1)}, u32[]{:S(2)}, u32[]{:S(2)}) collective-permute-start(bf16[2048,128]{1,0:T(8,128)(2,1)S(1)} %get-tuple-element.38), channel_id=1, source_target_pairs={{0,4},{4,8},{8,12},{12,0},{1,5},{5,9},{9,13},{13,1},{2,6},{6,10},{... | collective-permute-start | bytes 1572872 | tf_op jit(solution)/shard_map/ppermute | solution.py:336
  27.9 18.5 %collective-permute-start.6 = (bf16[2048,128]{1,0:T(8,128)(2,1)S(1)}, bf16[2048,128]{1,0:T(8,128)(2,1)S(1)}, u32[]{:S(2)}, u32[]{:S(2)}) collective-permute-start(bf16[2048,128]{1,0:T(8,128)(2,1)S(1)} %get-tuple-element.40), channel_id=1, source_target_pairs={{0,12},{4,0},{8,4},{12,8},{1,13},{5,1},{9,5},{13,9},{2,14},{6,2},{... | collective-permute-start | bytes 1572872 | tf_op jit(solution)/shard_map/ppermute | solution.py:336
  30.6 16.0 %collective-permute-start.7 = (bf16[2048,128]{1,0:T(8,128)(2,1)S(1)}, bf16[2048,128]{1,0:T(8,128)(2,1)S(1)}, u32[]{:S(2)}, u32[]{:S(2)}) collective-permute-start(bf16[2048,128]{1,0:T(8,128)(2,1)S(1)} %get-tuple-element.42), channel_id=1, source_target_pairs={{0,64},{64,128},{128,192},{192,0},{1,65},{65,129},{129,193},{193,1... | collective-permute-start | bytes 1572872 | tf_op jit(solution)/shard_map/ppermute | solution.py:336
  32.2 14.4 %collective-permute-start.10 = (bf16[2048,128]{1,0:T(8,128)(2,1)S(1)}, bf16[2048,128]{1,0:T(8,128)(2,1)S(1)}, u32[]{:S(2)}, u32[]{:S(2)}) collective-permute-start(bf16[2048,128]{1,0:T(8,128)(2,1)S(1)} %get-tuple-element.44), channel_id=1, source_target_pairs={{0,192},{64,0},{128,64},{192,128},{1,193},{65,1},{129,65},{193,129... | collective-permute-start | bytes 1572872 | tf_op jit(solution)/shard_map/ppermute | solution.py:336
  37.3 8.6 %collective-permute-start.5 = (bf16[1024,128]{1,0:T(8,128)(2,1)S(1)}, bf16[1024,128]{1,0:T(8,128)(2,1)S(1)}, u32[]{:S(2)}, u32[]{:S(2)}) collective-permute-start(bf16[1024,128]{1,0:T(8,128)(2,1)S(1)} %get-tuple-element.37.refs_1_), channel_id=1, source_target_pairs={{0,8},{4,12},{8,0},{12,4},{1,9},{5,13},{9,1},{13,5},{2,10},{6,14},... | collective-permute-start | bytes 786440 | tf_op jit(solution)/shard_map/ppermute | solution.py:336
  47.5 2.7 %collective-permute-start.11 = (bf16[512,1024]{1,0:T(8,128)(2,1)S(1)}, bf16[512,1024]{1,0:T(8,128)(2,1)S(1)}, u32[]{:S(2)}, u32[]{:S(2)}) collective-permute-start(bf16[512,1024]{1,0:T(8,128)(2,1)S(1)} %multiply.4), channel_id=1, source_target_pairs={{0,2},{2,0},{1,3},{3,1},{4,6},{6,4},{5,7},{7,5},{8,10},{10,8},{9,1... | collective-permute-start | bytes 3145736 | tf_op jit(solution)/shard_map/ppermute | solution.py:336
  48.5 6.2 %collective-permute-start.14 = (bf16[512,1024]{1,0:T(8,128)(2,1)S(1)}, bf16[512,1024]{1,0:T(8,128)(2,1)S(1)}, u32[]{:S(2)}, u32[]{:S(2)}) collective-permute-start(bf16[512,1024]{1,0:T(8,128)(2,1)S(1)} %multiply.6), channel_id=1, source_target_pairs={{0,2},{2,0},{1,3},{3,1},{4,6},{6,4},{5,7},{7,5},{8,10},{10,8},{9,1... | collective-permute-start | bytes 3145736 | tf_op jit(solution)/shard_map/ppermute | solution.py:336
  51.2 10.6 %collective-permute-start.12 = (bf16[256,1024]{1,0:T(8,128)(2,1)S(1)}, bf16[256,1024]{1,0:T(8,128)(2,1)S(1)}, u32[]{:S(2)}, u32[]{:S(2)}) collective-permute-start(bf16[256,1024]{1,0:T(8,128)(2,1)S(1)} %get-tuple-element.45), channel_id=1, source_target_pairs={{0,64},{2,6},{4,68},{6,10},{8,72},{10,14},{12,76},{14,2},{64,128},... | collective-permute-start | bytes 1572872 | tf_op jit(solution)/shard_map/ppermute | solution.py:345
  52.8 14.2 %collective-permute-start.13 = (bf16[256,1024]{1,0:T(8,128)(2,1)S(1)}, bf16[256,1024]{1,0:T(8,128)(2,1)S(1)}, u32[]{:S(2)}, u32[]{:S(2)}) collective-permute-start(bf16[256,1024]{1,0:T(8,128)(2,1)S(1)} %get-tuple-element.46), channel_id=1, source_target_pairs={{0,192},{2,14},{4,196},{6,2},{8,200},{10,6},{12,204},{14,10},{64,0... | collective-permute-start | bytes 1572872 | tf_op jit(solution)/shard_map/ppermute | solution.py:345
  55.7 12.8 %collective-permute-start.15 = (bf16[256,1024]{1,0:T(8,128)(2,1)S(1)}, bf16[256,1024]{1,0:T(8,128)(2,1)S(1)}, u32[]{:S(2)}, u32[]{:S(2)}) collective-permute-start(bf16[256,1024]{1,0:T(8,128)(2,1)S(1)} %get-tuple-element.47), channel_id=1, source_target_pairs={{0,128},{2,10},{4,132},{6,14},{8,136},{10,2},{12,140},{14,6},{64,1... | collective-permute-start | bytes 1572872 | tf_op jit(solution)/shard_map/ppermute | solution.py:345

commit v5 on v4

--- a/solution.py
+++ b/solution.py
@@ -232,14 +232,14 @@
 
     def work(way):
         def step(number, carry):
-            off = offs[0] + number * (offs[1] - offs[0])
+            off = (offs[0] + number) & (SIDE - 1)
             total = product(way, pl.ds(pl.multiple_of(off * tile, tile), tile))
             at = pl.ds(pl.multiple_of(number * tile, tile), tile)
             if away:
                 rest[0][at, :] = total.astype(jnp.bfloat16)
                 return carry
             total = (total + rest[0][at, :].astype(jnp.float32)).astype(jnp.bfloat16)
-            for which in range(2):
+            for which in range(len(offs)):
 
                 @pl.when(number == which)
                 def _():
@@ -247,7 +247,7 @@
 
             return carry
 
-        lax.fori_loop(0, 2, step, 0)
+        lax.fori_loop(0, len(offs), step, 0)
 
     for way in range(2):
 
@@ -378,7 +378,7 @@
     for route, piece in zip(HERE, pieces):
         pairs[route] = (piece, value_grad)
     ways = [[pairs[way, steps] for steps in range(SIDE)] for way in WAYS]
-    halves = ((1, 3), (2, 0))
+    halves = ((2,), (3, 0, 1))
     got = []
     for offs in halves:
         (away,) = multiplied(offs, ways)

time: 96.4 us -> 97.2 us (level)
    ppermute x10, waiting for transfers between devices: 9.92 us -> 11.9 us  [ahead(): lax.ppermute(value, axis, [(i, (i + steps) % count) for i in range(count)])]
    ppermute x3, waiting for transfers between devices: 10.9 us -> 9.89 us  [crossed(): return lax.ppermute(value, ('y', 'x', 'c'), pairs)]
  transfers between devices with their start and end apart: 16 -> 16, of which waited for: 9 -> 8; matrix products, arithmetic and copies ran while one was open for 0% -> 0% of each run, Pallas kernels for 22% -> 22%
where the time goes in v5:
time: 97.2 us; the launch traced here: 95.3 us
  blocking collectives  25.2 us (26%)
  starting transfers between devices  24.9 us (26%)
  Pallas kernels  22.9 us (24%)
  waiting for transfers between devices  22.1 us (23%)
    all_to_all x1, blocking collectives, body(): terms = lax.all_to_all(terms, Z, 0, 0, tiled=True)  25.2 us
    ppermute x10, starting transfers between devices, ahead(): lax.ppermute(value, axis, [(i, (i + steps) % count) for i in range(count)])  14.8 us
    pallas_call x3, Pallas kernels, picked_rows(): pl.pallas_call(functools.partial(first_pick_kernel if first else later_pi...  12.5 us
    ppermute x10, waiting for transfers between devices, ahead(): lax.ppermute(value, axis, [(i, (i + steps) % count) for i in range(count)])  11.9 us
    ppermute x3, waiting for transfers between devices, crossed(): return lax.ppermute(value, ('y', 'x', 'c'), pairs)  9.89 us
    pallas_call x2, Pallas kernels, attended(): pl.pallas_call(functools.partial(attend_kernel, first, groups), name='att...  5.58 us
    ppermute x3, starting transfers between devices, crossed(): return lax.ppermute(value, ('y', 'x', 'c'), pairs)  5.18 us
    pallas_call x4, Pallas kernels, multiplied(): pl.pallas_call(functools.partial(multiply_kernel, tuple(places), offs, aw...  3.7 us
  transfers between devices with their start and end apart: 16, of which 8 were waited for; matrix products, arithmetic and copies ran while one was open for 0% of the time, Pallas kernels for 22%

profile of v5, /device:TPU:0, one launch (start us, length us, event | category | flops | bytes accessed | tf_op | source)
XLA Modules:
  0.0 95.3 jit_solution(9069245924963020050)
XLA Ops:
  0.0 2.4 %collective-permute-start = (bf16[128,1024]{1,0:T(8,128)(2,1)}, bf16[128,1024]{1,0:T(8,128)(2,1)S(1)}, u32[]{:S(2)}, u32[]{:S(2)}) collective-permute-start(bf16[128,1024]{1,0:T(8,128)(2,1)} %keys_ref.3), channel_id=1, source_target_pairs={{0,1},{2,3},{4,5},{6,7},{8,9},{10,11},{12,13},{14,15},{16,17},{18,... | collective-permute-start | bytes 786440 | tf_op jit(solution)/shard_map/ppermute | solution.py:355
  2.4 4.2 %pick.3 = (f32[8192,128]{1,0:T(8,128)S(1)}, bf16[1024,128]{1,0:T(8,128)(2,1)S(1)}, bf16[1024,128]{1,0:T(8,128)(2,1)S(1)}) custom-call(s32[8192]{0:T(1024)} %layout_ref.5, bf16[128,8192]{1,0:T(8,128)(2,1)} %acts_ref.1), custom_call_target="tpu_custom_call" | custom-call | flops 2000000000 | bytes 4194304 | tf_op jit(solution)/shard_map/pick/pallas_call | solution.py:103
  6.6 3.1 %collective-permute-start.4 = (bf16[1024,128]{1,0:T(8,128)(2,1)S(1)}, bf16[1024,128]{1,0:T(8,128)(2,1)S(1)}, u32[]{:S(2)}, u32[]{:S(2)}) collective-permute-start(bf16[1024,128]{1,0:T(8,128)(2,1)S(1)} %get-tuple-element.38), channel_id=1, source_target_pairs={{0,8},{4,12},{8,0},{12,4},{1,9},{5,13},{9,1},{13,5},{2,10},{6,14},... | collective-permute-start | bytes 786440 | tf_op jit(solution)/shard_map/ppermute | solution.py:336
  9.8 3.2 %collective-permute-start.8 = (bf16[1024,128]{1,0:T(8,128)(2,1)S(1)}, bf16[1024,128]{1,0:T(8,128)(2,1)S(1)}, u32[]{:S(2)}, u32[]{:S(2)}) collective-permute-start(bf16[1024,128]{1,0:T(8,128)(2,1)S(1)} %get-tuple-element.42), channel_id=1, source_target_pairs={{0,128},{64,192},{128,0},{192,64},{1,129},{65,193},{129,1},{193,65... | collective-permute-start | bytes 786440 | tf_op jit(solution)/shard_map/ppermute | solution.py:336
  13.0 2.8 %attend.2 = (bf16[128,512]{1,0:T(8,128)(2,1)S(1)}, f32[128,512]{1,0:T(8,128)S(1)}) custom-call(bf16[128,8192]{1,0:T(8,128)(2,1)S(1)} %copy-done, bf16[128,1024]{1,0:T(8,128)(2,1)S(1)} %collective-permute-done.earlier_ref, bf16[128,1024]{1,0:T(8,128)(2,1)S(1)} %copy-done.2, bf16[128,8192]{1,0:T(8,128)(2,1)S(1)} %copy-done.1), custom_call_target="tpu_custom_call" | custom-call | flops 536870912 | bytes 3145728 | tf_op jit(solution)/shard_map/attend/pallas_call | solution.py:158
  15.8 1.3 %collective-permute-start.1 = (bf16[128,512]{1,0:T(8,128)(2,1)S(1)}, bf16[128,512]{1,0:T(8,128)(2,1)S(1)}, u32[]{:S(2)}, u32[]{:S(2)}) collective-permute-start(bf16[128,512]{1,0:T(8,128)(2,1)S(1)} %get-tuple-element.30), channel_id=1, source_target_pairs={{1,0},{3,2},{5,4},{7,6},{9,8},{11,10},{13,12},{15,14},{17,16},{19,... | collective-permute-start | bytes 393224 | tf_op jit(solution)/shard_map/ppermute | solution.py:369
  17.1 2.8 %attend.3 = (bf16[128,512]{1,0:T(8,128)(2,1)S(1)}, f32[128,512]{1,0:T(8,128)S(1)}) custom-call(bf16[128,8192]{1,0:T(8,128)(2,1)S(1)} %copy-done, bf16[128,1024]{1,0:T(8,128)(2,1)S(1)} %collective-permute-done.earlier_ref, bf16[128,1024]{1,0:T(8,128)(2,1)S(1)} %copy-done.2, bf16[128,8192]{1,0:T(8,128)(2,1)S(1)} %copy-done.1), custom_call_target="tpu_custom_call" | custom-call | flops 536870912 | bytes 3145728 | tf_op jit(solution)/shard_map/attend/pallas_call | solution.py:158
  19.9 1.3 %collective-permute-start.2 = (bf16[128,512]{1,0:T(8,128)(2,1)S(1)}, bf16[128,512]{1,0:T(8,128)(2,1)S(1)}, u32[]{:S(2)}, u32[]{:S(2)}) collective-permute-start(bf16[128,512]{1,0:T(8,128)(2,1)S(1)} %get-tuple-element.31), channel_id=1, source_target_pairs={{1,0},{3,2},{5,4},{7,6},{9,8},{11,10},{13,12},{15,14},{17,16},{19,... | collective-permute-start | bytes 393224 | tf_op jit(solution)/shard_map/ppermute | solution.py:369
  21.2 5.2 %pick.5 = (bf16[2048,128]{1,0:T(8,128)(2,1)S(1)}, bf16[2048,128]{1,0:T(8,128)(2,1)S(1)}, bf16[2048,128]{1,0:T(8,128)(2,1)S(1)}, bf16[2048,128]{1,0:T(8,128)(2,1)S(1)}) custom-call(s32[8192]{0:T(1024)S(1)} %copy-done.3, f32[8192,128]{1,0:T(8,128)S(1)} %get-tuple-element.26.flipped), custom_call_target="tpu_custom_call" | custom-call | flops 4000000000 | bytes 4194304 | tf_op jit(solution)/shard_map/pick/pallas_call | solution.py:103
  27.9 2.6 %collective-permute-start.6 = (bf16[2048,128]{1,0:T(8,128)(2,1)S(1)}, bf16[2048,128]{1,0:T(8,128)(2,1)S(1)}, u32[]{:S(2)}, u32[]{:S(2)}) collective-permute-start(bf16[2048,128]{1,0:T(8,128)(2,1)S(1)} %get-tuple-element.39), channel_id=1, source_target_pairs={{0,12},{4,0},{8,4},{12,8},{1,13},{5,1},{9,5},{13,9},{2,14},{6,2},{... | collective-permute-start | bytes 1572872 | tf_op jit(solution)/shard_map/ppermute | solution.py:336
  30.6 1.6 %collective-permute-start.7 = (bf16[2048,128]{1,0:T(8,128)(2,1)S(1)}, bf16[2048,128]{1,0:T(8,128)(2,1)S(1)}, u32[]{:S(2)}, u32[]{:S(2)}) collective-permute-start(bf16[2048,128]{1,0:T(8,128)(2,1)S(1)} %get-tuple-element.41), channel_id=1, source_target_pairs={{0,64},{64,128},{128,192},{192,0},{1,65},{65,129},{129,193},{193,1... | collective-permute-start | bytes 1572872 | tf_op jit(solution)/shard_map/ppermute | solution.py:336
  32.2 1.7 %collective-permute-start.10 = (bf16[2048,128]{1,0:T(8,128)(2,1)S(1)}, bf16[2048,128]{1,0:T(8,128)(2,1)S(1)}, u32[]{:S(2)}, u32[]{:S(2)}) collective-permute-start(bf16[2048,128]{1,0:T(8,128)(2,1)S(1)} %get-tuple-element.43), channel_id=1, source_target_pairs={{0,192},{64,0},{128,64},{192,128},{1,193},{65,1},{129,65},{193,129... | collective-permute-start | bytes 1572872 | tf_op jit(solution)/shard_map/ppermute | solution.py:336
  33.8 3.5 %collective-permute-done.9.refs_9_ = bf16[1024,128]{1,0:T(8,128)(2,1)S(1)} collective-permute-done((bf16[1024,128]{1,0:T(8,128)(2,1)S(1)}, bf16[1024,128]{1,0:T(8,128)(2,1)S(1)}, u32[]{:S(2)}, u32[]{:S(2)}) %collective-permute-start.9) | collective-permute-done | bytes 262176 | tf_op jit(solution)/shard_map/ppermute | solution.py:336
  38.2 3.1 %pick.4 = (bf16[1024,128]{1,0:T(8,128)(2,1)S(1)}, bf16[1024,128]{1,0:T(8,128)(2,1)S(1)}) custom-call(s32[8192]{0:T(1024)S(1)} %copy-done.3, f32[8192,128]{1,0:T(8,128)S(1)} %get-tuple-element.26.flipped), custom_call_target="tpu_custom_call" | custom-call | flops 2000000000 | bytes 4194304 | tf_op jit(solution)/shard_map/pick/pallas_call | solution.py:103
  41.3 4.5 %collective-permute-done.5.refs_4_ = bf16[1024,128]{1,0:T(8,128)(2,1)S(1)} collective-permute-done((bf16[1024,128]{1,0:T(8,128)(2,1)S(1)}, bf16[1024,128]{1,0:T(8,128)(2,1)S(1)}, u32[]{:S(2)}, u32[]{:S(2)}) %collective-permute-start.5) | collective-permute-done | bytes 262176 | tf_op jit(solution)/shard_map/ppermute | solution.py:336
  46.6 1.3 %multiply.6 = bf16[768,1024]{1,0:T(8,128)(2,1)S(1)} custom-call(bf16[1024,128]{1,0:T(8,128)(2,1)S(1)} %get-tuple-element.27.refs_0_, bf16[1024,128]{1,0:T(8,128)(2,1)S(1)} %get-tuple-element.36.refs_1_, bf16[2048,128]{1,0:T(8,128)(2,1)S(1)} %collective-permute-done.3.refs_2_, bf16[1024,128]{1,0:T(8,128)(2,1)S(1)} %collective-permute-done.4.refs_3_, ...), custom_call_target="tpu_custom_call" | custom-call | flops 805306368 | bytes 4194304 | tf_op jit(solution)/shard_map/multiply/pallas_call | solution.py:277
  49.1 3.1 %collective-permute-done.11.refs_11_ = bf16[256,1024]{1,0:T(8,128)(2,1)S(1)} collective-permute-done((bf16[256,1024]{1,0:T(8,128)(2,1)S(1)}, bf16[256,1024]{1,0:T(8,128)(2,1)S(1)}, u32[]{:S(2)}, u32[]{:S(2)}) %collective-permute-start.11) | collective-permute-done | bytes 524320 | tf_op jit(solution)/shard_map/ppermute | solution.py:336
  52.6 3.1 %collective-permute-start.12 = (bf16[256,1024]{1,0:T(8,128)(2,1)S(1)}, bf16[256,1024]{1,0:T(8,128)(2,1)S(1)}, u32[]{:S(2)}, u32[]{:S(2)}) collective-permute-start(bf16[256,1024]{1,0:T(8,128)(2,1)S(1)} %multiply.5), channel_id=1, source_target_pairs={{0,128},{2,10},{4,132},{6,14},{8,136},{10,2},{12,140},{14,6},{64,1... | collective-permute-start | bytes 1572872 | tf_op jit(solution)/shard_map/ppermute | solution.py:345
  55.7 1.5 %multiply.7 = (bf16[256,1024]{1,0:T(8,128)(2,1)S(1)}, bf16[256,1024]{1,0:T(8,128)(2,1)S(1)}, bf16[256,1024]{1,0:T(8,128)(2,1)S(1)}) custom-call(bf16[1024,128]{1,0:T(8,128)(2,1)S(1)} %get-tuple-element.27.refs_0_, bf16[1024,128]{1,0:T(8,128)(2,1)S(1)} %get-tuple-element.36.refs_1_, bf16[2048,128]{1,0:T(8,128)(2,1)S(1)} %collective-permute-done.3.refs_2_, ...), custom_call_target="tpu_custom_call" | custom-call | flops 805306368 | bytes 4194304 | tf_op jit(solution)/shard_map/multiply/pallas_call | solution.py:277
  57.2 1.1 %collective-permute-start.14 = (bf16[256,1024]{1,0:T(8,128)(2,1)S(1)}, bf16[256,1024]{1,0:T(8,128)(2,1)S(1)}, u32[]{:S(2)}, u32[]{:S(2)}) collective-permute-start(bf16[256,1024]{1,0:T(8,128)(2,1)S(1)} %get-tuple-element.44), channel_id=1, source_target_pairs={{0,192},{2,14},{4,196},{6,2},{8,200},{10,6},{12,204},{14,10},{64,0... | collective-permute-start | bytes 1572872 | tf_op jit(solution)/shard_map/ppermute | solution.py:345
  58.3 1.0 %collective-permute-start.15 = (bf16[256,1024]{1,0:T(8,128)(2,1)S(1)}, bf16[256,1024]{1,0:T(8,128)(2,1)S(1)}, u32[]{:S(2)}, u32[]{:S(2)}) collective-permute-start(bf16[256,1024]{1,0:T(8,128)(2,1)S(1)} %get-tuple-element.46), channel_id=1, source_target_pairs={{0,64},{2,6},{4,68},{6,10},{8,72},{10,14},{12,76},{14,2},{64,128},... | collective-permute-start | bytes 1572872 | tf_op jit(solution)/shard_map/ppermute | solution.py:345
  59.3 4.1 %collective-permute-done.12.refs_0_ = bf16[256,1024]{1,0:T(8,128)(2,1)S(1)} collective-permute-done((bf16[256,1024]{1,0:T(8,128)(2,1)S(1)}, bf16[256,1024]{1,0:T(8,128)(2,1)S(1)}, u32[]{:S(2)}, u32[]{:S(2)}) %collective-permute-start.12) | collective-permute-done | bytes 524320 | tf_op jit(solution)/shard_map/ppermute | solution.py:345
  63.4 5.8 %collective-permute-done.14.refs_1_ = bf16[256,1024]{1,0:T(8,128)(2,1)S(1)} collective-permute-done((bf16[256,1024]{1,0:T(8,128)(2,1)S(1)}, bf16[256,1024]{1,0:T(8,128)(2,1)S(1)}, u32[]{:S(2)}, u32[]{:S(2)}) %collective-permute-start.14) | collective-permute-done | bytes 524320 | tf_op jit(solution)/shard_map/ppermute | solution.py:345
  69.4 25.2 %all_to_all.5.parts_ref = bf16[8,32,1024]{2,1,0:T(8,128)(2,1)S(1)} all-to-all(bf16[8,32,1024]{2,1,0:T(8,128)(2,1)S(1)} %halfway.1), channel_id=1, replica_groups=mesh['y'=4,'zh'=4,'x'=4,'c'=2,'zl'=2] {'zh','zl'}, dimensions={0} | all-to-all | bytes 1048576 | tf_op jit(solution)/shard_map/all_to_all | solution.py:392
  (29 shorter events, 5.8 us)
Async XLA Ops:
  0.0 13.0 %copy-start.2 = (bf16[128,1024]{1,0:T(8,128)(2,1)S(1)}, bf16[128,1024]{1,0:T(8,128)(2,1)}, u32[]{:S(2)}) copy-start(bf16[128,1024]{1,0:T(8,128)(2,1)} %keys_ref.3) | copy-start | bytes 786436
  0.0 13.0 %copy-start.1 = (bf16[128,8192]{1,0:T(8,128)(2,1)S(1)}, bf16[128,8192]{1,0:T(8,128)(2,1)}, u32[]{:S(2)}) copy-start(bf16[128,8192]{1,0:T(8,128)(2,1)} %grads_ref.3) | copy-start | bytes 6291460
  0.0 13.0 %copy-start = (bf16[128,8192]{1,0:T(8,128)(2,1)S(1)}, bf16[128,8192]{1,0:T(8,128)(2,1)}, u32[]{:S(2)}) copy-start(bf16[128,8192]{1,0:T(8,128)(2,1)} %queries_ref.3) | copy-start | bytes 6291460
  0.0 12.9 %collective-permute-start = (bf16[128,1024]{1,0:T(8,128)(2,1)}, bf16[128,1024]{1,0:T(8,128)(2,1)S(1)}, u32[]{:S(2)}, u32[]{:S(2)}) collective-permute-start(bf16[128,1024]{1,0:T(8,128)(2,1)} %keys_ref.3), channel_id=1, source_target_pairs={{0,1},{2,3},{4,5},{6,7},{8,9},{10,11},{12,13},{14,15},{16,17},{18,... | collective-permute-start | bytes 786440 | tf_op jit(solution)/shard_map/ppermute | solution.py:355
  6.6 23.9 %collective-permute-start.4 = (bf16[1024,128]{1,0:T(8,128)(2,1)S(1)}, bf16[1024,128]{1,0:T(8,128)(2,1)S(1)}, u32[]{:S(2)}, u32[]{:S(2)}) collective-permute-start(bf16[1024,128]{1,0:T(8,128)(2,1)S(1)} %get-tuple-element.38), channel_id=1, source_target_pairs={{0,8},{4,12},{8,0},{12,4},{1,9},{5,13},{9,1},{13,5},{2,10},{6,14},... | collective-permute-start | bytes 786440 | tf_op jit(solution)/shard_map/ppermute | solution.py:336
  9.8 22.4 %collective-permute-start.8 = (bf16[1024,128]{1,0:T(8,128)(2,1)S(1)}, bf16[1024,128]{1,0:T(8,128)(2,1)S(1)}, u32[]{:S(2)}, u32[]{:S(2)}) collective-permute-start(bf16[1024,128]{1,0:T(8,128)(2,1)S(1)} %get-tuple-element.42), channel_id=1, source_target_pairs={{0,128},{64,192},{128,0},{192,64},{1,129},{65,193},{129,1},{193,65... | collective-permute-start | bytes 786440 | tf_op jit(solution)/shard_map/ppermute | solution.py:336
  15.8 5.4 %copy-start.3 = (s32[8192]{0:T(1024)S(1)}, s32[8192]{0:T(1024)}, u32[]{:S(2)}) copy-start(s32[8192]{0:T(1024)} %layout_ref.5) | copy-start | bytes 98308
  15.8 10.6 %collective-permute-start.1 = (bf16[128,512]{1,0:T(8,128)(2,1)S(1)}, bf16[128,512]{1,0:T(8,128)(2,1)S(1)}, u32[]{:S(2)}, u32[]{:S(2)}) collective-permute-start(bf16[128,512]{1,0:T(8,128)(2,1)S(1)} %get-tuple-element.30), channel_id=1, source_target_pairs={{1,0},{3,2},{5,4},{7,6},{9,8},{11,10},{13,12},{15,14},{17,16},{19,... | collective-permute-start | bytes 393224 | tf_op jit(solution)/shard_map/ppermute | solution.py:369
  19.9 6.9 %collective-permute-start.2 = (bf16[128,512]{1,0:T(8,128)(2,1)S(1)}, bf16[128,512]{1,0:T(8,128)(2,1)S(1)}, u32[]{:S(2)}, u32[]{:S(2)}) collective-permute-start(bf16[128,512]{1,0:T(8,128)(2,1)S(1)} %get-tuple-element.31), channel_id=1, source_target_pairs={{1,0},{3,2},{5,4},{7,6},{9,8},{11,10},{13,12},{15,14},{17,16},{19,... | collective-permute-start | bytes 393224 | tf_op jit(solution)/shard_map/ppermute | solution.py:369
  26.9 10.4 %collective-permute-start.9 = (bf16[1024,128]{1,0:T(8,128)(2,1)S(1)}, bf16[1024,128]{1,0:T(8,128)(2,1)S(1)}, u32[]{:S(2)}, u32[]{:S(2)}) collective-permute-start(bf16[1024,128]{1,0:T(8,128)(2,1)S(1)} %get-tuple-element.36.refs_1_), channel_id=1, source_target_pairs={{0,128},{64,192},{128,0},{192,64},{1,129},{65,193},{129,1},{193,65... | collective-permute-start | bytes 786440 | tf_op jit(solution)/shard_map/ppermute | solution.py:336
  27.3 19.0 %collective-permute-start.3 = (bf16[2048,128]{1,0:T(8,128)(2,1)S(1)}, bf16[2048,128]{1,0:T(8,128)(2,1)S(1)}, u32[]{:S(2)}, u32[]{:S(2)}) collective-permute-start(bf16[2048,128]{1,0:T(8,128)(2,1)S(1)} %get-tuple-element.37), channel_id=1, source_target_pairs={{0,4},{4,8},{8,12},{12,0},{1,5},{5,9},{9,13},{13,1},{2,6},{6,10},{... | collective-permute-start | bytes 1572872 | tf_op jit(solution)/shard_map/ppermute | solution.py:336
  27.9 18.5 %collective-permute-start.6 = (bf16[2048,128]{1,0:T(8,128)(2,1)S(1)}, bf16[2048,128]{1,0:T(8,128)(2,1)S(1)}, u32[]{:S(2)}, u32[]{:S(2)}) collective-permute-start(bf16[2048,128]{1,0:T(8,128)(2,1)S(1)} %get-tuple-element.39), channel_id=1, source_target_pairs={{0,12},{4,0},{8,4},{12,8},{1,13},{5,1},{9,5},{13,9},{2,14},{6,2},{... | collective-permute-start | bytes 1572872 | tf_op jit(solution)/shard_map/ppermute | solution.py:336
  30.6 16.0 %collective-permute-start.7 = (bf16[2048,128]{1,0:T(8,128)(2,1)S(1)}, bf16[2048,128]{1,0:T(8,128)(2,1)S(1)}, u32[]{:S(2)}, u32[]{:S(2)}) collective-permute-start(bf16[2048,128]{1,0:T(8,128)(2,1)S(1)} %get-tuple-element.41), channel_id=1, source_target_pairs={{0,64},{64,128},{128,192},{192,0},{1,65},{65,129},{129,193},{193,1... | collective-permute-start | bytes 1572872 | tf_op jit(solution)/shard_map/ppermute | solution.py:336
  32.2 14.4 %collective-permute-start.10 = (bf16[2048,128]{1,0:T(8,128)(2,1)S(1)}, bf16[2048,128]{1,0:T(8,128)(2,1)S(1)}, u32[]{:S(2)}, u32[]{:S(2)}) collective-permute-start(bf16[2048,128]{1,0:T(8,128)(2,1)S(1)} %get-tuple-element.43), channel_id=1, source_target_pairs={{0,192},{64,0},{128,64},{192,128},{1,193},{65,1},{129,65},{193,129... | collective-permute-start | bytes 1572872 | tf_op jit(solution)/shard_map/ppermute | solution.py:336
  37.3 8.6 %collective-permute-start.5 = (bf16[1024,128]{1,0:T(8,128)(2,1)S(1)}, bf16[1024,128]{1,0:T(8,128)(2,1)S(1)}, u32[]{:S(2)}, u32[]{:S(2)}) collective-permute-start(bf16[1024,128]{1,0:T(8,128)(2,1)S(1)} %get-tuple-element.36.refs_1_), channel_id=1, source_target_pairs={{0,8},{4,12},{8,0},{12,4},{1,9},{5,13},{9,1},{13,5},{2,10},{6,14},... | collective-permute-start | bytes 786440 | tf_op jit(solution)/shard_map/ppermute | solution.py:336
  47.9 7.8 %collective-permute-start.13 = (bf16[768,1024]{1,0:T(8,128)(2,1)S(1)}, bf16[768,1024]{1,0:T(8,128)(2,1)S(1)}, u32[]{:S(2)}, u32[]{:S(2)}) collective-permute-start(bf16[768,1024]{1,0:T(8,128)(2,1)S(1)} %multiply.6), channel_id=1, source_target_pairs={{0,2},{2,0},{1,3},{3,1},{4,6},{6,4},{5,7},{7,5},{8,10},{10,8},{9,1... | collective-permute-start | bytes 4718600 | tf_op jit(solution)/shard_map/ppermute | solution.py:336
  48.5 3.7 %collective-permute-start.11 = (bf16[256,1024]{1,0:T(8,128)(2,1)S(1)}, bf16[256,1024]{1,0:T(8,128)(2,1)S(1)}, u32[]{:S(2)}, u32[]{:S(2)}) collective-permute-start(bf16[256,1024]{1,0:T(8,128)(2,1)S(1)} %multiply.4), channel_id=1, source_target_pairs={{0,2},{2,0},{1,3},{3,1},{4,6},{6,4},{5,7},{7,5},{8,10},{10,8},{9,1... | collective-permute-start | bytes 1572872 | tf_op jit(solution)/shard_map/ppermute | solution.py:336
  52.6 10.8 %collective-permute-start.12 = (bf16[256,1024]{1,0:T(8,128)(2,1)S(1)}, bf16[256,1024]{1,0:T(8,128)(2,1)S(1)}, u32[]{:S(2)}, u32[]{:S(2)}) collective-permute-start(bf16[256,1024]{1,0:T(8,128)(2,1)S(1)} %multiply.5), channel_id=1, source_target_pairs={{0,128},{2,10},{4,132},{6,14},{8,136},{10,2},{12,140},{14,6},{64,1... | collective-permute-start | bytes 1572872 | tf_op jit(solution)/shard_map/ppermute | solution.py:345
  57.2 12.0 %collective-permute-start.14 = (bf16[256,1024]{1,0:T(8,128)(2,1)S(1)}, bf16[256,1024]{1,0:T(8,128)(2,1)S(1)}, u32[]{:S(2)}, u32[]{:S(2)}) collective-permute-start(bf16[256,1024]{1,0:T(8,128)(2,1)S(1)} %get-tuple-element.44), channel_id=1, source_target_pairs={{0,192},{2,14},{4,196},{6,2},{8,200},{10,6},{12,204},{14,10},{64,0... | collective-permute-start | bytes 1572872 | tf_op jit(solution)/shard_map/ppermute | solution.py:345
  58.3 10.9 %collective-permute-start.15 = (bf16[256,1024]{1,0:T(8,128)(2,1)S(1)}, bf16[256,1024]{1,0:T(8,128)(2,1)S(1)}, u32[]{:S(2)}, u32[]{:S(2)}) collective-permute-start(bf16[256,1024]{1,0:T(8,128)(2,1)S(1)} %get-tuple-element.46), channel_id=1, source_target_pairs={{0,64},{2,6},{4,68},{6,10},{8,72},{10,14},{12,76},{14,2},{64,128},... | collective-permute-start | bytes 1572872 | tf_op jit(solution)/shard_map/ppermute | solution.py:345
